TPU v7x, 8 devices: a whole 2x2x1 slice. The times are simulated.
8 devices in a mesh: x: 2 (over z, y), yz: 4 (over x, core).
Axes of the slice: x: 2, y: 2, z: 1, core: 2. Of those that a mesh axis runs over, the one named last changes fastest.
Arguments:
- x_in: bfloat16 [192, 2560], P(None, ('x', 'yz'))
- ln_scale: float32 [2560], P(('x', 'yz'))
- w_gate_up: bfloat16 [2560, 2, 10240], P('x', None, 'yz')
- w_attn: bfloat16 [2560, 2720], P('x', 'yz')
- w_down: bfloat16 [10240, 2560], P('yz', 'x')
- w_out: bfloat16 [2560, 2560], P('yz', 'x')
- k_cache: bfloat16 [192, 4096, 80], P(('x', 'yz'))
- v_cache: bfloat16 [192, 4096, 80], P(('x', 'yz'))
- lengths: int32 [192], P(('x', 'yz'))
- positions: int32 [192], P(('x', 'yz'))
Outputs:
- output 1: bfloat16 [192, 2560], P(None, ('x', 'yz'))
- output 2: bfloat16 [192, 4096, 80], P(('x', 'yz'))
- output 3: bfloat16 [192, 4096, 80], P(('x', 'yz'))
All inputs are finite; a program needn't handle non-finite values.
Results may differ from a plain program's by a relative error of at most 0.00361131.
Values are sent between devices in bfloat16 or wider.
A program may use at most 1 GiB of HBM per device.

v0:
```python
import jax
import jax.numpy as jnp
from jax import lax
from jax.sharding import PartitionSpec as P

LN_EPS = 1e-6
ROPE_BASE = 10000.0


def rotary(values, positions):
    half_dim = values.shape[-1] // 2
    inv_freq = ROPE_BASE ** (-jnp.arange(half_dim, dtype=jnp.float32) / half_dim)
    angles = positions.astype(jnp.float32)[:, None, None] * inv_freq
    cos_part = jnp.cos(angles)
    sin_part = jnp.sin(angles)
    lo_half = values[..., :half_dim]
    hi_half = values[..., half_dim:]
    return jnp.concatenate([lo_half * cos_part - hi_half * sin_part, hi_half * cos_part + lo_half * sin_part], axis=-1)


def solution(mesh):
    x_size = mesh.shape['x']
    yz_size = mesh.shape['yz']
    all_axes = ('x', 'yz')

    def local_step(x_in, ln_scale, w_gate_up, w_attn, w_down, w_out, k_cache, v_cache, lengths, positions):
        local_rows, seq_len, head_dim = k_cache.shape
        q_width = w_out.shape[0] * yz_size
        num_heads = q_width // head_dim
        d_model = x_in.shape[1] * x_size * yz_size
        x_float = x_in.astype(jnp.float32)
        ln_sums = jnp.stack([jnp.sum(x_float, axis=1), jnp.sum(x_float * x_float, axis=1)], axis=1)
        ln_sums = lax.psum(ln_sums, all_axes)
        mean_val = ln_sums[:, 0:1] / d_model
        var_val = ln_sums[:, 1:2] / d_model - mean_val * mean_val
        normed = ((x_float - mean_val) * lax.rsqrt(var_val + LN_EPS) * ln_scale).astype(jnp.bfloat16)
        h_rows = lax.all_gather(normed, 'yz', axis=1, tiled=True)
        gu_part = jnp.einsum('bd,dgf->bgf', h_rows, w_gate_up, preferred_element_type=jnp.float32)
        gate_up = lax.psum_scatter(gu_part, 'x', scatter_dimension=2, tiled=True).astype(jnp.bfloat16)
        hidden = (jax.nn.silu(gate_up[:, 0].astype(jnp.float32)) * gate_up[:, 1].astype(jnp.float32)).astype(jnp.bfloat16)
        hidden_rows = lax.all_gather(hidden, 'x', axis=1, tiled=True)
        proj_part = jnp.dot(h_rows, w_attn, preferred_element_type=jnp.float32)
        proj_rows = lax.psum_scatter(proj_part, 'x', scatter_dimension=0, tiled=True).astype(jnp.bfloat16)
        proj_local = lax.all_to_all(proj_rows, 'yz', 0, 1, tiled=True)
        q_raw = proj_local[:, :q_width].reshape(local_rows, num_heads, head_dim)
        k_tok = proj_local[:, q_width:q_width + head_dim]
        v_tok = proj_local[:, q_width + head_dim:]
        q_rot = rotary(q_raw.astype(jnp.float32), positions).astype(jnp.bfloat16)
        k_rot = rotary(k_tok[:, None, :].astype(jnp.float32), positions)[:, 0].astype(jnp.bfloat16)
        slot_ids = jnp.arange(seq_len)
        new_slot = (slot_ids[None, :] == lengths[:, None])[:, :, None]
        k_new = jnp.where(new_slot, k_rot[:, None, :], k_cache)
        v_new = jnp.where(new_slot, v_tok[:, None, :], v_cache)
        scores = jnp.einsum('bhd,bsd->bhs', q_rot, k_new, preferred_element_type=jnp.float32) * head_dim ** -0.5
        in_range = slot_ids[None, None, :] <= lengths[:, None, None]
        scores = jnp.where(in_range, scores, -1e30)
        prob_rows = jax.nn.softmax(scores, axis=-1).astype(jnp.bfloat16)
        attn_out = jnp.einsum('bhs,bsd->bhd', prob_rows, v_new, preferred_element_type=jnp.float32).astype(jnp.bfloat16)
        attn_out = attn_out.reshape(local_rows, q_width)
        o_rows = lax.all_to_all(attn_out, 'yz', 1, 0, tiled=True)
        o_all = lax.all_gather(o_rows, 'x', axis=0, tiled=True)
        mixed_sum = jnp.dot(hidden_rows, w_down, preferred_element_type=jnp.float32) + jnp.dot(o_all, w_out, preferred_element_type=jnp.float32)
        mixed_sum = lax.psum_scatter(mixed_sum, 'yz', scatter_dimension=1, tiled=True)
        y_out = (x_float + mixed_sum).astype(jnp.bfloat16)
        return y_out, k_new, v_new

    row_spec = P(None, all_axes)
    vec_spec = P(all_axes)
    cache_spec = P(all_axes, None, None)
    return jax.shard_map(
        local_step,
        mesh=mesh,
        in_specs=(row_spec, vec_spec, P('x', None, 'yz'), P('x', 'yz'), P('yz', 'x'), P('yz', 'x'), cache_spec, cache_spec, vec_spec, vec_spec),
        out_specs=(row_spec, cache_spec, cache_spec),
        check_vma=False,
    )
```

profile of v0, /device:TPU:0, one launch (start us, length us, event | category | flops | bytes accessed | tf_op | source)
XLA Modules:
  0.0 189.9 jit_solution(2975827362444386494)
XLA Ops:
  7.2 0.0 copy-start
  7.2 0.0 reduce-scatter.8.cloned.1.call-start
  7.2 1.2 convert_reduce_fusion
  8.4 25.1 %psum.7 = f32[192,2]{0,1:T(2,128)S(1)} all-reduce(f32[192,2]{0,1:T(2,128)S(1)} %pad_maximum_fusion.1), channel_id=1, replica_groups=mesh['x'=2,'yz'=4] {'x','yz'}, use_global_device_ids=true, to_apply=%region_2.0 | all-reduce | flops 384 | bytes 3072 | tf_op jit(solution)/shard_map/psum | solution.py:33
  33.5 1.0 fusion.23
  34.6 11.1 %all-gather = bf16[4,320,192]{1,2,0:T(8,128)(2,1)S(1)} all-gather(bf16[1,320,192]{1,2,0:T(8,128)(2,1)S(1)} %fusion.23), channel_id=1, replica_groups=mesh['x'=2,'yz'=4] {'yz'}, dimensions={0}, use_global_device_ids=true | all-gather | bytes 614400 | tf_op jit(solution)/shard_map/all_gather | solution.py:37
  45.6 0.5 copy.19
  46.1 0.5 reshape.193
  46.6 1.5 fusion.41
  48.1 0.0 reduce-scatter.8.cloned.1.call-update
  48.1 0.0 reduce-scatter.6.cloned.1.call-start
  48.1 0.5 reshape.194
  48.6 0.0 copy-start.4
  48.6 9.4 %fusion.1 = f32[192,2,2560]{2,0,1:T(8,128)} fusion(bf16[1280,192,1]{0,1,2:T(8,128)(2,1)S(1)} %reshape.194, bf16[1280,2,2560]{2,1,0:T(2,128)(2,1)} %param.12), kind=kOutput, calls=%fused_computation.3 | convolution fusion | flops 2516582400 | bytes 17530880 | tf_op jit(solution)/shard_map/bd,dgf->bgf/dot_general | solution.py:38
  58.0 0.0 reduce-scatter.6.cloned.1.call-update
  58.1 0.2 iota_compare_fusion.1
  58.2 2.5 %reduce-scatter.8.cloned.1.call-done = f32[96,680]{1,0:T(8,128)} async-done(((f32[192,680]{1,0:T(8,128)}), f32[96,680]{1,0:T(8,128)}) %reduce-scatter.8.cloned.1.call-update) | async-done | bytes 261136 | tf_op jit(solution)/shard_map/reduce_scatter | solution.py:43
  60.7 1.6 convert_element_type.66
  62.4 3.3 %all-to-all-start = ((bf16[4,24,680]{2,1,0:T(8,128)(2,1)}), bf16[4,24,680]{2,1,0:T(8,128)(2,1)S(1)}, u32[]{:S(2)}, u32[]{:S(2)}) async-start(bf16[4,24,680]{2,1,0:T(8,128)(2,1)} %bitcast.9), calls=%async_computation.2 | async-start | bytes 294912 | tf_op jit(solution)/shard_map/all_to_all | solution.py:44
  65.7 0.2 reduce-scatter.10.cloned.1.call-start
  65.9 0.1 multiply_cosine_fusion.1
  66.1 4.2 %all-to-all-done = bf16[4,24,680]{2,1,0:T(8,128)(2,1)S(1)} async-done(((bf16[4,24,680]{2,1,0:T(8,128)(2,1)}), bf16[4,24,680]{2,1,0:T(8,128)(2,1)S(1)}, u32[]{:S(2)}, u32[]{:S(2)}) %all-to-all-start) | async-done | bytes 130592 | tf_op jit(solution)/shard_map/all_to_all | solution.py:44
  70.2 0.1 copy.21
  70.3 0.1 all_to_all.31
  70.5 0.2 reshape.190
  70.7 0.1 fusion.32
  70.8 0.1 fusion.34
  70.9 0.1 pad_maximum_fusion
  71.0 0.2 subtract_convert_fusion
  71.2 16.9 %broadcast_select_fusion.1 = (bf16[24,4096,80]{1,2,0:T(8,128)(2,1)S(1)}, bf16[24,4096,80]{1,2,0:T(8,128)(2,1)}) fusion(bf16[24,4096,80]{1,2,0:T(8,128)(2,1)} %param.16, pred[24,4096]{1,0:T(8,128)(4,1)S(1)} %get-tuple-element.18, bf16[24,80]{1,0:T(8,128)(2,1)S(1)} %pad_maximum_fusion, bf16[24,4096,80]{1,2,0:T(8,128)(2,1)} %param.17, ...), kind=kLoop, calls=%fused_computation.2 | loop fusion | flops 15728640 | bytes 63020544 | tf_op jit(solution)/shard_map/jit(_where)/select_n | solution.py:52
  88.1 6.3 %fusion.19 = f32[24,32,4096]{2,1,0:T(8,128)} fusion(bf16[24,4096,80]{1,2,0:T(8,128)(2,1)S(1)} %get-tuple-element.9, bf16[24,32,40]{2,1,0:T(8,128)(2,1)S(1)} %get-tuple-element.6, bf16[24,32,40]{2,1,0:T(8,128)(2,1)S(1)} %get-tuple-element.5), kind=kOutput, calls=%fused_computation.37 | convolution fusion | flops 503562240 | bytes 28434432 | tf_op jit(solution)/shard_map/bhd,bsd->bhs/dot_general | solution.py:54
  94.4 3.3 %copy-done.2 = bf16[24,4096,80]{1,2,0:T(8,128)(2,1)} copy-done((bf16[24,4096,80]{1,2,0:T(8,128)(2,1)}, bf16[24,4096,80]{1,2,0:T(8,128)(2,1)S(1)}, u32[]{:S(2)}) %copy-start.2) | copy-done | bytes 15728664
  97.7 16.9 %fusion.39 = (f32[24,32]{1,0:T(8,128)S(1)}, f32[24,32,4096]{2,1,0:T(8,128)}) fusion(f32[24,32,4096]{2,1,0:T(8,128)} %fusion.19, pred[24,4096]{1,0:T(8,128)(4,1)S(1)} %get-tuple-element.17), kind=kOutput, calls=%fused_computation.69 | output fusion | flops 18878464 | bytes 25267200 | tf_op jit(solution)/shard_map/sub | solution.py:57
  114.6 11.4 %fusion.8 = bf16[24,32,80]{2,1,0:T(8,128)(2,1)S(1)} fusion(bf16[24,4096,80]{1,2,0:T(8,128)(2,1)} %get-tuple-element.10, f32[24,32,4096]{2,1,0:T(8,128)} %get-tuple-element.20, f32[24,32]{1,0:T(8,128)S(1)} %get-tuple-element.19), kind=kOutput, calls=%fused_computation.16 | convolution fusion | flops 509669376 | bytes 28437504 | tf_op jit(solution)/shard_map/bhs,bsd->bhd/dot_general | solution.py:58
  126.0 0.2 all_to_all.32
  126.3 6.9 %all_to_all.38 = bf16[24,4,640]{2,0,1:T(8,128)(2,1)S(1)} all-to-all(bf16[24,4,640]{2,0,1:T(8,128)(2,1)S(1)} %copy.22), channel_id=1, replica_groups=mesh['x'=2,'yz'=4] {'yz'}, dimensions={1} | all-to-all | bytes 245760 | tf_op jit(solution)/shard_map/all_to_all | solution.py:60
  133.2 5.5 %all_gather.11 = bf16[192,640]{1,0:T(8,128)(2,1)S(1)} all-gather(bf16[96,640]{1,0:T(8,128)(2,1)S(1)} %bitcast.49), channel_id=1, replica_groups=mesh['x'=2,'yz'=4] {'x'}, dimensions={0}, use_global_device_ids=true | all-gather | bytes 368640 | tf_op jit(solution)/shard_map/all_gather | solution.py:61
  138.7 1.6 convert_element_type.60
  140.3 0.3 fusion.13
  140.7 0.0 copy-start.3
  140.7 12.3 %all_gather.10 = bf16[192,2560]{1,0:T(8,128)(2,1)S(1)} all-gather(bf16[192,1280]{1,0:T(8,128)(2,1)S(1)} %fusion.13), channel_id=1, replica_groups=mesh['x'=2,'yz'=4] {'x'}, dimensions={1}, use_global_device_ids=true | all-gather | bytes 1474560 | tf_op jit(solution)/shard_map/all_gather | solution.py:41
  152.9 4.3 %fusion.40 = f32[192,1280]{1,0:T(8,128)S(1)} fusion(bf16[192,2560]{1,0:T(8,128)(2,1)S(1)} %all_gather.10, bf16[2560,1280]{1,0:T(8,128)(2,1)} %param.14), kind=kOutput, calls=%fused_computation.70 | convolution fusion | flops 1258291200 | bytes 8519680 | tf_op jit(solution)/shard_map/dot_general | solution.py:62
  157.2 2.0 %convolution_add_fusion = f32[192,1280]{1,0:T(8,128)S(1)} fusion(f32[192,1280]{1,0:T(8,128)S(1)} %fusion.40, bf16[192,640]{1,0:T(8,128)(2,1)S(1)} %all_gather.11, bf16[640,1280]{1,0:T(8,128)(2,1)} %param.15), kind=kOutput, calls=%fused_computation.13 | convolution fusion | flops 314818560 | bytes 3850240 | tf_op jit(solution)/shard_map/dot_general | solution.py:62
  159.3 1.5 copy.23
  160.7 0.0 reduce-scatter.10.cloned.1.call-update
  160.8 20.8 %reduce-scatter.10.cloned.1.call-done = f32[320,192]{1,0:T(8,128)} async-done(((f32[1280,192]{1,0:T(8,128)}), f32[320,192]{1,0:T(8,128)}) %reduce-scatter.10.cloned.1.call-update) | async-done | bytes 245776
  181.5 1.1 copy.24
  182.7 0.7 fusion.18
  (15 shorter events, 0.1 us)
Async XLA Ops:
  7.2 39.4 %copy-start = (bf16[1280,680]{0,1:T(8,128)(2,1)S(1)}, bf16[1280,680]{0,1:T(8,128)(2,1)}, u32[]{:S(2)}) copy-start(bf16[1280,680]{0,1:T(8,128)(2,1)} %param.13) | copy-start | bytes 5222404
  7.2 53.5 %reduce-scatter.8.cloned.1.call-start = ((), (), s32[]{:S(2)}) async-start(), calls=%async_computation.6 | async-start | bytes 884736 | tf_op jit(solution)/shard_map/reduce_scatter | solution.py:43
  48.1 90.6 %reduce-scatter.6.cloned.1.call-start = ((), (), s32[]{:S(2)}) async-start(), calls=%async_computation.5 | async-start | bytes 5898240 | tf_op jit(solution)/shard_map/reduce_scatter | solution.py:39
  48.6 9.4 %copy-start.5 = (s32[24]{0:T(128)S(1)}, s32[24]{0:T(128)}, u32[]{:S(2)}) copy-start(s32[24]{0:T(128)} %param.19) | copy-start | bytes 292
  48.6 9.4 %copy-start.4 = (s32[24]{0:T(128)S(1)}, s32[24]{0:T(128)}, u32[]{:S(2)}) copy-start(s32[24]{0:T(128)} %param.18) | copy-start | bytes 292
  62.4 7.9 %all-to-all-start = ((bf16[4,24,680]{2,1,0:T(8,128)(2,1)}), bf16[4,24,680]{2,1,0:T(8,128)(2,1)S(1)}, u32[]{:S(2)}, u32[]{:S(2)}) async-start(bf16[4,24,680]{2,1,0:T(8,128)(2,1)} %bitcast.9), calls=%async_computation.2 | async-start | bytes 294912 | tf_op jit(solution)/shard_map/all_to_all | solution.py:44
  65.7 115.8 %reduce-scatter.10.cloned.1.call-start = ((), (), s32[]{:S(2)}) async-start(), calls=%async_computation.7 | async-start | bytes 1638400
  88.1 9.6 %copy-start.2 = (bf16[24,4096,80]{1,2,0:T(8,128)(2,1)}, bf16[24,4096,80]{1,2,0:T(8,128)(2,1)S(1)}, u32[]{:S(2)}) copy-start(bf16[24,4096,80]{1,2,0:T(8,128)(2,1)S(1)} %get-tuple-element.9) | copy-start | bytes 47185924
  140.7 42.0 %copy-start.3 = (bf16[192,320]{1,0:T(8,128)(2,1)S(1)}, bf16[192,320]{1,0:T(8,128)(2,1)}, u32[]{:S(2)}) copy-start(bf16[192,320]{1,0:T(8,128)(2,1)} %param.10) | copy-start | bytes 368644
  140.7 42.7 %copy-start.1 = (bf16[1280,680]{0,1:T(8,128)(2,1)S(1)}, bf16[1280,680]{0,1:T(8,128)(2,1)}, u32[]{:S(2)}) copy-start(bf16[1280,680]{0,1:T(8,128)(2,1)} %param.13) | copy-start | bytes 5222404
Sparse Core Ops, SparseCore 0:
  48.2 12.4 reduce-scatter.7
  62.9 49.1 reduce-scatter.5
  160.9 20.6 reduce-scatter.9
where the time goes:
time: 190 us
  blocking collectives  60.8 us (32%)
  other arithmetic  41.1 us (22%)
  matrix products  34.9 us (18%)
  waiting for transfers between devices  27.5 us (14%)
  between operations  14 us (7%)
  local copies, waits for them, and re-layouts  7.92 us (4%)
  starting transfers between devices  3.64 us (2%)
    psum x1, blocking collectives, local_step(): ln_sums = lax.psum(ln_sums, all_axes)  25.1 us
    unnamed x4, waiting for transfers between devices  20.8 us
    select_n x1, other arithmetic, local_step(): k_new = jnp.where(new_slot, k_rot[:, None, :], k_cache)  16.9 us
    sub x1, other arithmetic, local_step(): prob_rows = jax.nn.softmax(scores, axis=-1).astype(jnp.bfloat16)  16.9 us
    all_gather x1, blocking collectives, local_step(): hidden_rows = lax.all_gather(hidden, 'x', axis=1, tiled=True)  12.3 us
    dot_general x1, matrix products, local_step(): jnp.einsum('bhs,bsd->bhd', prob_rows, v_new, preferred_element_type=jnp.f...  11.4 us
    all_gather x1, blocking collectives, local_step(): h_rows = lax.all_gather(normed, 'yz', axis=1, tiled=True)  11.1 us
    dot_general x1, matrix products, local_step(): jnp.einsum('bd,dgf->bgf', h_rows, w_gate_up, preferred_element_type=jnp.f...  9.36 us
  transfers between devices with their start and end apart: 4, of which 3 were waited for; matrix products, arithmetic and copies ran while one was open for 34% of the time, Pallas kernels for 0%

commit v1 on v0

--- a/solution.py
+++ b/solution.py
@@ -1,10 +1,93 @@
+import functools
+
 import jax
 import jax.numpy as jnp
 from jax import lax
+from jax.experimental import pallas as pl
+from jax.experimental.pallas import tpu as pltpu
 from jax.sharding import PartitionSpec as P
 
 LN_EPS = 1e-6
 ROPE_BASE = 10000.0
+VMEM_MOST = 64 * 1024 * 1024 - 64 * 1024
+
+
+def attention_kernel(scale, len_ref, q_ref, cols_ref, k_hbm, v_hbm, o_ref, ko_hbm, vo_hbm, k_buf, v_buf, in_sem, out_sem):
+    rows, _, seq_len = k_buf.shape
+
+    def load(which, b):
+        src, dst = ((k_hbm, k_buf), (v_hbm, v_buf))[which]
+        return pltpu.make_async_copy(src.at[b], dst.at[b], in_sem.at[which, b])
+
+    def save(which, b):
+        src, dst = ((k_buf, ko_hbm), (v_buf, vo_hbm))[which]
+        return pltpu.make_async_copy(src.at[b], dst.at[b], out_sem.at[which, b])
+
+    for b in range(rows):
+        load(0, b).start()
+        load(1, b).start()
+
+    lane = lax.broadcasted_iota(jnp.int32, (1, 128), 1)
+    slots = lax.broadcasted_iota(jnp.int32, (1, seq_len), 1)
+
+    def row(b, carry):
+        length = len_ref[b]
+        window = pl.ds(pl.multiple_of((length // 128) * 128, 128), 128)
+        here = lane == length % 128
+        for which, buf in enumerate((k_buf, v_buf)):
+            load(which, b).wait()
+            col = jnp.sum(jnp.where(lane == b, cols_ref[which], 0.0), axis=1, keepdims=True)
+            tile = buf[b, :, window].astype(jnp.float32)
+            buf[b, :, window] = jnp.where(here, col, tile).astype(jnp.bfloat16)
+        scores = jnp.dot(q_ref[b], k_buf[b], preferred_element_type=jnp.float32) * scale
+        scores = jnp.where(slots <= length, scores, -1e30)
+        top = jnp.max(scores, axis=1, keepdims=True)
+        weights = jnp.exp(scores - top)
+        total = jnp.sum(weights, axis=1, keepdims=True)
+        probs = (weights * (1.0 / total)).astype(jnp.bfloat16)
+        save(0, b).start()
+        save(1, b).start()
+        o_ref[b] = lax.dot_general(probs, v_buf[b], (((1,), (1,)), ((), ())), preferred_element_type=jnp.float32).astype(jnp.bfloat16)
+        return carry
+
+    lax.fori_loop(0, rows, row, 0)
+    for b in range(rows):
+        save(0, b).wait()
+        save(1, b).wait()
+
+
+def attend(q_rot, cols, k_cache, v_cache, lengths):
+    rows, heads, head_dim = q_rot.shape
+    seq_len = k_cache.shape[1]
+    k_t = jnp.swapaxes(k_cache, 1, 2)
+    v_t = jnp.swapaxes(v_cache, 1, 2)
+    cache = jax.ShapeDtypeStruct((rows, head_dim, seq_len), jnp.bfloat16)
+    o, k_new, v_new = pl.pallas_call(
+        functools.partial(attention_kernel, head_dim ** -0.5),
+        out_shape=(jax.ShapeDtypeStruct((rows, heads, head_dim), jnp.bfloat16), cache, cache),
+        in_specs=[
+            pl.BlockSpec(memory_space=pltpu.SMEM),
+            pl.BlockSpec(memory_space=pltpu.VMEM),
+            pl.BlockSpec(memory_space=pltpu.VMEM),
+            pl.BlockSpec(memory_space=pl.ANY),
+            pl.BlockSpec(memory_space=pl.ANY),
+        ],
+        out_specs=(pl.BlockSpec(memory_space=pltpu.VMEM), pl.BlockSpec(memory_space=pl.ANY), pl.BlockSpec(memory_space=pl.ANY)),
+        scratch_shapes=[
+            pltpu.VMEM((rows, head_dim, seq_len), jnp.bfloat16),
+            pltpu.VMEM((rows, head_dim, seq_len), jnp.bfloat16),
+            pltpu.SemaphoreType.DMA((2, rows)),
+            pltpu.SemaphoreType.DMA((2, rows)),
+        ],
+        compiler_params=pltpu.CompilerParams(vmem_limit_bytes=48 * 1024 * 1024),
+        cost_estimate=pl.CostEstimate(
+            flops=4 * rows * heads * head_dim * seq_len,
+            bytes_accessed=8 * rows * head_dim * seq_len,
+            transcendentals=rows * heads * seq_len,
+        ),
+        name='attend',
+    )(lengths, q_rot, cols, k_t, v_t)
+    return o, jnp.swapaxes(k_new, 1, 2), jnp.swapaxes(v_new, 1, 2)
 
 
 def rotary(values, positions):
@@ -47,15 +130,9 @@
         v_tok = proj_local[:, q_width + head_dim:]
         q_rot = rotary(q_raw.astype(jnp.float32), positions).astype(jnp.bfloat16)
         k_rot = rotary(k_tok[:, None, :].astype(jnp.float32), positions)[:, 0].astype(jnp.bfloat16)
-        slot_ids = jnp.arange(seq_len)
-        new_slot = (slot_ids[None, :] == lengths[:, None])[:, :, None]
-        k_new = jnp.where(new_slot, k_rot[:, None, :], k_cache)
-        v_new = jnp.where(new_slot, v_tok[:, None, :], v_cache)
-        scores = jnp.einsum('bhd,bsd->bhs', q_rot, k_new, preferred_element_type=jnp.float32) * head_dim ** -0.5
-        in_range = slot_ids[None, None, :] <= lengths[:, None, None]
-        scores = jnp.where(in_range, scores, -1e30)
-        prob_rows = jax.nn.softmax(scores, axis=-1).astype(jnp.bfloat16)
-        attn_out = jnp.einsum('bhs,bsd->bhd', prob_rows, v_new, preferred_element_type=jnp.float32).astype(jnp.bfloat16)
+        cols = jnp.stack([k_rot, v_tok]).astype(jnp.float32).transpose(0, 2, 1)
+        cols = jnp.pad(cols, ((0, 0), (0, 0), (0, 128 - local_rows)))
+        attn_out, k_new, v_new = attend(q_rot, cols, k_cache, v_cache, lengths)
         attn_out = attn_out.reshape(local_rows, q_width)
         o_rows = lax.all_to_all(attn_out, 'yz', 1, 0, tiled=True)
         o_all = lax.all_gather(o_rows, 'x', axis=0, tiled=True)

time: 190 us -> 166 us (0.87)
  other arithmetic: 41.1 us -> 7.28 us
  Pallas kernels: 0 us -> 23.7 us
  matrix products: 34.9 us -> 15.9 us
  blocking collectives: 60.8 us -> 65.5 us
  waiting for transfers between devices: 27.5 us -> 31.4 us
  local copies, waits for them, and re-layouts: 7.92 us -> 4.74 us
    pallas_call x0 -> x1, Pallas kernels: none -> 23.7 us  [attend(): pl.pallas_call(functools.partial(attention_kernel, head_dim ** (-0.5)), o...]
    dot_general x2 -> x0, matrix products: 17.7 us -> none  [the longest x1 11.4 us: local_step(): jnp.einsum('bhs,bsd->bhd', prob_rows, v_new, preferred_element_type=jnp.f...]
    select_n x1 -> x0, other arithmetic: 16.9 us -> none  [local_step(): k_new = jnp.where(new_slot, k_rot[:, None, :], k_cache)]
    sub x1 -> x0, other arithmetic: 16.9 us -> none  [local_step(): prob_rows = jax.nn.softmax(scores, axis=-1).astype(jnp.bfloat16)]
    all_gather x1, blocking collectives: 5.54 us -> 9.13 us  [local_step(): o_all = lax.all_gather(o_rows, 'x', axis=0, tiled=True)]
    reduce_scatter x1, waiting for transfers between devices: 0.01 us -> 3.37 us  [local_step(): lax.psum_scatter(gu_part, 'x', scatter_dimension=2, tiled=True)]
    unnamed x16, local copies, waits for them, and re-layouts: 6.85 us -> 3.55 us
  transfers between devices with their start and end apart: 4 -> 4, of which waited for: 3 -> 4; matrix products, arithmetic and copies ran while one was open for 34% -> 8% of each run, Pallas kernels for 0% -> 14%
where the time goes in v1:
time: 166 us
  blocking collectives  65.5 us (39%)
  waiting for transfers between devices  31.4 us (19%)
  Pallas kernels  23.7 us (14%)
  matrix products  15.9 us (10%)
  between operations  14 us (8%)
  other arithmetic  7.28 us (4%)
  local copies, waits for them, and re-layouts  4.74 us (3%)
  starting transfers between devices  3.46 us (2%)
    psum x1, blocking collectives, local_step(): ln_sums = lax.psum(ln_sums, all_axes)  25.1 us
    pallas_call x1, Pallas kernels, attend(): pl.pallas_call(functools.partial(attention_kernel, head_dim ** (-0.5)), o...  23.7 us
    unnamed x4, waiting for transfers between devices  21 us
    all_gather x1, blocking collectives, local_step(): hidden_rows = lax.all_gather(hidden, 'x', axis=1, tiled=True)  13.4 us
    all_gather x1, blocking collectives, local_step(): h_rows = lax.all_gather(normed, 'yz', axis=1, tiled=True)  11.1 us
    dot_general x1, matrix products, local_step(): jnp.einsum('bd,dgf->bgf', h_rows, w_gate_up, preferred_element_type=jnp.f...  9.32 us
    all_gather x1, blocking collectives, local_step(): o_all = lax.all_gather(o_rows, 'x', axis=0, tiled=True)  9.13 us
    all_to_all x1, blocking collectives, local_step(): o_rows = lax.all_to_all(attn_out, 'yz', 1, 0, tiled=True)  6.9 us
  transfers between devices with their start and end apart: 4, of which 4 were waited for; matrix products, arithmetic and copies ran while one was open for 8% of the time, Pallas kernels for 14%

profile of v1, /device:TPU:0, one launch (start us, length us, event | category | flops | bytes accessed | tf_op | source)
XLA Modules:
  0.0 166.0 jit_solution(16785901914802743424)
XLA Ops:
  7.2 0.0 copy-start
  7.2 0.0 reduce-scatter.8.cloned.1.call-start
  7.2 1.2 convert_reduce_fusion
  8.4 25.1 %psum.7 = f32[192,2]{0,1:T(2,128)S(1)} all-reduce(f32[192,2]{0,1:T(2,128)S(1)} %pad_maximum_fusion.2), channel_id=1, replica_groups=mesh['x'=2,'yz'=4] {'x','yz'}, use_global_device_ids=true, to_apply=%region_2.0 | all-reduce | flops 384 | bytes 3072 | tf_op jit(solution)/shard_map/psum | solution.py:116
  33.5 1.0 fusion.12
  34.6 11.1 %all-gather = bf16[4,320,192]{1,2,0:T(8,128)(2,1)S(1)} all-gather(bf16[1,320,192]{1,2,0:T(8,128)(2,1)S(1)} %fusion.12), channel_id=1, replica_groups=mesh['x'=2,'yz'=4] {'yz'}, dimensions={0}, use_global_device_ids=true | all-gather | bytes 614400 | tf_op jit(solution)/shard_map/all_gather | solution.py:120
  45.6 0.5 copy.28
  46.1 0.5 reshape.146
  46.5 0.0 copy-done
  46.6 1.5 fusion.24
  48.1 0.0 reduce-scatter.8.cloned.1.call-update
  48.1 0.0 reduce-scatter.6.cloned.1.call-start
  48.1 0.5 reshape.147
  48.6 0.0 copy-start.5
  48.6 9.3 %fusion = f32[192,2,2560]{2,0,1:T(8,128)} fusion(bf16[1280,192,1]{0,1,2:T(8,128)(2,1)S(1)} %reshape.147, bf16[1280,2,2560]{2,1,0:T(2,128)(2,1)} %param.12), kind=kOutput, calls=%fused_computation | convolution fusion | flops 2516582400 | bytes 17530880 | tf_op jit(solution)/shard_map/bd,dgf->bgf/dot_general | solution.py:121
  57.9 0.0 reduce-scatter.6.cloned.1.call-update
  58.0 0.0 copy-done.5
  58.0 2.7 %reduce-scatter.8.cloned.1.call-done = f32[96,680]{1,0:T(8,128)} async-done(((f32[192,680]{1,0:T(8,128)}), f32[96,680]{1,0:T(8,128)}) %reduce-scatter.8.cloned.1.call-update) | async-done | bytes 261136 | tf_op jit(solution)/shard_map/reduce_scatter | solution.py:126
  60.7 1.6 convert_element_type.69
  62.4 3.3 %all-to-all-start = ((bf16[4,24,680]{2,1,0:T(8,128)(2,1)}), bf16[4,24,680]{2,1,0:T(8,128)(2,1)S(1)}, u32[]{:S(2)}, u32[]{:S(2)}) async-start(bf16[4,24,680]{2,1,0:T(8,128)(2,1)} %bitcast.9), calls=%async_computation.2 | async-start | bytes 294912 | tf_op jit(solution)/shard_map/all_to_all | solution.py:127
  65.7 0.0 reduce-scatter.10.cloned.1.call-start
  65.7 0.1 multiply_cosine_fusion.1
  65.9 4.4 %all-to-all-done = bf16[4,24,680]{2,1,0:T(8,128)(2,1)S(1)} async-done(((bf16[4,24,680]{2,1,0:T(8,128)(2,1)}), bf16[4,24,680]{2,1,0:T(8,128)(2,1)S(1)}, u32[]{:S(2)}, u32[]{:S(2)}) %all-to-all-start) | async-done | bytes 130592 | tf_op jit(solution)/shard_map/all_to_all | solution.py:127
  70.2 0.1 copy.30
  70.3 0.1 all_to_all.31
  70.4 0.1 fusion.21
  70.5 0.1 fusion.18
  70.7 0.1 maximum_bitcast_fusion
  70.7 0.1 copy.31
  70.9 0.2 reshape.143
  71.1 0.2 subtract_convert_fusion
  71.3 0.1 pad_maximum_fusion.q_ref
  71.4 23.7 %attend.1 = (bf16[24,32,80]{2,1,0:T(8,128)(2,1)S(1)}, bf16[24,80,4096]{2,1,0:T(8,128)(2,1)}, bf16[24,80,4096]{2,1,0:T(8,128)(2,1)}) custom-call(s32[24]{0:T(128)S(1)} %copy-done.2, bf16[24,32,80]{2,1,0:T(8,128)(2,1)S(1)} %pad_maximum_fusion.q_ref, f32[2,80,128]{2,1,0:T(8,128)S(1)} %pad_convert_fusion.cols_ref, bf16[24,80,4096]{2,1,0:T(8,128)(2,1)} %bitcast.50, ...), custom_call_target="tpu_custom_call" | custom-call | flops 1006632960 | bytes 62914560 | tf_op jit(solution)/shard_map/attend/pallas_call | solution.py:65
  95.2 0.2 all_to_all.32
  95.4 6.9 %all_to_all.38 = bf16[24,4,640]{2,0,1:T(8,128)(2,1)S(1)} all-to-all(bf16[24,4,640]{2,0,1:T(8,128)(2,1)S(1)} %copy.32), channel_id=1, replica_groups=mesh['x'=2,'yz'=4] {'yz'}, dimensions={1} | all-to-all | bytes 245760 | tf_op jit(solution)/shard_map/all_to_all | solution.py:137
  102.3 9.1 %all_gather.11 = bf16[192,640]{1,0:T(8,128)(2,1)S(1)} all-gather(bf16[96,640]{1,0:T(8,128)(2,1)S(1)} %bitcast.54), channel_id=1, replica_groups=mesh['x'=2,'yz'=4] {'x'}, dimensions={0}, use_global_device_ids=true | all-gather | bytes 368640 | tf_op jit(solution)/shard_map/all_gather | solution.py:138
  111.4 3.4 %reduce-scatter.6.cloned.1.call-done = f32[192,2,1280]{2,0,1:T(8,128)} async-done(((f32[192,2,2560]{2,0,1:T(8,128)}), f32[192,2,1280]{2,0,1:T(8,128)}) %reduce-scatter.6.cloned.1.call-update) | async-done | bytes 1966096 | tf_op jit(solution)/shard_map/reduce_scatter | solution.py:122
  114.8 1.6 convert_element_type.63
  116.4 0.3 fusion.6
  116.7 13.4 %all_gather.10 = bf16[192,2560]{1,0:T(8,128)(2,1)S(1)} all-gather(bf16[192,1280]{1,0:T(8,128)(2,1)S(1)} %fusion.6), channel_id=1, replica_groups=mesh['x'=2,'yz'=4] {'x'}, dimensions={1}, use_global_device_ids=true | all-gather | bytes 1474560 | tf_op jit(solution)/shard_map/all_gather | solution.py:124
  130.1 4.4 %fusion.23 = f32[192,1280]{1,0:T(8,128)S(1)} fusion(bf16[192,2560]{1,0:T(8,128)(2,1)S(1)} %all_gather.10, bf16[2560,1280]{1,0:T(8,128)(2,1)} %param.14), kind=kOutput, calls=%fused_computation.50 | convolution fusion | flops 1258291200 | bytes 8519680 | tf_op jit(solution)/shard_map/dot_general | solution.py:139
  134.6 0.0 copy-start.4
  134.6 0.6 convolution_add_fusion
  135.2 1.5 copy.33
  136.7 0.0 reduce-scatter.10.cloned.1.call-update
  136.7 20.9 %reduce-scatter.10.cloned.1.call-done = f32[320,192]{1,0:T(8,128)} async-done(((f32[1280,192]{1,0:T(8,128)}), f32[320,192]{1,0:T(8,128)}) %reduce-scatter.10.cloned.1.call-update) | async-done | bytes 245776
  157.6 1.1 copy.34
  158.7 0.7 fusion.11
  (15 shorter events, 0.1 us)
Async XLA Ops:
  7.2 39.4 %copy-start = (bf16[1280,680]{0,1:T(8,128)(2,1)S(1)}, bf16[1280,680]{0,1:T(8,128)(2,1)}, u32[]{:S(2)}) copy-start(bf16[1280,680]{0,1:T(8,128)(2,1)} %param.13) | copy-start | bytes 5222404
  7.2 53.5 %reduce-scatter.8.cloned.1.call-start = ((), (), s32[]{:S(2)}) async-start(), calls=%async_computation.6 | async-start | bytes 884736 | tf_op jit(solution)/shard_map/reduce_scatter | solution.py:126
  48.1 66.7 %reduce-scatter.6.cloned.1.call-start = ((), (), s32[]{:S(2)}) async-start(), calls=%async_computation.5 | async-start | bytes 5898240 | tf_op jit(solution)/shard_map/reduce_scatter | solution.py:122
  48.6 9.4 %copy-start.5 = (s32[24]{0:T(128)S(1)}, s32[24]{0:T(128)}, u32[]{:S(2)}) copy-start(s32[24]{0:T(128)} %param.19) | copy-start | bytes 292
  57.9 13.5 %copy-start.2 = (s32[24]{0:T(128)S(1)}, s32[24]{0:T(128)}, u32[]{:S(2)}) copy-start(s32[24]{0:T(128)} %len_ref.1) | copy-start | bytes 292
  62.4 7.9 %all-to-all-start = ((bf16[4,24,680]{2,1,0:T(8,128)(2,1)}), bf16[4,24,680]{2,1,0:T(8,128)(2,1)S(1)}, u32[]{:S(2)}, u32[]{:S(2)}) async-start(bf16[4,24,680]{2,1,0:T(8,128)(2,1)} %bitcast.9), calls=%async_computation.2 | async-start | bytes 294912 | tf_op jit(solution)/shard_map/all_to_all | solution.py:127
  65.7 91.9 %reduce-scatter.10.cloned.1.call-start = ((), (), s32[]{:S(2)}) async-start(), calls=%async_computation.7 | async-start | bytes 1638400
  130.1 4.5 %copy-start.3 = (bf16[640,1280]{1,0:T(8,128)(2,1)S(1)}, bf16[640,1280]{1,0:T(8,128)(2,1)}, u32[]{:S(2)}) copy-start(bf16[640,1280]{1,0:T(8,128)(2,1)} %param.15) | copy-start | bytes 4915204
  130.1 29.3 %copy-start.1 = (bf16[1280,680]{0,1:T(8,128)(2,1)S(1)}, bf16[1280,680]{0,1:T(8,128)(2,1)}, u32[]{:S(2)}) copy-start(bf16[1280,680]{0,1:T(8,128)(2,1)} %param.13) | copy-start | bytes 5222404
  134.6 24.2 %copy-start.4 = (bf16[192,320]{1,0:T(8,128)(2,1)S(1)}, bf16[192,320]{1,0:T(8,128)(2,1)}, u32[]{:S(2)}) copy-start(bf16[192,320]{1,0:T(8,128)(2,1)} %param.10) | copy-start | bytes 368644
Sparse Core Ops, SparseCore 0:
  48.2 12.4 reduce-scatter.7
  62.9 51.7 reduce-scatter.5
  136.8 20.7 reduce-scatter.9

commit v2 on v1

--- a/solution.py
+++ b/solution.py
@@ -9,7 +9,7 @@
 
 LN_EPS = 1e-6
 ROPE_BASE = 10000.0
-VMEM_MOST = 64 * 1024 * 1024 - 64 * 1024
+MESH = pl.DeviceIdType.MESH
 
 
 def attention_kernel(scale, len_ref, q_ref, cols_ref, k_hbm, v_hbm, o_ref, ko_hbm, vo_hbm, k_buf, v_buf, in_sem, out_sem):
@@ -90,6 +90,341 @@
     return o, jnp.swapaxes(k_new, 1, 2), jnp.swapaxes(v_new, 1, 2)
 
 
+def start_barrier(me_x, me_yz):
+    barrier = pltpu.get_barrier_semaphore()
+    for dx in range(2):
+        for k in range(4):
+            if dx or k:
+                peer = (lax.rem(me_x + dx, 2), lax.rem(me_yz + k, 4))
+                pl.semaphore_signal(barrier, inc=1, device_id=peer, device_id_type=MESH)
+    pl.semaphore_wait(barrier, 7)
+
+
+def spread(rows, cols, first):
+    i = lax.broadcasted_iota(jnp.int32, (rows, cols), 0)
+    c = lax.broadcasted_iota(jnp.int32, (rows, cols), 1)
+    return jnp.where(c == 2 * i + first, 1.0, 0.0).astype(jnp.bfloat16)
+
+
+def head_kernel(
+    d_model, x_hbm, scale_hbm, wg_hbm, wa_hbm, z_ref, send_hbm, own_hbm,
+    xg, sg, stats, h_buf, hx, hc, wg, wa, z_send, z_own, z_recv, zb, zg, gp,
+    in_sem, wg_sem, x_send, x_recv, s_send, s_recv, t_send, t_recv, z_sems, a_send, a_recv, out_sem,
+):
+    me_x = lax.axis_index('x')
+    me_yz = lax.axis_index('yz')
+    rows, chunk = xg.shape[1:]
+    half = rows // 2
+    pieces = wg_sem.shape[0]
+    depth = wg.shape[0] // pieces
+    ff = wg.shape[2]
+    x_in = pltpu.make_async_copy(x_hbm, xg.at[me_yz], in_sem.at[0])
+    scale_in = pltpu.make_async_copy(scale_hbm, sg.at[me_yz], in_sem.at[1])
+    wa_in = pltpu.make_async_copy(wa_hbm, wa, in_sem.at[2])
+    wg_in = [
+        pltpu.make_async_copy(wg_hbm.at[pl.ds(depth * i, depth)], wg.at[pl.ds(depth * i, depth)], wg_sem.at[i]) for i in range(pieces)
+    ]
+    x_in.start()
+    scale_in.start()
+    wa_in.start()
+    for copy in wg_in:
+        copy.start()
+    start_barrier(me_x, me_yz)
+
+    def to_peer(src, dst, sems, i, k, dx=0):
+        return pltpu.make_async_remote_copy(
+            src_ref=src, dst_ref=dst, send_sem=sems[0].at[i], recv_sem=sems[1].at[i],
+            device_id=(lax.rem(me_x + dx, 2), lax.rem(me_yz + k, 4)), device_id_type=MESH,
+        )
+
+    x_in.wait()
+    x_out = [to_peer(xg.at[me_yz], xg.at[me_yz], (x_send, x_recv), k, k) for k in (1, 2, 3)]
+    for copy in x_out:
+        copy.start()
+    scale_in.wait()
+    s_out = [to_peer(sg.at[me_yz], sg.at[me_yz], (s_send, s_recv), k, k) for k in (1, 2, 3)]
+    for copy in s_out:
+        copy.start()
+    lane = lax.broadcasted_iota(jnp.int32, (8, 128), 1)
+    mine = xg[me_yz].astype(jnp.float32)
+    sum_1 = jnp.sum(mine, axis=1, keepdims=True)
+    sum_2 = jnp.sum(mine * mine, axis=1, keepdims=True)
+    tile = jnp.zeros((8, 128), jnp.float32)
+    for j in range(rows // 8):
+        tile = jnp.where(lane == j, sum_1[8 * j:8 * j + 8], tile)
+        tile = jnp.where(lane == 32 + j, sum_2[8 * j:8 * j + 8], tile)
+    me = me_x * 4 + me_yz
+    stats[me] = tile
+    t_out = [
+        to_peer(stats.at[me], stats.at[me], (t_send, t_recv), 4 * dx + k, k, dx) for dx in range(2) for k in range(4) if dx or k
+    ]
+    for copy in t_out:
+        copy.start()
+    for copy in t_out:
+        copy.wait()
+    total = stats[0]
+    for i in range(1, 8):
+        total = total + stats[i]
+    mean_t = total / d_model
+    var_t = pltpu.roll(total, 96, 1) / d_model - mean_t * mean_t
+    rstd_t = lax.rsqrt(var_t + LN_EPS)
+    mean = jnp.concatenate([mean_t[:, j:j + 1] for j in range(rows // 8)], axis=0)
+    rstd = jnp.concatenate([rstd_t[:, j:j + 1] for j in range(rows // 8)], axis=0)
+    for copy in s_out:
+        copy.wait()
+    for copy in x_out:
+        copy.wait()
+    for s in range(4):
+        h_buf[s] = ((xg[s].astype(jnp.float32) - mean) * rstd * sg[s]).astype(jnp.bfloat16)
+
+    wide, thin = spread(128, 256, 0), spread(64, 128, 0)
+    wide_u, thin_u = spread(128, 256, 1), spread(64, 128, 1)
+    i = lax.broadcasted_iota(jnp.int32, (256, 128), 0)
+    c = lax.broadcasted_iota(jnp.int32, (256, 128), 1)
+    gather = jnp.where(i == 2 * c, 1.0, 0.0).astype(jnp.bfloat16)
+
+    def start_of(part):
+        first = lax.rem(me_x + 1 - part, 2)
+        return pl.ds(pl.multiple_of(first * half, 32), half)
+
+    def spread_half(part, g):
+        out = pl.ds((2 * part + g) * half, half)
+        a, b = ((wide, thin), (wide_u, thin_u))[g]
+        for s in range(4):
+            base = 2 * chunk * s
+            part_rows = start_of(part)
+            for t in range(2):
+                piece = h_buf[s, part_rows, 128 * t:128 * t + 128]
+                hx[out, base + 256 * t:base + 256 * t + 256] = jnp.dot(piece, a, preferred_element_type=jnp.float32).astype(jnp.bfloat16)
+            piece = h_buf[s, part_rows, 256:320]
+            hx[out, base + 512:base + 640] = jnp.dot(piece, b, preferred_element_type=jnp.float32).astype(jnp.bfloat16)
+
+    def project(part):
+        spread_half(part, 0)
+        src = pl.ds(2 * part * half, half)
+        for t in range(4 * chunk // 128):
+            hc[:, 128 * t:128 * t + 128] = jnp.dot(hx[src, 256 * t:256 * t + 256], gather, preferred_element_type=jnp.float32).astype(jnp.bfloat16)
+        z = lax.dot_general(hc[...], wa[...], (((1,), (1,)), ((), ())), preferred_element_type=jnp.float32)
+        return z.reshape(z_send.shape)
+
+    wa_in.wait()
+    z_send[...] = project(0)
+    z_copy = pltpu.make_async_remote_copy(
+        src_ref=z_send, dst_ref=z_recv, send_sem=z_sems.at[0], recv_sem=z_sems.at[1],
+        device_id=(lax.rem(me_x + 1, 2), me_yz), device_id_type=MESH,
+    )
+    z_copy.start()
+    z_own[...] = project(1)
+    spread_half(0, 1)
+    spread_half(1, 1)
+    for copy in wg_in:
+        copy.wait()
+    flat = wg.reshape(wg.shape[0] * 2, ff)
+
+    def columns(c, carry):
+        at = pl.ds(pl.multiple_of(c * 256, 256), 256)
+        up = pl.ds(pl.multiple_of(ff + c * 256, 256), 256)
+        out = jnp.dot(hx[...], flat[:, at], preferred_element_type=jnp.float32)
+        gp[0, :, at] = out[:half]
+        gp[0, :, up] = out[half:2 * half]
+        gp[1, :, at] = out[2 * half:3 * half]
+        gp[1, :, up] = out[3 * half:]
+        return carry
+
+    lax.fori_loop(0, ff // 256, columns, 0)
+    save = [pltpu.make_async_copy(gp.at[0], send_hbm, out_sem.at[0]), pltpu.make_async_copy(gp.at[1], own_hbm, out_sem.at[1])]
+    for copy in save:
+        copy.start()
+    z_copy.wait()
+    zb[...] = (z_own[...] + z_recv[...]).astype(jnp.bfloat16)
+    a_out = [
+        to_peer(zb.at[lax.rem(me_yz + k, 4)], zg.at[me_yz], (a_send, a_recv), k, k) for k in (1, 2, 3)
+    ]
+    for copy in a_out:
+        copy.start()
+    zg[me_yz] = zb[me_yz]
+    for copy in a_out:
+        copy.wait()
+    z_ref[...] = zg[...]
+    for copy in save:
+        copy.wait()
+
+
+def head(x_in, ln_scale, w_gate_up, w_attn, d_model):
+    rows, chunk = x_in.shape
+    depth, _, ff = w_gate_up.shape
+    z_cols = w_attn.shape[1]
+    owned = rows // 8
+    half = rows // 2
+    part = jax.ShapeDtypeStruct((half, 2 * ff), jnp.float32)
+    any_spec = pl.BlockSpec(memory_space=pl.ANY)
+    dma = pltpu.SemaphoreType.DMA
+    return pl.pallas_call(
+        functools.partial(head_kernel, d_model),
+        out_shape=(jax.ShapeDtypeStruct((4, owned, z_cols), jnp.bfloat16), part, part),
+        in_specs=[any_spec] * 4,
+        out_specs=(pl.BlockSpec(memory_space=pltpu.VMEM), any_spec, any_spec),
+        scratch_shapes=[
+            pltpu.VMEM((4, rows, chunk), jnp.bfloat16),
+            pltpu.VMEM((4, 1, chunk), jnp.float32),
+            pltpu.VMEM((8, 8, 128), jnp.float32),
+            pltpu.VMEM((4, rows, chunk), jnp.bfloat16),
+            pltpu.VMEM((2 * rows, 2 * depth), jnp.bfloat16),
+            pltpu.VMEM((half, depth), jnp.bfloat16),
+            pltpu.VMEM((depth, 2, ff), jnp.bfloat16),
+            pltpu.VMEM((z_cols, depth), jnp.bfloat16),
+            pltpu.VMEM((4, owned, z_cols), jnp.float32),
+            pltpu.VMEM((4, owned, z_cols), jnp.float32),
+            pltpu.VMEM((4, owned, z_cols), jnp.float32),
+            pltpu.VMEM((4, owned, z_cols), jnp.bfloat16),
+            pltpu.VMEM((4, owned, z_cols), jnp.bfloat16),
+            pltpu.VMEM((2, half, 2 * ff), jnp.float32),
+            dma((3,)), dma((8,)), dma((4,)), dma((4,)), dma((4,)), dma((4,)), dma((8,)), dma((8,)), dma((2,)), dma((4,)), dma((4,)), dma((2,)),
+        ],
+        compiler_params=pltpu.CompilerParams(collective_id=0, has_side_effects=True, vmem_limit_bytes=48 * 1024 * 1024),
+        cost_estimate=pl.CostEstimate(flops=4 * rows * depth * 2 * ff, bytes_accessed=4 * depth * ff, transcendentals=0),
+        name='head',
+    )(x_in, ln_scale.reshape(1, chunk), w_gate_up, w_attn.T)
+
+
+def tail_kernel(
+    x_hbm, own_hbm, peer_hbm, o_hbm, wd_hbm, wo_hbm, y_ref,
+    xv, g_own, g_peer, ov, oa, of, hb, wd, wo, out_part, y_send, y_recv,
+    in_sem, g_sem, o_send, o_recv, h_send, h_recv, y_ssem, y_rsem,
+):
+    me_x = lax.axis_index('x')
+    me_yz = lax.axis_index('yz')
+    groups, _, span, ff = hb.shape
+    rows, chunk = xv.shape
+    half = rows // 2
+    owned = ov.shape[1]
+    g_in = []
+    for i in range(groups):
+        at = pl.ds(span * i, span)
+        g_in.append((
+            pltpu.make_async_copy(own_hbm.at[at], g_own.at[at], g_sem.at[0, i]),
+            pltpu.make_async_copy(peer_hbm.at[at], g_peer.at[at], g_sem.at[1, i]),
+        ))
+    o_in = pltpu.make_async_copy(o_hbm, ov, in_sem.at[0])
+    wo_in = pltpu.make_async_copy(wo_hbm, wo, in_sem.at[1])
+    wd_in = pltpu.make_async_copy(wd_hbm, wd, in_sem.at[2])
+    x_in = pltpu.make_async_copy(x_hbm, xv, in_sem.at[3])
+    o_in.start()
+    for pair in g_in:
+        pair[0].start()
+        pair[1].start()
+    wo_in.start()
+    wd_in.start()
+    x_in.start()
+    start_barrier(me_x, me_yz)
+    me = me_x * 4 + me_yz
+    o_in.wait()
+    o_out = []
+    for dx in range(2):
+        for k in range(4):
+            if dx or k:
+                there = lax.rem(me_yz + k, 4)
+                o_out.append(pltpu.make_async_remote_copy(
+                    src_ref=ov.at[there], dst_ref=oa.at[me], send_sem=o_send.at[4 * dx + k], recv_sem=o_recv.at[4 * dx + k],
+                    device_id=(lax.rem(me_x + dx, 2), there), device_id_type=MESH,
+                ))
+    for copy in o_out:
+        copy.start()
+    oa[me] = ov[me_yz]
+
+    h_out = []
+    for i in range(groups):
+        at = pl.ds(span * i, span)
+        g_in[i][0].wait()
+        g_in[i][1].wait()
+        both = (g_own[at] + g_peer[at]).astype(jnp.bfloat16).astype(jnp.float32)
+        hb[i, me_x] = (jax.nn.silu(both[:, :ff]) * both[:, ff:]).astype(jnp.bfloat16)
+        copy = pltpu.make_async_remote_copy(
+            src_ref=hb.at[i, me_x], dst_ref=hb.at[i, me_x], send_sem=h_send.at[i], recv_sem=h_recv.at[i],
+            device_id=(lax.rem(me_x + 1, 2), me_yz), device_id_type=MESH,
+        )
+        copy.start()
+        h_out.append(copy)
+
+    for copy in o_out:
+        copy.wait()
+    for e in range(8):
+        of[owned * e:owned * e + owned] = oa[e].astype(jnp.float32)
+    wo_in.wait()
+    out_part[...] = jnp.dot(of[...].astype(jnp.bfloat16), wo[...], preferred_element_type=jnp.float32)
+    wd_in.wait()
+    x_in.wait()
+
+    y_out = []
+
+    def finish(i):
+        for copy in y_out[i]:
+            copy.wait()
+        total = y_send[i, me_yz]
+        for k in (1, 2, 3):
+            total = total + y_recv[i, lax.rem(me_yz + k, 4)]
+        for e in range(2):
+            at = pl.ds(half * e + span * i, span)
+            y_ref[at, :] = (xv[at, :].astype(jnp.float32) + total[span * e:span * e + span]).astype(jnp.bfloat16)
+
+    for i in range(groups):
+        h_out[i].wait()
+        part = jnp.dot(hb[i].reshape(2 * span, ff), wd[...], preferred_element_type=jnp.float32)
+        part = part + jnp.concatenate([out_part[span * i:span * i + span], out_part[half + span * i:half + span * i + span]], axis=0)
+        for j in range(4):
+            moved = part if j == 0 else pltpu.roll(part, (4 - j) * chunk, 1)
+            y_send[i, j] = moved[:, :chunk]
+        sends = []
+        for k in (1, 2, 3):
+            there = lax.rem(me_yz + k, 4)
+            sends.append(pltpu.make_async_remote_copy(
+                src_ref=y_send.at[i, there], dst_ref=y_recv.at[i, me_yz], send_sem=y_ssem.at[i, k], recv_sem=y_rsem.at[i, k],
+                device_id=(me_x, there), device_id_type=MESH,
+            ))
+        for copy in sends:
+            copy.start()
+        y_out.append(sends)
+        if i:
+            finish(i - 1)
+    finish(groups - 1)
+
+
+def tail(x_in, g_own, g_peer, o_blocks, w_down, w_out):
+    rows, chunk = x_in.shape
+    half = rows // 2
+    span = 16
+    groups = half // span
+    ff, cols = w_down.shape
+    owned = o_blocks.shape[1]
+    o_width = w_out.shape[0]
+    any_spec = pl.BlockSpec(memory_space=pl.ANY)
+    dma = pltpu.SemaphoreType.DMA
+    return pl.pallas_call(
+        tail_kernel,
+        out_shape=jax.ShapeDtypeStruct((rows, chunk), jnp.bfloat16),
+        in_specs=[any_spec] * 6,
+        out_specs=pl.BlockSpec(memory_space=pltpu.VMEM),
+        scratch_shapes=[
+            pltpu.VMEM((rows, chunk), jnp.bfloat16),
+            pltpu.VMEM((half, 2 * ff), jnp.float32),
+            pltpu.VMEM((half, 2 * ff), jnp.float32),
+            pltpu.VMEM((4, owned, o_width), jnp.bfloat16),
+            pltpu.VMEM((8, owned, o_width), jnp.bfloat16),
+            pltpu.VMEM((rows, o_width), jnp.float32),
+            pltpu.VMEM((groups, 2, span, ff), jnp.bfloat16),
+            pltpu.VMEM((ff, cols), jnp.bfloat16),
+            pltpu.VMEM((o_width, cols), jnp.bfloat16),
+            pltpu.VMEM((rows, cols), jnp.float32),
+            pltpu.VMEM((groups, 4, 2 * span, chunk), jnp.float32),
+            pltpu.VMEM((groups, 4, 2 * span, chunk), jnp.float32),
+            dma((4,)), dma((2, groups)), dma((8,)), dma((8,)), dma((groups,)), dma((groups,)), dma((groups, 4)), dma((groups, 4)),
+        ],
+        compiler_params=pltpu.CompilerParams(collective_id=1, has_side_effects=True, vmem_limit_bytes=48 * 1024 * 1024),
+        cost_estimate=pl.CostEstimate(flops=2 * rows * (ff + o_width) * cols, bytes_accessed=2 * (ff + o_width) * cols, transcendentals=half * ff),
+        name='tail',
+    )(x_in, g_own, g_peer, o_blocks, w_down, w_out)
+
+
 def rotary(values, positions):
     half_dim = values.shape[-1] // 2
     inv_freq = ROPE_BASE ** (-jnp.arange(half_dim, dtype=jnp.float32) / half_dim)
@@ -111,20 +446,9 @@
         q_width = w_out.shape[0] * yz_size
         num_heads = q_width // head_dim
         d_model = x_in.shape[1] * x_size * yz_size
-        x_float = x_in.astype(jnp.float32)
-        ln_sums = jnp.stack([jnp.sum(x_float, axis=1), jnp.sum(x_float * x_float, axis=1)], axis=1)
-        ln_sums = lax.psum(ln_sums, all_axes)
-        mean_val = ln_sums[:, 0:1] / d_model
-        var_val = ln_sums[:, 1:2] / d_model - mean_val * mean_val
-        normed = ((x_float - mean_val) * lax.rsqrt(var_val + LN_EPS) * ln_scale).astype(jnp.bfloat16)
-        h_rows = lax.all_gather(normed, 'yz', axis=1, tiled=True)
-        gu_part = jnp.einsum('bd,dgf->bgf', h_rows, w_gate_up, preferred_element_type=jnp.float32)
-        gate_up = lax.psum_scatter(gu_part, 'x', scatter_dimension=2, tiled=True).astype(jnp.bfloat16)
-        hidden = (jax.nn.silu(gate_up[:, 0].astype(jnp.float32)) * gate_up[:, 1].astype(jnp.float32)).astype(jnp.bfloat16)
-        hidden_rows = lax.all_gather(hidden, 'x', axis=1, tiled=True)
-        proj_part = jnp.dot(h_rows, w_attn, preferred_element_type=jnp.float32)
-        proj_rows = lax.psum_scatter(proj_part, 'x', scatter_dimension=0, tiled=True).astype(jnp.bfloat16)
-        proj_local = lax.all_to_all(proj_rows, 'yz', 0, 1, tiled=True)
+        z_blocks, g_send, g_own = head(x_in, ln_scale, w_gate_up, w_attn, d_model)
+        g_peer = lax.ppermute(g_send, 'x', [(0, 1), (1, 0)])
+        proj_local = z_blocks.transpose(1, 0, 2).reshape(local_rows, -1)
         q_raw = proj_local[:, :q_width].reshape(local_rows, num_heads, head_dim)
         k_tok = proj_local[:, q_width:q_width + head_dim]
         v_tok = proj_local[:, q_width + head_dim:]
@@ -133,12 +457,8 @@
         cols = jnp.stack([k_rot, v_tok]).astype(jnp.float32).transpose(0, 2, 1)
         cols = jnp.pad(cols, ((0, 0), (0, 0), (0, 128 - local_rows)))
         attn_out, k_new, v_new = attend(q_rot, cols, k_cache, v_cache, lengths)
-        attn_out = attn_out.reshape(local_rows, q_width)
-        o_rows = lax.all_to_all(attn_out, 'yz', 1, 0, tiled=True)
-        o_all = lax.all_gather(o_rows, 'x', axis=0, tiled=True)
-        mixed_sum = jnp.dot(hidden_rows, w_down, preferred_element_type=jnp.float32) + jnp.dot(o_all, w_out, preferred_element_type=jnp.float32)
-        mixed_sum = lax.psum_scatter(mixed_sum, 'yz', scatter_dimension=1, tiled=True)
-        y_out = (x_float + mixed_sum).astype(jnp.bfloat16)
+        o_blocks = attn_out.reshape(local_rows, yz_size, q_width // yz_size).transpose(1, 0, 2)
+        y_out = tail(x_in, g_own, g_peer, o_blocks, w_down, w_out)
         return y_out, k_new, v_new
 
     row_spec = P(None, all_axes)

time: 166 us -> 107 us (0.64)
  blocking collectives: 65.5 us -> 0 us
  Pallas kernels: 23.7 us -> 79.6 us
  matrix products: 15.9 us -> 0 us
  between operations: 14 us -> 0.75 us
  waiting for transfers between devices: 31.4 us -> 18.2 us
  other arithmetic: 7.28 us -> 0.78 us
  starting transfers between devices: 3.46 us -> 1.49 us
    pallas_call x0 -> x2, Pallas kernels: none -> 55.9 us  [the longest x1 28.1 us: tail(): pl.pallas_call(tail_kernel, out_shape=jax.ShapeDtypeStruct((rows, chunk),...]
    all_gather x3 -> x0, blocking collectives: 33.6 us -> none  [the longest x1 13.4 us: local_step(): hidden_rows = lax.all_gather(hidden, 'x', axis=1, tiled=True)]
    psum x1 -> x0, blocking collectives: 25.1 us -> none  [local_step(): ln_sums = lax.psum(ln_sums, all_axes)]
    unnamed x4 -> x0, waiting for transfers between devices: 21 us -> none
    ppermute x0 -> x1, waiting for transfers between devices: none -> 18.2 us  [local_step(): g_peer = lax.ppermute(g_send, 'x', [(0, 1), (1, 0)])]
    dot_general x4 -> x0, matrix products: 15.9 us -> none  [the longest x1 9.32 us: local_step(): jnp.einsum('bd,dgf->bgf', h_rows, w_gate_up, preferred_element_type=jnp.f...]
    all_to_all x1 -> x0, blocking collectives: 6.9 us -> none  [local_step(): o_rows = lax.all_to_all(attn_out, 'yz', 1, 0, tiled=True)]
    reduce_scatter x2 -> x0, waiting for transfers between devices: 6.08 us -> none  [the longest x1 3.37 us: local_step(): lax.psum_scatter(gu_part, 'x', scatter_dimension=2, tiled=True)]
  transfers between devices with their start and end apart: 4 -> 1, of which waited for: 4 -> 1; matrix products, arithmetic and copies ran while one was open for 8% -> 1% of each run, Pallas kernels for 14% -> 22%
where the time goes in v2:
time: 107 us
  Pallas kernels  79.6 us (74%)
  waiting for transfers between devices  18.2 us (17%)
  local copies, waits for them, and re-layouts  5.9 us (6%)
  starting transfers between devices  1.49 us (1%)
    pallas_call x1, Pallas kernels, tail(): pl.pallas_call(tail_kernel, out_shape=jax.ShapeDtypeStruct((rows, chunk),...  28.1 us
    pallas_call x1, Pallas kernels, head(): pl.pallas_call(functools.partial(head_kernel, d_model), out_shape=(jax.Sh...  27.8 us
    pallas_call x1, Pallas kernels, attend(): pl.pallas_call(functools.partial(attention_kernel, head_dim ** (-0.5)), o...  23.7 us
    ppermute x1, waiting for transfers between devices, local_step(): g_peer = lax.ppermute(g_send, 'x', [(0, 1), (1, 0)])  18.2 us
    unnamed x13, local copies, waits for them, and re-layouts  4.48 us
  transfers between devices with their start and end apart: 1, of which 1 were waited for; matrix products, arithmetic and copies ran while one was open for 1% of the time, Pallas kernels for 22%

profile of v2, /device:TPU:0, one launch (start us, length us, event | category | flops | bytes accessed | tf_op | source)
XLA Modules:
  0.0 106.7 jit_solution(4582015591542158009)
XLA Ops:
  0.6 0.7 reshape.137.scale_hbm
  1.3 0.0 copy-start.1
  1.3 0.9 copy-done.1
  2.2 0.0 copy-start.4
  2.2 1.5 %copy-done.4 = bf16[1280,680]{0,1:T(8,128)(2,1)S(1)} copy-done((bf16[1280,680]{0,1:T(8,128)(2,1)S(1)}, bf16[1280,680]{0,1:T(8,128)(2,1)}, u32[]{:S(2)}) %copy-start.4) | copy-done | bytes 1740824
  3.7 0.0 copy-start.5
  3.7 0.0 copy-start.3
  3.7 27.8 %head.1 = (bf16[4,24,680]{2,1,0:T(8,128)(2,1)S(1)}, f32[96,5120]{1,0:T(8,128)}, f32[96,5120]{1,0:T(8,128)S(1)}) custom-call(bf16[192,320]{1,0:T(8,128)(2,1)S(1)} %copy-done.1, f32[1,320]{1,0:T(1,128)S(1)} %reshape.137.scale_hbm, bf16[1280,2,2560]{2,1,0:T(2,128)(2,1)} %wg_hbm.1, bf16[680,1280]{1,0:T(8,128)(2,1)S(1)} %bitcast.21), custom_call_target="tpu_custom_call" | custom-call | flops 5033164800 | bytes 13107200 | tf_op jit(solution)/shard_map/head/pallas_call | solution.py:262
  31.5 1.5 %collective-permute-start = (f32[96,5120]{1,0:T(8,128)}, f32[96,5120]{1,0:T(8,128)}, u32[]{:S(2)}, u32[]{:S(2)}) collective-permute-start(f32[96,5120]{1,0:T(8,128)} %get-tuple-element.10), channel_id=1, source_target_pairs={{0,4},{4,0},{1,5},{5,1},{2,6},{6,2},{3,7},{7,3}} | collective-permute-start | bytes 5898248 | tf_op jit(solution)/shard_map/ppermute | solution.py:450
  33.0 0.1 copy.22
  33.0 0.1 reshape.138
  33.2 0.1 fusion.8
  33.3 0.0 copy-done.5
  33.3 0.1 fusion.5
  33.4 0.1 maximum_bitcast_fusion
  33.5 0.1 copy.23
  33.7 0.2 reshape.140
  33.9 0.1 multiply_cosine_fusion.1
  34.0 0.2 subtract_convert_fusion
  34.2 0.1 pad_maximum_fusion.q_ref
  34.3 0.0 copy-done.3
  34.4 0.0 copy-start.2
  34.4 23.7 %attend.1 = (bf16[24,32,80]{2,1,0:T(8,128)(2,1)S(1)}, bf16[24,80,4096]{2,1,0:T(8,128)(2,1)}, bf16[24,80,4096]{2,1,0:T(8,128)(2,1)}) custom-call(s32[24]{0:T(128)S(1)} %copy-done.3, bf16[24,32,80]{2,1,0:T(8,128)(2,1)S(1)} %pad_maximum_fusion.q_ref, f32[2,80,128]{2,1,0:T(8,128)S(1)} %pad_convert_fusion.cols_ref, bf16[24,80,4096]{2,1,0:T(8,128)(2,1)} %bitcast.22, ...), custom_call_target="tpu_custom_call" | custom-call | flops 1006632960 | bytes 62914560 | tf_op jit(solution)/shard_map/attend/pallas_call | solution.py:65
  58.0 0.2 reshape.139
  58.3 18.2 %collective-permute-done.peer_hbm = f32[96,5120]{1,0:T(8,128)} collective-permute-done((f32[96,5120]{1,0:T(8,128)}, f32[96,5120]{1,0:T(8,128)}, u32[]{:S(2)}, u32[]{:S(2)}) %collective-permute-start) | collective-permute-done | bytes 1966112 | tf_op jit(solution)/shard_map/ppermute | solution.py:450
  76.5 0.0 copy-done.2
  76.5 0.0 copy-start
  76.5 1.4 %copy-done = bf16[640,1280]{1,0:T(8,128)(2,1)S(1)} copy-done((bf16[640,1280]{1,0:T(8,128)(2,1)S(1)}, bf16[640,1280]{1,0:T(8,128)(2,1)}, u32[]{:S(2)}) %copy-start) | copy-done | bytes 1638424
  77.9 28.1 %tail.1 = bf16[192,320]{1,0:T(8,128)(2,1)S(1)} custom-call(bf16[192,320]{1,0:T(8,128)(2,1)S(1)} %copy-done.2, f32[96,5120]{1,0:T(8,128)S(1)} %get-tuple-element.9.own_hbm, f32[96,5120]{1,0:T(8,128)} %collective-permute-done.peer_hbm, bf16[4,24,640]{2,1,0:T(8,128)(2,1)S(1)} %bitcast.19, bf16[2560,1280]{1,0:T(8,128)(2,1)} %wd_hbm.1, bf16[640,1280]{1,0:T(8,128)(2,1)S(1)} %copy-done), custom_call_target="tpu_custom_call" | custom-call | flops 1572864000 | bytes 8192000 | tf_op jit(solution)/shard_map/tail/pallas_call | solution.py:402
  106.0 0.7 copy.28
  (6 shorter events, 0.1 us)
Async XLA Ops:
  1.3 0.9 copy-start.1
  2.2 1.5 %copy-start.4 = (bf16[1280,680]{0,1:T(8,128)(2,1)S(1)}, bf16[1280,680]{0,1:T(8,128)(2,1)}, u32[]{:S(2)}) copy-start(bf16[1280,680]{0,1:T(8,128)(2,1)} %param.13) | copy-start | bytes 5222404
  3.7 29.6 %copy-start.5 = (s32[24]{0:T(128)S(1)}, s32[24]{0:T(128)}, u32[]{:S(2)}) copy-start(s32[24]{0:T(128)} %param.19) | copy-start | bytes 292
  3.7 30.7 %copy-start.3 = (s32[24]{0:T(128)S(1)}, s32[24]{0:T(128)}, u32[]{:S(2)}) copy-start(s32[24]{0:T(128)} %len_ref.1) | copy-start | bytes 292
  31.5 45.0 %collective-permute-start = (f32[96,5120]{1,0:T(8,128)}, f32[96,5120]{1,0:T(8,128)}, u32[]{:S(2)}, u32[]{:S(2)}) collective-permute-start(f32[96,5120]{1,0:T(8,128)} %get-tuple-element.10), channel_id=1, source_target_pairs={{0,4},{4,0},{1,5},{5,1},{2,6},{6,2},{3,7},{7,3}} | collective-permute-start | bytes 5898248 | tf_op jit(solution)/shard_map/ppermute | solution.py:450
  34.4 42.1 %copy-start.2 = (bf16[192,320]{1,0:T(8,128)(2,1)S(1)}, bf16[192,320]{1,0:T(8,128)(2,1)}, u32[]{:S(2)}) copy-start(bf16[192,320]{1,0:T(8,128)(2,1)} %x_hbm.3) | copy-start | bytes 368644
  76.5 1.4 %copy-start = (bf16[640,1280]{1,0:T(8,128)(2,1)S(1)}, bf16[640,1280]{1,0:T(8,128)(2,1)}, u32[]{:S(2)}) copy-start(bf16[640,1280]{1,0:T(8,128)(2,1)} %wo_hbm.1) | copy-start | bytes 4915204

commit v3 on v2

v3 whole, which is shorter than its diff:
```python
import functools

import jax
import jax.numpy as jnp
from jax import lax
from jax.experimental import pallas as pl
from jax.experimental.pallas import tpu as pltpu
from jax.sharding import PartitionSpec as P

LN_EPS = 1e-6
ROPE_BASE = 10000.0
MESH = pl.DeviceIdType.MESH
VMEM_MOST = 64 * 1024 * 1024 - 64 * 1024
EARLY = 2
ROWS_A = 64


def attention_kernel(scale, len_ref, q_ref, cols_ref, k_hbm, v_hbm, o_ref, ko_hbm, vo_hbm, k_buf, v_buf, in_sem, out_sem):
    rows, _, seq_len = k_buf.shape

    def load(which, b):
        src, dst = ((k_hbm, k_buf), (v_hbm, v_buf))[which]
        return pltpu.make_async_copy(src.at[b], dst.at[b], in_sem.at[which, b])

    def save(which, b):
        src, dst = ((k_buf, ko_hbm), (v_buf, vo_hbm))[which]
        return pltpu.make_async_copy(src.at[b], dst.at[b], out_sem.at[which, b])

    for b in range(rows):
        load(0, b).start()
        load(1, b).start()

    lane = lax.broadcasted_iota(jnp.int32, (1, 128), 1)
    slots = lax.broadcasted_iota(jnp.int32, (1, seq_len), 1)

    def row(b, carry):
        length = len_ref[b]
        window = pl.ds(pl.multiple_of((length // 128) * 128, 128), 128)
        here = lane == length % 128
        for which, buf in enumerate((k_buf, v_buf)):
            load(which, b).wait()
            col = jnp.sum(jnp.where(lane == b, cols_ref[which], 0.0), axis=1, keepdims=True)
            tile = buf[b, :, window].astype(jnp.float32)
            buf[b, :, window] = jnp.where(here, col, tile).astype(jnp.bfloat16)
        scores = jnp.dot(q_ref[b], k_buf[b], preferred_element_type=jnp.float32) * scale
        scores = jnp.where(slots <= length, scores, -1e30)
        top = jnp.max(scores, axis=1, keepdims=True)
        weights = jnp.exp(scores - top)
        total = jnp.sum(weights, axis=1, keepdims=True)
        probs = (weights * (1.0 / total)).astype(jnp.bfloat16)
        save(0, b).start()
        save(1, b).start()
        o_ref[b] = lax.dot_general(probs, v_buf[b], (((1,), (1,)), ((), ())), preferred_element_type=jnp.float32).astype(jnp.bfloat16)
        return carry

    lax.fori_loop(0, rows, row, 0)
    for b in range(rows):
        save(0, b).wait()
        save(1, b).wait()


def attend(q_rot, cols, k_cache, v_cache, lengths):
    rows, heads, head_dim = q_rot.shape
    seq_len = k_cache.shape[1]
    k_t = jnp.swapaxes(k_cache, 1, 2)
    v_t = jnp.swapaxes(v_cache, 1, 2)
    cache = jax.ShapeDtypeStruct((rows, head_dim, seq_len), jnp.bfloat16)
    o, k_new, v_new = pl.pallas_call(
        functools.partial(attention_kernel, head_dim ** -0.5),
        out_shape=(jax.ShapeDtypeStruct((rows, heads, head_dim), jnp.bfloat16), cache, cache),
        in_specs=[
            pl.BlockSpec(memory_space=pltpu.SMEM),
            pl.BlockSpec(memory_space=pltpu.VMEM),
            pl.BlockSpec(memory_space=pltpu.VMEM),
            pl.BlockSpec(memory_space=pl.ANY),
            pl.BlockSpec(memory_space=pl.ANY),
        ],
        out_specs=(pl.BlockSpec(memory_space=pltpu.VMEM), pl.BlockSpec(memory_space=pl.ANY), pl.BlockSpec(memory_space=pl.ANY)),
        scratch_shapes=[
            pltpu.VMEM((rows, head_dim, seq_len), jnp.bfloat16),
            pltpu.VMEM((rows, head_dim, seq_len), jnp.bfloat16),
            pltpu.SemaphoreType.DMA((2, rows)),
            pltpu.SemaphoreType.DMA((2, rows)),
        ],
        compiler_params=pltpu.CompilerParams(vmem_limit_bytes=48 * 1024 * 1024),
        cost_estimate=pl.CostEstimate(
            flops=4 * rows * heads * head_dim * seq_len,
            bytes_accessed=8 * rows * head_dim * seq_len,
            transcendentals=rows * heads * seq_len,
        ),
        name='attend',
    )(lengths, q_rot, cols, k_t, v_t)
    return o, jnp.swapaxes(k_new, 1, 2), jnp.swapaxes(v_new, 1, 2)


def start_barrier(me_x, me_yz):
    barrier = pltpu.get_barrier_semaphore()
    for dx in range(2):
        for k in range(4):
            if dx or k:
                peer = (lax.rem(me_x + dx, 2), lax.rem(me_yz + k, 4))
                pl.semaphore_signal(barrier, inc=1, device_id=peer, device_id_type=MESH)
    pl.semaphore_wait(barrier, 7)


def spread(rows, cols, first):
    i = lax.broadcasted_iota(jnp.int32, (rows, cols), 0)
    c = lax.broadcasted_iota(jnp.int32, (rows, cols), 1)
    return jnp.where(c == 2 * i + first, 1.0, 0.0).astype(jnp.bfloat16)


def head_kernel(
    d_model, early, x_hbm, scale_hbm, wg_hbm, wa_hbm, z_ref, first_hbm, send_a_hbm, send_b_hbm, own_hbm,
    xg, sg, stats, h_buf, hx, hc, wg, wa, z_send, z_own, z_recv, zb, zg, g_first, g_got, g_rest, g_own,
    in_sem, wg_sem, x_send, x_recv, s_send, s_recv, t_send, t_recv, z_sems, a_send, a_recv, f_send, f_recv, out_sem,
):
    me_x = lax.axis_index('x')
    me_yz = lax.axis_index('yz')
    half, chunk = xg.shape[2:]
    rows = 2 * half
    pieces = wg_sem.shape[0]
    depth = wg.shape[0] // pieces
    ff = wg.shape[2]
    wide_cols = 256
    other_x = lax.rem(me_x + 1, 2)
    across = lax.rem(me_yz + 2, 4)
    core = lax.rem(me_yz, 2)
    partner = me_yz + 1 - 2 * core
    order = (other_x, me_x)
    x_in = [
        pltpu.make_async_copy(x_hbm.at[pl.ds(pl.multiple_of(order[p] * half, 32), half)], xg.at[me_yz, order[p]], in_sem.at[p]) for p in range(2)
    ]
    scale_in = pltpu.make_async_copy(scale_hbm, sg.at[me_yz], in_sem.at[2])
    wa_in = pltpu.make_async_copy(wa_hbm, wa, in_sem.at[3])
    wg_in = [
        pltpu.make_async_copy(wg_hbm.at[pl.ds(depth * i, depth)], wg.at[pl.ds(depth * i, depth)], wg_sem.at[i]) for i in range(pieces)
    ]
    for copy in (*x_in, scale_in, wa_in, *wg_in):
        copy.start()
    start_barrier(me_x, me_yz)

    def remote(src, dst, send, recv, to_x, to_yz):
        return pltpu.make_async_remote_copy(
            src_ref=src, dst_ref=dst, send_sem=send, recv_sem=recv, device_id=(to_x, to_yz), device_id_type=MESH,
        )

    def x_copy(kind, p):
        owner = across if kind == 2 else me_yz
        at = xg.at[owner, order[p]]
        return remote(at, at, x_send.at[kind, p], x_recv.at[kind, p], me_x, across if kind == 1 else partner)

    for p in range(2):
        x_in[p].wait()
        x_copy(1, p).start()
        x_copy(0, p).start()
    scale_in.wait()
    s_out = [remote(sg.at[me_yz], sg.at[me_yz], s_send.at[k], s_recv.at[k], me_x, lax.rem(me_yz + k, 4)) for k in (1, 2, 3)]
    for copy in s_out:
        copy.start()
    lane = lax.broadcasted_iota(jnp.int32, (8, 128), 1)
    tile = jnp.zeros((8, 128), jnp.float32)
    for e in range(2):
        mine = xg[me_yz, e].astype(jnp.float32)
        sum_1 = jnp.sum(mine, axis=1, keepdims=True)
        sum_2 = jnp.sum(mine * mine, axis=1, keepdims=True)
        for j in range(half // 8):
            col = e * (half // 8) + j
            tile = jnp.where(lane == col, sum_1[8 * j:8 * j + 8], tile)
            tile = jnp.where(lane == 32 + col, sum_2[8 * j:8 * j + 8], tile)
    me = me_x * 4 + me_yz
    stats[me] = tile
    t_out = [
        remote(stats.at[me], stats.at[me], t_send.at[4 * dx + k], t_recv.at[4 * dx + k], lax.rem(me_x + dx, 2), lax.rem(me_yz + k, 4))
        for dx in range(2) for k in range(4) if dx or k
    ]
    for copy in t_out:
        copy.start()
    wide, thin = spread(128, 256, 0), spread(64, 128, 0)
    wide_u, thin_u = spread(128, 256, 1), spread(64, 128, 1)
    i = lax.broadcasted_iota(jnp.int32, (256, 128), 0)
    c = lax.broadcasted_iota(jnp.int32, (256, 128), 1)
    gather = jnp.where(i == 2 * c, 1.0, 0.0).astype(jnp.bfloat16)
    for copy in t_out:
        copy.wait()
    total = stats[0]
    for i in range(1, 8):
        total = total + stats[i]
    mean_t = total / d_model
    var_t = pltpu.roll(total, 96, 1) / d_model - mean_t * mean_t
    rstd_t = lax.rsqrt(var_t + LN_EPS)
    for copy in s_out:
        copy.wait()

    def normalize(p):
        shift = lax.rem(128 - order[p] * (half // 8), 128)
        mean_p = pltpu.roll(mean_t, shift, 1)
        rstd_p = pltpu.roll(rstd_t, shift, 1)
        mean = jnp.concatenate([mean_p[:, j:j + 1] for j in range(half // 8)], axis=0)
        rstd = jnp.concatenate([rstd_p[:, j:j + 1] for j in range(half // 8)], axis=0)
        x_copy(1, p).wait()
        x_copy(2, p).start()
        x_copy(0, p).wait()
        x_copy(2, p).wait()
        for s in range(4):
            h_buf[s] = ((xg[s, order[p]].astype(jnp.float32) - mean) * rstd * sg[s]).astype(jnp.bfloat16)

    def spread_half(part, g):
        out = pl.ds((2 * part + g) * half, half)
        a, b = ((wide, thin), (wide_u, thin_u))[g]
        for s in range(4):
            base = 2 * chunk * s
            for t in range(2):
                piece = h_buf[s, :, 128 * t:128 * t + 128]
                hx[out, base + 256 * t:base + 256 * t + 256] = jnp.dot(piece, a, preferred_element_type=jnp.float32).astype(jnp.bfloat16)
            piece = h_buf[s, :, 256:320]
            hx[out, base + 512:base + 640] = jnp.dot(piece, b, preferred_element_type=jnp.float32).astype(jnp.bfloat16)

    def project(part):
        src = pl.ds(2 * part * half, half)
        for t in range(4 * chunk // 128):
            hc[:, 128 * t:128 * t + 128] = jnp.dot(hx[src, 256 * t:256 * t + 256], gather, preferred_element_type=jnp.float32).astype(jnp.bfloat16)
        z = lax.dot_general(hc[...], wa[...], (((1,), (1,)), ((), ())), preferred_element_type=jnp.float32)
        return z.reshape(z_send.shape)

    normalize(0)
    spread_half(0, 0)
    wa_in.wait()
    z_send[...] = project(0)
    z_copy = remote(z_send, z_recv, z_sems.at[0], z_sems.at[1], other_x, me_yz)
    z_copy.start()
    spread_half(0, 1)
    normalize(1)
    spread_half(1, 0)
    spread_half(1, 1)
    for copy in wg_in:
        copy.wait()

    def columns(c):
        at = pl.ds(pl.multiple_of(c * wide_cols, wide_cols), wide_cols)
        block = wg[:, :, at].reshape(2 * wg.shape[0], wide_cols)
        out = jnp.dot(hx[...], block, preferred_element_type=jnp.float32)
        up = pl.ds(pl.multiple_of(ff + c * wide_cols, wide_cols), wide_cols)
        g_own[:, at] = out[2 * half:3 * half]
        g_own[:, up] = out[3 * half:]
        return out

    first = []
    for c in range(early):
        out = columns(c)
        g_first[c, :, :wide_cols] = out[:half]
        g_first[c, :, wide_cols:] = out[half:2 * half]
        first.append(remote(g_first.at[c], g_got.at[c], f_send.at[c], f_recv.at[c], other_x, me_yz))
        first[-1].start()

    def rest(c, carry):
        out = columns(c)
        at = (c - early) * wide_cols
        g_rest[:, pl.ds(pl.multiple_of(at, wide_cols), wide_cols)] = out[:half]
        g_rest[:, pl.ds(pl.multiple_of(ff - early * wide_cols + at, wide_cols), wide_cols)] = out[half:2 * half]
        return carry

    lax.fori_loop(early, ff // wide_cols, rest, 0)
    rows_a = send_a_hbm.shape[0]
    save = [
        pltpu.make_async_copy(g_rest.at[pl.ds(0, rows_a)], send_a_hbm, out_sem.at[0]),
        pltpu.make_async_copy(g_rest.at[pl.ds(rows_a, half - rows_a)], send_b_hbm, out_sem.at[1]),
        pltpu.make_async_copy(g_own, own_hbm, out_sem.at[2]),
    ]
    for copy in save:
        copy.start()
    z_own[...] = project(1)
    z_copy.wait()
    zb[...] = (z_own[...] + z_recv[...]).astype(jnp.bfloat16)
    a_out = [remote(zb.at[lax.rem(me_yz + k, 4)], zg.at[me_yz], a_send.at[k], a_recv.at[k], me_x, lax.rem(me_yz + k, 4)) for k in (1, 2, 3)]
    for copy in a_out:
        copy.start()
    zg[me_yz] = zb[me_yz]
    for copy in a_out:
        copy.wait()
    z_ref[...] = zg[...]
    for copy in first:
        copy.wait()
    keep = pltpu.make_async_copy(g_got, first_hbm, out_sem.at[3])
    keep.start()
    keep.wait()
    for copy in save:
        copy.wait()


def head(x_in, ln_scale, w_gate_up, w_attn, d_model, early, rows_a):
    rows, chunk = x_in.shape
    depth, _, ff = w_gate_up.shape
    z_cols = w_attn.shape[1]
    owned = rows // 8
    half = rows // 2
    width = 2 * (ff - 256 * early)
    any_spec = pl.BlockSpec(memory_space=pl.ANY)
    dma = pltpu.SemaphoreType.DMA
    f32, bf16 = jnp.float32, jnp.bfloat16
    return pl.pallas_call(
        functools.partial(head_kernel, d_model, early),
        out_shape=(
            jax.ShapeDtypeStruct((4, owned, z_cols), bf16),
            jax.ShapeDtypeStruct((early, half, 512), f32),
            jax.ShapeDtypeStruct((rows_a, width), f32),
            jax.ShapeDtypeStruct((half - rows_a, width), f32),
            jax.ShapeDtypeStruct((half, 2 * ff), f32),
        ),
        in_specs=[any_spec] * 4,
        out_specs=(pl.BlockSpec(memory_space=pltpu.VMEM), *[any_spec] * 4),
        scratch_shapes=[
            pltpu.VMEM((4, 2, half, chunk), bf16),
            pltpu.VMEM((4, 1, chunk), f32),
            pltpu.VMEM((8, 8, 128), f32),
            pltpu.VMEM((4, half, chunk), bf16),
            pltpu.VMEM((2 * rows, 2 * depth), bf16),
            pltpu.VMEM((half, depth), bf16),
            pltpu.VMEM((depth, 2, ff), bf16),
            pltpu.VMEM((z_cols, depth), bf16),
            pltpu.VMEM((4, owned, z_cols), f32),
            pltpu.VMEM((4, owned, z_cols), f32),
            pltpu.VMEM((4, owned, z_cols), f32),
            pltpu.VMEM((4, owned, z_cols), bf16),
            pltpu.VMEM((4, owned, z_cols), bf16),
            pltpu.VMEM((early, half, 512), f32),
            pltpu.VMEM((early, half, 512), f32),
            pltpu.VMEM((half, width), f32),
            pltpu.VMEM((half, 2 * ff), f32),
            dma((4,)), dma((8,)), dma((3, 2)), dma((3, 2)), dma((4,)), dma((4,)), dma((8,)), dma((8,)), dma((2,)), dma((4,)), dma((4,)),
            dma((early,)), dma((early,)), dma((4,)),
        ],
        compiler_params=pltpu.CompilerParams(collective_id=0, has_side_effects=True, vmem_limit_bytes=VMEM_MOST),
        cost_estimate=pl.CostEstimate(flops=4 * rows * depth * 2 * ff, bytes_accessed=4 * depth * ff, transcendentals=0),
        name='head',
    )(x_in, ln_scale.reshape(1, chunk), w_gate_up, w_attn.T)


def tail_kernel(
    x_hbm, first_hbm, peer_hbm, late_hbm, own_hbm, o_hbm, wd_hbm, wo_hbm, y_ref,
    xv, g_first, g_peer, g_late, g_got, g_own, ov, oa, of, hb, wd, wo, out_part, y_send, y_pair, y_over, y_recv,
    in_sem, g_sem, b_send, b_recv, o_send, o_recv, h_send, h_recv, p_send, p_recv, y_ssem, y_rsem,
):
    me_x = lax.axis_index('x')
    me_yz = lax.axis_index('yz')
    groups, _, span, ff = hb.shape
    rows, chunk = xv.shape
    half = rows // 2
    owned = ov.shape[1]
    early, _, wide = g_first.shape
    wide = wide // 2
    groups_a = g_peer.shape[0] // span
    core = lax.rem(me_yz, 2)
    col = me_yz // 2
    partner = me_yz + 1 - 2 * core
    across = lax.rem(me_yz + 2, 4)
    other_x = lax.rem(me_x + 1, 2)

    def rows_of(i):
        return pl.ds(span * i, span)

    late_in = pltpu.make_async_copy(late_hbm, g_late, in_sem.at[4])
    o_in = pltpu.make_async_copy(o_hbm, ov, in_sem.at[0])
    first_in = pltpu.make_async_copy(first_hbm, g_first, in_sem.at[5])
    own_in = [pltpu.make_async_copy(own_hbm.at[rows_of(i)], g_own.at[rows_of(i)], g_sem.at[0, i]) for i in range(groups)]
    peer_in = [pltpu.make_async_copy(peer_hbm.at[rows_of(i)], g_peer.at[rows_of(i)], g_sem.at[1, i]) for i in range(groups_a)]
    wo_in = pltpu.make_async_copy(wo_hbm, wo, in_sem.at[1])
    wd_in = pltpu.make_async_copy(wd_hbm, wd, in_sem.at[2])
    x_in = pltpu.make_async_copy(x_hbm, xv, in_sem.at[3])
    for copy in (o_in, late_in, first_in):
        copy.start()
    for i in range(groups):
        own_in[i].start()
        if i < groups_a:
            peer_in[i].start()
    for copy in (wo_in, wd_in, x_in):
        copy.start()
    start_barrier(me_x, me_yz)
    me = me_x * 4 + me_yz

    def remote(src, dst, send, recv, to_x, to_yz):
        return pltpu.make_async_remote_copy(
            src_ref=src, dst_ref=dst, send_sem=send, recv_sem=recv, device_id=(to_x, to_yz), device_id_type=MESH,
        )

    o_in.wait()
    o_out = []
    for dx in range(2):
        for k in range(4):
            if dx or k:
                there = lax.rem(me_yz + k, 4)
                o_out.append(remote(ov.at[there], oa.at[me], o_send.at[4 * dx + k], o_recv.at[4 * dx + k], lax.rem(me_x + dx, 2), there))
    for copy in o_out:
        copy.start()
    late_in.wait()
    b_out = [
        remote(g_late.at[rows_of(i)], g_got.at[rows_of(i)], b_send.at[i], b_recv.at[i], other_x, me_yz) for i in range(groups - groups_a)
    ]
    for copy in b_out:
        copy.start()
    oa[me] = ov[me_yz]
    first_in.wait()

    h_out = []

    def activate(i):
        own_in[i].wait()
        at = rows_of(i)
        if i < groups_a:
            peer_in[i].wait()
            got, got_at = g_peer, at
        else:
            b_out[i - groups_a].wait()
            got, got_at = g_got, rows_of(i - groups_a)

        def act(gate, up):
            gate = gate.astype(jnp.bfloat16).astype(jnp.float32)
            up = up.astype(jnp.bfloat16).astype(jnp.float32)
            return (jax.nn.silu(gate) * up).astype(jnp.bfloat16)

        for c in range(early):
            cols = slice(wide * c, wide * c + wide)
            up_cols = slice(ff + wide * c, ff + wide * c + wide)
            hb[i, me_x, :, cols] = act(g_own[at, cols] + g_first[c, at, :wide], g_own[at, up_cols] + g_first[c, at, wide:])
        done = early * wide
        hb[i, me_x, :, done:] = act(g_own[at, done:ff] + got[got_at, :ff - done], g_own[at, ff + done:] + got[got_at, ff - done:])
        copy = remote(hb.at[i, me_x], hb.at[i, me_x], h_send.at[i], h_recv.at[i], other_x, me_yz)
        copy.start()
        h_out.append(copy)

    for i in range(groups_a):
        activate(i)
    for copy in o_out:
        copy.wait()
    for e in range(8):
        of[owned * e:owned * e + owned] = oa[e].astype(jnp.float32)
    wo_in.wait()
    out_part[...] = jnp.dot(of[...].astype(jnp.bfloat16), wo[...], preferred_element_type=jnp.float32)
    for i in range(groups_a, groups):
        activate(i)
    wd_in.wait()
    x_in.wait()

    pair = []
    over = []

    def product(i):
        h_out[i].wait()
        part = jnp.dot(hb[i].reshape(2 * span, ff), wd[...], preferred_element_type=jnp.float32)
        part = part + jnp.concatenate([out_part[span * i:span * i + span], out_part[half + span * i:half + span * i + span]], axis=0)
        for j in range(4):
            moved = part if j == 0 else pltpu.roll(part, (4 - j) * chunk, 1)
            y_send[i, j] = moved[:, :chunk]
        pair.append([
            remote(y_send.at[i, 2 * e + 1 - core], y_pair.at[i, e], p_send.at[i, e], p_recv.at[i, e], me_x, partner) for e in range(2)
        ])
        for copy in pair[i]:
            copy.start()

    def cross(i):
        for copy in pair[i]:
            copy.wait()
        y_over[i] = y_send[i, across] + y_pair[i, 1 - col]
        over.append(remote(y_over.at[i], y_recv.at[i], y_ssem.at[i], y_rsem.at[i], me_x, across))
        over[i].start()

    def finish(i):
        over[i].wait()
        total = y_send[i, me_yz] + y_pair[i, col] + y_recv[i]
        for e in range(2):
            at = pl.ds(half * e + span * i, span)
            y_ref[at, :] = (xv[at, :].astype(jnp.float32) + total[span * e:span * e + span]).astype(jnp.bfloat16)

    for i in range(groups):
        product(i)
        if i >= 1:
            cross(i - 1)
        if i >= 2:
            finish(i - 2)
    cross(groups - 1)
    finish(groups - 2)
    finish(groups - 1)


def tail(x_in, g_first, g_peer, g_late, g_own, o_blocks, w_down, w_out):
    rows, chunk = x_in.shape
    half = rows // 2
    span = 16
    groups = half // span
    ff, cols = w_down.shape
    owned = o_blocks.shape[1]
    o_width = w_out.shape[0]
    any_spec = pl.BlockSpec(memory_space=pl.ANY)
    dma = pltpu.SemaphoreType.DMA
    f32, bf16 = jnp.float32, jnp.bfloat16
    late_groups = g_late.shape[0] // span
    return pl.pallas_call(
        tail_kernel,
        out_shape=jax.ShapeDtypeStruct((rows, chunk), bf16),
        in_specs=[any_spec] * 8,
        out_specs=pl.BlockSpec(memory_space=pltpu.VMEM),
        scratch_shapes=[
            pltpu.VMEM((rows, chunk), bf16),
            pltpu.VMEM(g_first.shape, f32),
            pltpu.VMEM(g_peer.shape, f32),
            pltpu.VMEM(g_late.shape, f32),
            pltpu.VMEM(g_late.shape, f32),
            pltpu.VMEM((half, 2 * ff), f32),
            pltpu.VMEM((4, owned, o_width), bf16),
            pltpu.VMEM((8, owned, o_width), bf16),
            pltpu.VMEM((rows, o_width), f32),
            pltpu.VMEM((groups, 2, span, ff), bf16),
            pltpu.VMEM((ff, cols), bf16),
            pltpu.VMEM((o_width, cols), bf16),
            pltpu.VMEM((rows, cols), f32),
            pltpu.VMEM((groups, 4, 2 * span, chunk), f32),
            pltpu.VMEM((groups, 2, 2 * span, chunk), f32),
            pltpu.VMEM((groups, 2 * span, chunk), f32),
            pltpu.VMEM((groups, 2 * span, chunk), f32),
            dma((6,)), dma((2, groups)), dma((late_groups,)), dma((late_groups,)), dma((8,)), dma((8,)), dma((groups,)), dma((groups,)),
            dma((groups, 2)), dma((groups, 2)), dma((groups,)), dma((groups,)),
        ],
        compiler_params=pltpu.CompilerParams(collective_id=1, has_side_effects=True, vmem_limit_bytes=VMEM_MOST),
        cost_estimate=pl.CostEstimate(flops=2 * rows * (ff + o_width) * cols, bytes_accessed=2 * (ff + o_width) * cols, transcendentals=half * ff),
        name='tail',
    )(x_in, g_first, g_peer, g_late, g_own, o_blocks, w_down, w_out)


def rotary(values, positions):
    half_dim = values.shape[-1] // 2
    inv_freq = ROPE_BASE ** (-jnp.arange(half_dim, dtype=jnp.float32) / half_dim)
    angles = positions.astype(jnp.float32)[:, None, None] * inv_freq
    cos_part = jnp.cos(angles)
    sin_part = jnp.sin(angles)
    lo_half = values[..., :half_dim]
    hi_half = values[..., half_dim:]
    return jnp.concatenate([lo_half * cos_part - hi_half * sin_part, hi_half * cos_part + lo_half * sin_part], axis=-1)


def solution(mesh):
    x_size = mesh.shape['x']
    yz_size = mesh.shape['yz']
    all_axes = ('x', 'yz')

    def local_step(x_in, ln_scale, w_gate_up, w_attn, w_down, w_out, k_cache, v_cache, lengths, positions):
        local_rows, seq_len, head_dim = k_cache.shape
        q_width = w_out.shape[0] * yz_size
        num_heads = q_width // head_dim
        d_model = x_in.shape[1] * x_size * yz_size
        z_blocks, g_first, g_send, g_late, g_own = head(x_in, ln_scale, w_gate_up, w_attn, d_model, EARLY, ROWS_A)
        g_peer = lax.ppermute(g_send, 'x', [(0, 1), (1, 0)])
        proj_local = z_blocks.transpose(1, 0, 2).reshape(local_rows, -1)
        q_raw = proj_local[:, :q_width].reshape(local_rows, num_heads, head_dim)
        k_tok = proj_local[:, q_width:q_width + head_dim]
        v_tok = proj_local[:, q_width + head_dim:]
        q_rot = rotary(q_raw.astype(jnp.float32), positions).astype(jnp.bfloat16)
        k_rot = rotary(k_tok[:, None, :].astype(jnp.float32), positions)[:, 0].astype(jnp.bfloat16)
        cols = jnp.stack([k_rot, v_tok]).astype(jnp.float32).transpose(0, 2, 1)
        cols = jnp.pad(cols, ((0, 0), (0, 0), (0, 128 - local_rows)))
        attn_out, k_new, v_new = attend(q_rot, cols, k_cache, v_cache, lengths)
        o_blocks = attn_out.reshape(local_rows, yz_size, q_width // yz_size).transpose(1, 0, 2)
        y_out = tail(x_in, g_first, g_peer, g_late, g_own, o_blocks, w_down, w_out)
        return y_out, k_new, v_new

    row_spec = P(None, all_axes)
    vec_spec = P(all_axes)
    cache_spec = P(all_axes, None, None)
    return jax.shard_map(
        local_step,
        mesh=mesh,
        in_specs=(row_spec, vec_spec, P('x', None, 'yz'), P('x', 'yz'), P('yz', 'x'), P('yz', 'x'), cache_spec, cache_spec, vec_spec, vec_spec),
        out_specs=(row_spec, cache_spec, cache_spec),
        check_vma=False,
    )
```

time: 107 us -> 104 us (0.972)
  waiting for transfers between devices: 18.2 us -> 0.01 us
  Pallas kernels: 79.6 us -> 94 us
    ppermute x1, waiting for transfers between devices: 18.2 us -> 0.01 us  [local_step(): g_peer = lax.ppermute(g_send, 'x', [(0, 1), (1, 0)])]
    pallas_call x1, Pallas kernels: 28.1 us -> 37.6 us  [tail(): pl.pallas_call(tail_kernel, out_shape=jax.ShapeDtypeStruct((rows, chunk),...]
    pallas_call x1, Pallas kernels: 27.8 us -> 32.8 us  [head(): pl.pallas_call(functools.partial(head_kernel, d_model, early), out_shape=...]
    unnamed x13 -> x3, local copies, waits for them, and re-layouts: 4.48 us -> 2.24 us
  transfers between devices with their start and end apart: 1 -> 1, of which waited for: 1 -> 0; matrix products, arithmetic and copies ran while one was open for 1% -> 4% of each run, Pallas kernels for 22% -> 23%
where the time goes in v3:
time: 104 us
  Pallas kernels  94 us (90%)
  local copies, waits for them, and re-layouts  5.78 us (6%)
  starting transfers between devices  1.55 us (1%)
  other arithmetic  1.44 us (1%)
    pallas_call x1, Pallas kernels, tail(): pl.pallas_call(tail_kernel, out_shape=jax.ShapeDtypeStruct((rows, chunk),...  37.6 us
    pallas_call x1, Pallas kernels, head(): pl.pallas_call(functools.partial(head_kernel, d_model, early), out_shape=...  32.8 us
    pallas_call x1, Pallas kernels, attend(): pl.pallas_call(functools.partial(attention_kernel, head_dim ** (-0.5)), o...  23.7 us
    unnamed x3, local copies, waits for them, and re-layouts  2.24 us
  transfers between devices with their start and end apart: 1, of which 0 were waited for; matrix products, arithmetic and copies ran while one was open for 4% of the time, Pallas kernels for 23%

profile of v3, /device:TPU:0, one launch (start us, length us, event | category | flops | bytes accessed | tf_op | source)
XLA Modules:
  0.0 103.5 jit_solution(4508319855511952922)
XLA Ops:
  0.6 1.2 %reshape.137.scale_hbm = f32[1,320]{1,0:T(1,128)} reshape(f32[320]{0:T(512)} %param.11) | data formatting | bytes 2560 | tf_op jit(solution)/shard_map/reshape | solution.py:335
  1.9 32.8 %head.1 = (bf16[4,24,680]{2,1,0:T(8,128)(2,1)}, f32[2,96,512]{2,1,0:T(8,128)}, f32[64,4096]{1,0:T(8,128)}, f32[32,4096]{1,0:T(8,128)}, f32[96,5120]{1,0:T(8,128)}) custom-call(bf16[192,320]{1,0:T(8,128)(2,1)} %x_hbm.3, f32[1,320]{1,0:T(1,128)} %reshape.137.scale_hbm, bf16[1280,2,2560]{2,1,0:T(2,128)(2,1)} %wg_hbm.1, bf16[680,1280]{1,0:T(8,128)(2,1)} %bitcast.26), custom_call_target="tpu_custom_call" | custom-call | flops 5033164800 | bytes 13107200 | tf_op jit(solution)/shard_map/head/pallas_call | solution.py:300
  34.7 1.6 %collective-permute-start = (f32[64,4096]{1,0:T(8,128)}, f32[64,4096]{1,0:T(8,128)}, u32[]{:S(2)}, u32[]{:S(2)}) collective-permute-start(f32[64,4096]{1,0:T(8,128)} %get-tuple-element.12), channel_id=1, source_target_pairs={{0,4},{4,0},{1,5},{5,1},{2,6},{6,2},{3,7},{7,3}} | collective-permute-start | bytes 3145736 | tf_op jit(solution)/shard_map/ppermute | solution.py:550
  36.3 1.0 copy.22
  37.2 0.1 reshape.138
  37.4 0.1 fusion.8
  37.5 0.7 convert_element_type.33
  38.2 0.1 fusion.5
  38.3 0.1 maximum_bitcast_fusion
  38.4 0.1 copy.23
  38.5 0.2 reshape.140
  38.7 0.1 multiply_cosine_fusion.1
  38.8 0.2 subtract_convert_fusion
  39.0 0.1 pad_maximum_fusion.q_ref
  39.2 0.0 copy-start
  39.2 0.6 copy-done
  39.8 23.7 %attend.1 = (bf16[24,32,80]{2,1,0:T(8,128)(2,1)S(1)}, bf16[24,80,4096]{2,1,0:T(8,128)(2,1)}, bf16[24,80,4096]{2,1,0:T(8,128)(2,1)}) custom-call(s32[24]{0:T(128)S(1)} %copy-done, bf16[24,32,80]{2,1,0:T(8,128)(2,1)S(1)} %pad_maximum_fusion.q_ref, f32[2,80,128]{2,1,0:T(8,128)S(1)} %pad_convert_fusion.cols_ref, bf16[24,80,4096]{2,1,0:T(8,128)(2,1)} %bitcast.19, ...), custom_call_target="tpu_custom_call" | custom-call | flops 1006632960 | bytes 62914560 | tf_op jit(solution)/shard_map/attend/pallas_call | solution.py:68
  63.5 0.2 reshape.139
  63.7 0.7 copy.26
  64.4 0.0 collective-permute-done.peer_hbm
  64.4 37.6 %tail.1 = bf16[192,320]{1,0:T(8,128)(2,1)} custom-call(bf16[192,320]{1,0:T(8,128)(2,1)} %x_hbm.3, f32[2,96,512]{2,1,0:T(8,128)} %get-tuple-element.11.first_hbm, f32[64,4096]{1,0:T(8,128)} %collective-permute-done.peer_hbm, f32[32,4096]{1,0:T(8,128)} %get-tuple-element.13.late_hbm, f32[96,5120]{1,0:T(8,128)} %get-tuple-element.14.own_hbm, ...), custom_call_target="tpu_custom_call" | custom-call | flops 1572864000 | bytes 8192000 | tf_op jit(solution)/shard_map/tail/pallas_call | solution.py:496
  101.9 1.6 %copy.28 = bf16[192,320]{1,0:T(8,128)(2,1)} copy(bf16[192,320]{1,0:T(8,128)(2,1)} %tail.1) | data formatting | bytes 245760
  (4 shorter events, 0.0 us)
Async XLA Ops:
  34.7 29.7 %collective-permute-start = (f32[64,4096]{1,0:T(8,128)}, f32[64,4096]{1,0:T(8,128)}, u32[]{:S(2)}, u32[]{:S(2)}) collective-permute-start(f32[64,4096]{1,0:T(8,128)} %get-tuple-element.12), channel_id=1, source_target_pairs={{0,4},{4,0},{1,5},{5,1},{2,6},{6,2},{3,7},{7,3}} | collective-permute-start | bytes 3145736 | tf_op jit(solution)/shard_map/ppermute | solution.py:550
  39.2 0.7 copy-start

commit v4 on v3

--- a/solution.py
+++ b/solution.py
@@ -12,7 +12,7 @@
 MESH = pl.DeviceIdType.MESH
 VMEM_MOST = 64 * 1024 * 1024 - 64 * 1024
 EARLY = 2
-ROWS_A = 64
+ROWS_A = 80
 
 
 def attention_kernel(scale, len_ref, q_ref, cols_ref, k_hbm, v_hbm, o_ref, ko_hbm, vo_hbm, k_buf, v_buf, in_sem, out_sem):
@@ -151,12 +151,6 @@
 
     for p in range(2):
         x_in[p].wait()
-        x_copy(1, p).start()
-        x_copy(0, p).start()
-    scale_in.wait()
-    s_out = [remote(sg.at[me_yz], sg.at[me_yz], s_send.at[k], s_recv.at[k], me_x, lax.rem(me_yz + k, 4)) for k in (1, 2, 3)]
-    for copy in s_out:
-        copy.start()
     lane = lax.broadcasted_iota(jnp.int32, (8, 128), 1)
     tile = jnp.zeros((8, 128), jnp.float32)
     for e in range(2):
@@ -175,6 +169,13 @@
     ]
     for copy in t_out:
         copy.start()
+    scale_in.wait()
+    s_out = [remote(sg.at[me_yz], sg.at[me_yz], s_send.at[k], s_recv.at[k], me_x, lax.rem(me_yz + k, 4)) for k in (1, 2, 3)]
+    for copy in s_out:
+        copy.start()
+    for p in range(2):
+        x_copy(1, p).start()
+        x_copy(0, p).start()
     wide, thin = spread(128, 256, 0), spread(64, 128, 0)
     wide_u, thin_u = spread(128, 256, 1), spread(64, 128, 1)
     i = lax.broadcasted_iota(jnp.int32, (256, 128), 0)
@@ -337,8 +338,8 @@
 
 def tail_kernel(
     x_hbm, first_hbm, peer_hbm, late_hbm, own_hbm, o_hbm, wd_hbm, wo_hbm, y_ref,
-    xv, g_first, g_peer, g_late, g_got, g_own, ov, oa, of, hb, wd, wo, out_part, y_send, y_pair, y_over, y_recv,
-    in_sem, g_sem, b_send, b_recv, o_send, o_recv, h_send, h_recv, p_send, p_recv, y_ssem, y_rsem,
+    xv, g_first, g_peer, g_late, g_got, g_own, ov, oa, of, hb, wd, wo, out_part, y_send, y_pair, y_over, y_recv, y_last,
+    in_sem, g_sem, b_send, b_recv, o_send, o_recv, h_send, h_recv, p_send, p_recv, y_ssem, y_rsem, l_send, l_recv,
 ):
     me_x = lax.axis_index('x')
     me_yz = lax.axis_index('yz')
@@ -366,7 +367,7 @@
     wo_in = pltpu.make_async_copy(wo_hbm, wo, in_sem.at[1])
     wd_in = pltpu.make_async_copy(wd_hbm, wd, in_sem.at[2])
     x_in = pltpu.make_async_copy(x_hbm, xv, in_sem.at[3])
-    for copy in (o_in, late_in, first_in):
+    for copy in (late_in, o_in, first_in):
         copy.start()
     for i in range(groups):
         own_in[i].start()
@@ -382,6 +383,12 @@
             src_ref=src, dst_ref=dst, send_sem=send, recv_sem=recv, device_id=(to_x, to_yz), device_id_type=MESH,
         )
 
+    late_in.wait()
+    b_out = [
+        remote(g_late.at[rows_of(i)], g_got.at[rows_of(i)], b_send.at[i], b_recv.at[i], other_x, me_yz) for i in range(groups - groups_a)
+    ]
+    for copy in b_out:
+        copy.start()
     o_in.wait()
     o_out = []
     for dx in range(2):
@@ -390,12 +397,6 @@
                 there = lax.rem(me_yz + k, 4)
                 o_out.append(remote(ov.at[there], oa.at[me], o_send.at[4 * dx + k], o_recv.at[4 * dx + k], lax.rem(me_x + dx, 2), there))
     for copy in o_out:
-        copy.start()
-    late_in.wait()
-    b_out = [
-        remote(g_late.at[rows_of(i)], g_got.at[rows_of(i)], b_send.at[i], b_recv.at[i], other_x, me_yz) for i in range(groups - groups_a)
-    ]
-    for copy in b_out:
         copy.start()
     oa[me] = ov[me_yz]
     first_in.wait()
@@ -440,8 +441,7 @@
     wd_in.wait()
     x_in.wait()
 
-    pair = []
-    over = []
+    pair, over, last = [], [], []
 
     def product(i):
         h_out[i].wait()
@@ -450,11 +450,17 @@
         for j in range(4):
             moved = part if j == 0 else pltpu.roll(part, (4 - j) * chunk, 1)
             y_send[i, j] = moved[:, :chunk]
-        pair.append([
-            remote(y_send.at[i, 2 * e + 1 - core], y_pair.at[i, e], p_send.at[i, e], p_recv.at[i, e], me_x, partner) for e in range(2)
-        ])
-        for copy in pair[i]:
-            copy.start()
+        if i < groups - 1:
+            pair.append([
+                remote(y_send.at[i, 2 * e + 1 - core], y_pair.at[i, e], p_send.at[i, e], p_recv.at[i, e], me_x, partner) for e in range(2)
+            ])
+            for copy in pair[i]:
+                copy.start()
+        else:
+            for k in (2, 3, 1):
+                there = lax.rem(me_yz + k, 4)
+                last.append(remote(y_send.at[i, there], y_last.at[me_yz], l_send.at[k], l_recv.at[k], me_x, there))
+                last[-1].start()
 
     def cross(i):
         for copy in pair[i]:
@@ -464,8 +470,15 @@
         over[i].start()
 
     def finish(i):
-        over[i].wait()
-        total = y_send[i, me_yz] + y_pair[i, col] + y_recv[i]
+        if i < groups - 1:
+            over[i].wait()
+            total = y_send[i, me_yz] + y_pair[i, col] + y_recv[i]
+        else:
+            for copy in last:
+                copy.wait()
+            total = y_send[i, me_yz]
+            for k in (1, 2, 3):
+                total = total + y_last[lax.rem(me_yz + k, 4)]
         for e in range(2):
             at = pl.ds(half * e + span * i, span)
             y_ref[at, :] = (xv[at, :].astype(jnp.float32) + total[span * e:span * e + span]).astype(jnp.bfloat16)
@@ -476,7 +489,6 @@
             cross(i - 1)
         if i >= 2:
             finish(i - 2)
-    cross(groups - 1)
     finish(groups - 2)
     finish(groups - 1)
 
@@ -516,10 +528,11 @@
             pltpu.VMEM((groups, 2, 2 * span, chunk), f32),
             pltpu.VMEM((groups, 2 * span, chunk), f32),
             pltpu.VMEM((groups, 2 * span, chunk), f32),
+            pltpu.VMEM((4, 2 * span, chunk), f32),
             dma((6,)), dma((2, groups)), dma((late_groups,)), dma((late_groups,)), dma((8,)), dma((8,)), dma((groups,)), dma((groups,)),
-            dma((groups, 2)), dma((groups, 2)), dma((groups,)), dma((groups,)),
+            dma((groups, 2)), dma((groups, 2)), dma((groups,)), dma((groups,)), dma((4,)), dma((4,)),
         ],
-        compiler_params=pltpu.CompilerParams(collective_id=1, has_side_effects=True, vmem_limit_bytes=VMEM_MOST),
+        compiler_params=pltpu.CompilerParams(collective_id=1, has_side_effects=True, vmem_limit_bytes=VMEM_MOST - 1536 * 1024),
         cost_estimate=pl.CostEstimate(flops=2 * rows * (ff + o_width) * cols, bytes_accessed=2 * (ff + o_width) * cols, transcendentals=half * ff),
         name='tail',
     )(x_in, g_first, g_peer, g_late, g_own, o_blocks, w_down, w_out)

time: 104 us -> 99.4 us (0.956)
  Pallas kernels: 94 us -> 87.8 us
  waiting for transfers between devices: 0.01 us -> 1.87 us
  local copies, waits for them, and re-layouts: 5.78 us -> 6.84 us
    pallas_call x1, Pallas kernels: 37.6 us -> 31.9 us  [tail(): pl.pallas_call(tail_kernel, out_shape=jax.ShapeDtypeStruct((rows, chunk),...]
    ppermute x1, waiting for transfers between devices: 0.01 us -> 1.87 us  [local_step(): g_peer = lax.ppermute(g_send, 'x', [(0, 1), (1, 0)])]
    unnamed x3 -> x5, local copies, waits for them, and re-layouts: 2.24 us -> 3.31 us
  transfers between devices with their start and end apart: 1 -> 1, of which waited for: 0 -> 1; matrix products, arithmetic and copies ran while one was open for 4% -> 4% of each run, Pallas kernels for 23% -> 24%
where the time goes in v4:
time: 99.4 us; the launch traced here: 99.2 us
  Pallas kernels  87.8 us (88%)
  local copies, waits for them, and re-layouts  6.84 us (7%)
  waiting for transfers between devices  1.87 us (2%)
  other arithmetic  1.43 us (1%)
    pallas_call x1, Pallas kernels, head(): pl.pallas_call(functools.partial(head_kernel, d_model, early), out_shape=...  32.3 us
    pallas_call x1, Pallas kernels, tail(): pl.pallas_call(tail_kernel, out_shape=jax.ShapeDtypeStruct((rows, chunk),...  31.9 us
    pallas_call x1, Pallas kernels, attend(): pl.pallas_call(functools.partial(attention_kernel, head_dim ** (-0.5)), o...  23.6 us
    unnamed x5, local copies, waits for them, and re-layouts  3.31 us
  transfers between devices with their start and end apart: 1, of which 1 were waited for; matrix products, arithmetic and copies ran while one was open for 4% of the time, Pallas kernels for 24%

profile of v4, /device:TPU:0, one launch (start us, length us, event | category | flops | bytes accessed | tf_op | source)
XLA Modules:
  0.0 99.2 jit_solution(335086148485351738)
XLA Ops:
  0.6 1.2 %reshape.137.scale_hbm = f32[1,320]{1,0:T(1,128)} reshape(f32[320]{0:T(512)} %param.11) | data formatting | bytes 2560 | tf_op jit(solution)/shard_map/reshape | solution.py:336
  1.9 32.3 %head.1 = (bf16[4,24,680]{2,1,0:T(8,128)(2,1)}, f32[2,96,512]{2,1,0:T(8,128)}, f32[80,4096]{1,0:T(8,128)}, f32[16,4096]{1,0:T(8,128)}, f32[96,5120]{1,0:T(8,128)}) custom-call(bf16[192,320]{1,0:T(8,128)(2,1)} %x_hbm.3, f32[1,320]{1,0:T(1,128)} %reshape.137.scale_hbm, bf16[1280,2,2560]{2,1,0:T(2,128)(2,1)} %wg_hbm.1, bf16[680,1280]{1,0:T(8,128)(2,1)} %bitcast.26), custom_call_target="tpu_custom_call" | custom-call | flops 5033164800 | bytes 13107200 | tf_op jit(solution)/shard_map/head/pallas_call | solution.py:301
  34.2 0.5 collective-permute-start
  34.7 0.7 convert_element_type.33
  35.4 1.0 copy.22
  36.3 0.1 reshape.138
  36.5 0.1 fusion.8
  36.6 0.1 fusion.5
  36.7 0.1 maximum_bitcast_fusion
  36.8 0.1 copy.23
  36.9 0.2 reshape.140
  37.2 0.1 multiply_cosine_fusion.1
  37.3 0.2 subtract_convert_fusion
  37.5 0.1 pad_maximum_fusion.q_ref
  37.6 0.0 copy-start
  37.6 0.6 copy-done
  38.3 23.6 %attend.1 = (bf16[24,32,80]{2,1,0:T(8,128)(2,1)S(1)}, bf16[24,80,4096]{2,1,0:T(8,128)(2,1)}, bf16[24,80,4096]{2,1,0:T(8,128)(2,1)}) custom-call(s32[24]{0:T(128)S(1)} %copy-done, bf16[24,32,80]{2,1,0:T(8,128)(2,1)S(1)} %pad_maximum_fusion.q_ref, f32[2,80,128]{2,1,0:T(8,128)S(1)} %pad_convert_fusion.cols_ref, bf16[24,80,4096]{2,1,0:T(8,128)(2,1)} %bitcast.19, ...), custom_call_target="tpu_custom_call" | custom-call | flops 1006632960 | bytes 62914560 | tf_op jit(solution)/shard_map/attend/pallas_call | solution.py:68
  61.9 0.2 reshape.139
  62.1 0.7 copy.26
  62.8 1.9 %collective-permute-done.peer_hbm = f32[80,4096]{1,0:T(8,128)S(1)} collective-permute-done((f32[80,4096]{1,0:T(8,128)}, f32[80,4096]{1,0:T(8,128)S(1)}, u32[]{:S(2)}, u32[]{:S(2)}) %collective-permute-start) | collective-permute-done | bytes 1310752 | tf_op jit(solution)/shard_map/ppermute | solution.py:563
  64.7 0.0 copy-start.1
  64.7 1.1 %copy-done.1 = f32[80,4096]{1,0:T(8,128)} copy-done((f32[80,4096]{1,0:T(8,128)}, f32[80,4096]{1,0:T(8,128)S(1)}, u32[]{:S(2)}) %copy-start.1) | copy-done | bytes 1310744
  65.7 31.9 %tail.1 = bf16[192,320]{1,0:T(8,128)(2,1)} custom-call(bf16[192,320]{1,0:T(8,128)(2,1)} %x_hbm.3, f32[2,96,512]{2,1,0:T(8,128)} %get-tuple-element.11.first_hbm, f32[80,4096]{1,0:T(8,128)} %copy-done.1, f32[16,4096]{1,0:T(8,128)} %get-tuple-element.13.late_hbm, f32[96,5120]{1,0:T(8,128)} %get-tuple-element.14.own_hbm, bf16[4,24,640]{2,1,0:T(8,128)(2,1)} %bitcast.21, ...), custom_call_target="tpu_custom_call" | custom-call | flops 1572864000 | bytes 8192000 | tf_op jit(solution)/shard_map/tail/pallas_call | solution.py:508
  97.7 1.6 %copy.28 = bf16[192,320]{1,0:T(8,128)(2,1)} copy(bf16[192,320]{1,0:T(8,128)(2,1)} %tail.1) | data formatting | bytes 245760
  (4 shorter events, 0.1 us)
Async XLA Ops:
  34.2 30.5 %collective-permute-start = (f32[80,4096]{1,0:T(8,128)}, f32[80,4096]{1,0:T(8,128)S(1)}, u32[]{:S(2)}, u32[]{:S(2)}) collective-permute-start(f32[80,4096]{1,0:T(8,128)} %get-tuple-element.12), channel_id=1, source_target_pairs={{0,4},{4,0},{1,5},{5,1},{2,6},{6,2},{3,7},{7,3}} | collective-permute-start | bytes 3932168 | tf_op jit(solution)/shard_map/ppermute | solution.py:563
  37.6 0.7 copy-start
  64.7 1.1 %copy-start.1 = (f32[80,4096]{1,0:T(8,128)}, f32[80,4096]{1,0:T(8,128)S(1)}, u32[]{:S(2)}) copy-start(f32[80,4096]{1,0:T(8,128)S(1)} %collective-permute-done.peer_hbm) | copy-start | bytes 3932164

commit v5 on v4

--- a/solution.py
+++ b/solution.py
@@ -100,7 +100,7 @@
             if dx or k:
                 peer = (lax.rem(me_x + dx, 2), lax.rem(me_yz + k, 4))
                 pl.semaphore_signal(barrier, inc=1, device_id=peer, device_id_type=MESH)
-    pl.semaphore_wait(barrier, 7)
+    return lambda: pl.semaphore_wait(barrier, 7)
 
 
 def spread(rows, cols, first):
@@ -110,8 +110,8 @@
 
 
 def head_kernel(
-    d_model, early, x_hbm, scale_hbm, wg_hbm, wa_hbm, z_ref, first_hbm, send_a_hbm, send_b_hbm, own_hbm,
-    xg, sg, stats, h_buf, hx, hc, wg, wa, z_send, z_own, z_recv, zb, zg, g_first, g_got, g_rest, g_own,
+    d_model, early, x_hbm, scale_hbm, wg_hbm, wa_hbm, z_hbm, first_hbm, send_a_hbm, send_b_hbm, own_hbm,
+    xg, scale_row, sg, stats, h_buf, hx, hc, wg, wa, z_send, z_own, z_recv, zb, zg, g_first, g_rest, g_own,
     in_sem, wg_sem, x_send, x_recv, s_send, s_recv, t_send, t_recv, z_sems, a_send, a_recv, f_send, f_recv, out_sem,
 ):
     me_x = lax.axis_index('x')
@@ -130,14 +130,14 @@
     x_in = [
         pltpu.make_async_copy(x_hbm.at[pl.ds(pl.multiple_of(order[p] * half, 32), half)], xg.at[me_yz, order[p]], in_sem.at[p]) for p in range(2)
     ]
-    scale_in = pltpu.make_async_copy(scale_hbm, sg.at[me_yz], in_sem.at[2])
+    scale_in = pltpu.make_async_copy(scale_hbm, scale_row, in_sem.at[2])
     wa_in = pltpu.make_async_copy(wa_hbm, wa, in_sem.at[3])
     wg_in = [
         pltpu.make_async_copy(wg_hbm.at[pl.ds(depth * i, depth)], wg.at[pl.ds(depth * i, depth)], wg_sem.at[i]) for i in range(pieces)
     ]
     for copy in (*x_in, scale_in, wa_in, *wg_in):
         copy.start()
-    start_barrier(me_x, me_yz)
+    others_ready = start_barrier(me_x, me_yz)
 
     def remote(src, dst, send, recv, to_x, to_yz):
         return pltpu.make_async_remote_copy(
@@ -163,6 +163,7 @@
             tile = jnp.where(lane == 32 + col, sum_2[8 * j:8 * j + 8], tile)
     me = me_x * 4 + me_yz
     stats[me] = tile
+    others_ready()
     t_out = [
         remote(stats.at[me], stats.at[me], t_send.at[4 * dx + k], t_recv.at[4 * dx + k], lax.rem(me_x + dx, 2), lax.rem(me_yz + k, 4))
         for dx in range(2) for k in range(4) if dx or k
@@ -170,6 +171,7 @@
     for copy in t_out:
         copy.start()
     scale_in.wait()
+    sg[me_yz] = scale_row[...].reshape(1, chunk)
     s_out = [remote(sg.at[me_yz], sg.at[me_yz], s_send.at[k], s_recv.at[k], me_x, lax.rem(me_yz + k, 4)) for k in (1, 2, 3)]
     for copy in s_out:
         copy.start()
@@ -250,7 +252,7 @@
         out = columns(c)
         g_first[c, :, :wide_cols] = out[:half]
         g_first[c, :, wide_cols:] = out[half:2 * half]
-        first.append(remote(g_first.at[c], g_got.at[c], f_send.at[c], f_recv.at[c], other_x, me_yz))
+        first.append(remote(g_first.at[c], first_hbm.at[c], f_send.at[c], f_recv.at[c], other_x, me_yz))
         first[-1].start()
 
     def rest(c, carry):
@@ -278,12 +280,10 @@
     zg[me_yz] = zb[me_yz]
     for copy in a_out:
         copy.wait()
-    z_ref[...] = zg[...]
+    save.append(pltpu.make_async_copy(zg, z_hbm, out_sem.at[3]))
+    save[-1].start()
     for copy in first:
         copy.wait()
-    keep = pltpu.make_async_copy(g_got, first_hbm, out_sem.at[3])
-    keep.start()
-    keep.wait()
     for copy in save:
         copy.wait()
 
@@ -308,9 +308,10 @@
             jax.ShapeDtypeStruct((half, 2 * ff), f32),
         ),
         in_specs=[any_spec] * 4,
-        out_specs=(pl.BlockSpec(memory_space=pltpu.VMEM), *[any_spec] * 4),
+        out_specs=[any_spec] * 5,
         scratch_shapes=[
             pltpu.VMEM((4, 2, half, chunk), bf16),
+            pltpu.VMEM((chunk,), f32),
             pltpu.VMEM((4, 1, chunk), f32),
             pltpu.VMEM((8, 8, 128), f32),
             pltpu.VMEM((4, half, chunk), bf16),
@@ -324,7 +325,6 @@
             pltpu.VMEM((4, owned, z_cols), bf16),
             pltpu.VMEM((4, owned, z_cols), bf16),
             pltpu.VMEM((early, half, 512), f32),
-            pltpu.VMEM((early, half, 512), f32),
             pltpu.VMEM((half, width), f32),
             pltpu.VMEM((half, 2 * ff), f32),
             dma((4,)), dma((8,)), dma((3, 2)), dma((3, 2)), dma((4,)), dma((4,)), dma((8,)), dma((8,)), dma((2,)), dma((4,)), dma((4,)),
@@ -333,18 +333,18 @@
         compiler_params=pltpu.CompilerParams(collective_id=0, has_side_effects=True, vmem_limit_bytes=VMEM_MOST),
         cost_estimate=pl.CostEstimate(flops=4 * rows * depth * 2 * ff, bytes_accessed=4 * depth * ff, transcendentals=0),
         name='head',
-    )(x_in, ln_scale.reshape(1, chunk), w_gate_up, w_attn.T)
+    )(x_in, ln_scale, w_gate_up, w_attn.T)
 
 
 def tail_kernel(
-    x_hbm, first_hbm, peer_hbm, late_hbm, own_hbm, o_hbm, wd_hbm, wo_hbm, y_ref,
-    xv, g_first, g_peer, g_late, g_got, g_own, ov, oa, of, hb, wd, wo, out_part, y_send, y_pair, y_over, y_recv, y_last,
-    in_sem, g_sem, b_send, b_recv, o_send, o_recv, h_send, h_recv, p_send, p_recv, y_ssem, y_rsem, l_send, l_recv,
+    g_first, g_peer, g_late, own_hbm, ov, wd_hbm, wo_hbm, y_ref,
+    g_got, g_own, oa, of, hb, wd, wo, out_part, y_send, y_pair, y_over, y_recv, y_last,
+    in_sem, own_sem, b_send, b_recv, o_send, o_recv, h_send, h_recv, p_send, p_recv, y_ssem, y_rsem, l_send, l_recv,
 ):
     me_x = lax.axis_index('x')
     me_yz = lax.axis_index('yz')
     groups, _, span, ff = hb.shape
-    rows, chunk = xv.shape
+    rows, chunk = y_ref.shape
     half = rows // 2
     owned = ov.shape[1]
     early, _, wide = g_first.shape
@@ -359,23 +359,12 @@
     def rows_of(i):
         return pl.ds(span * i, span)
 
-    late_in = pltpu.make_async_copy(late_hbm, g_late, in_sem.at[4])
-    o_in = pltpu.make_async_copy(o_hbm, ov, in_sem.at[0])
-    first_in = pltpu.make_async_copy(first_hbm, g_first, in_sem.at[5])
-    own_in = [pltpu.make_async_copy(own_hbm.at[rows_of(i)], g_own.at[rows_of(i)], g_sem.at[0, i]) for i in range(groups)]
-    peer_in = [pltpu.make_async_copy(peer_hbm.at[rows_of(i)], g_peer.at[rows_of(i)], g_sem.at[1, i]) for i in range(groups_a)]
+    own_in = [pltpu.make_async_copy(own_hbm.at[rows_of(i)], g_own.at[rows_of(i)], own_sem.at[i]) for i in range(groups)]
     wo_in = pltpu.make_async_copy(wo_hbm, wo, in_sem.at[1])
     wd_in = pltpu.make_async_copy(wd_hbm, wd, in_sem.at[2])
-    x_in = pltpu.make_async_copy(x_hbm, xv, in_sem.at[3])
-    for copy in (late_in, o_in, first_in):
-        copy.start()
-    for i in range(groups):
-        own_in[i].start()
-        if i < groups_a:
-            peer_in[i].start()
-    for copy in (wo_in, wd_in, x_in):
-        copy.start()
-    start_barrier(me_x, me_yz)
+    for copy in (*own_in, wo_in, wd_in):
+        copy.start()
+    start_barrier(me_x, me_yz)()
     me = me_x * 4 + me_yz
 
     def remote(src, dst, send, recv, to_x, to_yz):
@@ -383,13 +372,11 @@
             src_ref=src, dst_ref=dst, send_sem=send, recv_sem=recv, device_id=(to_x, to_yz), device_id_type=MESH,
         )
 
-    late_in.wait()
     b_out = [
         remote(g_late.at[rows_of(i)], g_got.at[rows_of(i)], b_send.at[i], b_recv.at[i], other_x, me_yz) for i in range(groups - groups_a)
     ]
     for copy in b_out:
         copy.start()
-    o_in.wait()
     o_out = []
     for dx in range(2):
         for k in range(4):
@@ -399,7 +386,6 @@
     for copy in o_out:
         copy.start()
     oa[me] = ov[me_yz]
-    first_in.wait()
 
     h_out = []
 
@@ -407,7 +393,6 @@
         own_in[i].wait()
         at = rows_of(i)
         if i < groups_a:
-            peer_in[i].wait()
             got, got_at = g_peer, at
         else:
             b_out[i - groups_a].wait()
@@ -439,7 +424,6 @@
     for i in range(groups_a, groups):
         activate(i)
     wd_in.wait()
-    x_in.wait()
 
     pair, over, last = [], [], []
 
@@ -481,7 +465,7 @@
                 total = total + y_last[lax.rem(me_yz + k, 4)]
         for e in range(2):
             at = pl.ds(half * e + span * i, span)
-            y_ref[at, :] = (xv[at, :].astype(jnp.float32) + total[span * e:span * e + span]).astype(jnp.bfloat16)
+            y_ref[at, :] = total[span * e:span * e + span]
 
     for i in range(groups):
         product(i)
@@ -493,31 +477,27 @@
     finish(groups - 1)
 
 
-def tail(x_in, g_first, g_peer, g_late, g_own, o_blocks, w_down, w_out):
-    rows, chunk = x_in.shape
-    half = rows // 2
+def tail(g_first, g_peer, g_late, g_own, o_blocks, w_down, w_out):
+    half = g_own.shape[0]
+    rows = 2 * half
     span = 16
     groups = half // span
     ff, cols = w_down.shape
+    chunk = cols // 4
     owned = o_blocks.shape[1]
     o_width = w_out.shape[0]
-    any_spec = pl.BlockSpec(memory_space=pl.ANY)
+    any_spec, vmem_spec = pl.BlockSpec(memory_space=pl.ANY), pl.BlockSpec(memory_space=pltpu.VMEM)
     dma = pltpu.SemaphoreType.DMA
     f32, bf16 = jnp.float32, jnp.bfloat16
     late_groups = g_late.shape[0] // span
     return pl.pallas_call(
         tail_kernel,
-        out_shape=jax.ShapeDtypeStruct((rows, chunk), bf16),
-        in_specs=[any_spec] * 8,
+        out_shape=jax.ShapeDtypeStruct((rows, chunk), f32),
+        in_specs=[vmem_spec, vmem_spec, vmem_spec, any_spec, vmem_spec, any_spec, any_spec],
         out_specs=pl.BlockSpec(memory_space=pltpu.VMEM),
         scratch_shapes=[
-            pltpu.VMEM((rows, chunk), bf16),
-            pltpu.VMEM(g_first.shape, f32),
-            pltpu.VMEM(g_peer.shape, f32),
-            pltpu.VMEM(g_late.shape, f32),
             pltpu.VMEM(g_late.shape, f32),
             pltpu.VMEM((half, 2 * ff), f32),
-            pltpu.VMEM((4, owned, o_width), bf16),
             pltpu.VMEM((8, owned, o_width), bf16),
             pltpu.VMEM((rows, o_width), f32),
             pltpu.VMEM((groups, 2, span, ff), bf16),
@@ -529,13 +509,13 @@
             pltpu.VMEM((groups, 2 * span, chunk), f32),
             pltpu.VMEM((groups, 2 * span, chunk), f32),
             pltpu.VMEM((4, 2 * span, chunk), f32),
-            dma((6,)), dma((2, groups)), dma((late_groups,)), dma((late_groups,)), dma((8,)), dma((8,)), dma((groups,)), dma((groups,)),
+            dma((3,)), dma((groups,)), dma((late_groups,)), dma((late_groups,)), dma((8,)), dma((8,)), dma((groups,)), dma((groups,)),
             dma((groups, 2)), dma((groups, 2)), dma((groups,)), dma((groups,)), dma((4,)), dma((4,)),
         ],
-        compiler_params=pltpu.CompilerParams(collective_id=1, has_side_effects=True, vmem_limit_bytes=VMEM_MOST - 1536 * 1024),
+        compiler_params=pltpu.CompilerParams(collective_id=1, has_side_effects=True, vmem_limit_bytes=51 * 1024 * 1024),
         cost_estimate=pl.CostEstimate(flops=2 * rows * (ff + o_width) * cols, bytes_accessed=2 * (ff + o_width) * cols, transcendentals=half * ff),
         name='tail',
-    )(x_in, g_first, g_peer, g_late, g_own, o_blocks, w_down, w_out)
+    )(g_first, g_peer, g_late, g_own, o_blocks, w_down, w_out)
 
 
 def rotary(values, positions):
@@ -571,7 +551,8 @@
         cols = jnp.pad(cols, ((0, 0), (0, 0), (0, 128 - local_rows)))
         attn_out, k_new, v_new = attend(q_rot, cols, k_cache, v_cache, lengths)
         o_blocks = attn_out.reshape(local_rows, yz_size, q_width // yz_size).transpose(1, 0, 2)
-        y_out = tail(x_in, g_first, g_peer, g_late, g_own, o_blocks, w_down, w_out)
+        mixed_sum = tail(g_first, g_peer, g_late, g_own, o_blocks, w_down, w_out)
+        y_out = (x_in.astype(jnp.float32) + mixed_sum).astype(jnp.bfloat16)
         return y_out, k_new, v_new
 
     row_spec = P(None, all_axes)

time: 99.4 us -> 93.9 us (0.945)
  local copies, waits for them, and re-layouts: 6.84 us -> 2.3 us
  Pallas kernels: 87.8 us -> 85.4 us
    unnamed x5 -> x8, local copies, waits for them, and re-layouts: 3.31 us -> 0.66 us
    pallas_call x1, Pallas kernels: 32.3 us -> 30.6 us  [head(): pl.pallas_call(functools.partial(head_kernel, d_model, early), out_shape=...]
    reshape x1 -> x0, local copies, waits for them, and re-layouts: 1.25 us -> none  [head(): ln_scale.reshape(1, chunk)]
  transfers between devices with their start and end apart: 1 -> 1, of which waited for: 1 -> 1; matrix products, arithmetic and copies ran while one was open for 4% -> 3% of each run, Pallas kernels for 24% -> 25%
where the time goes in v5:
time: 93.9 us; the launch traced here: 93.7 us
  Pallas kernels  85.4 us (91%)
  waiting for transfers between devices  2.6 us (3%)
  local copies, waits for them, and re-layouts  2.3 us (2%)
  other arithmetic  2.14 us (2%)
    pallas_call x1, Pallas kernels, tail(): pl.pallas_call(tail_kernel, out_shape=jax.ShapeDtypeStruct((rows, chunk),...  31.2 us
    pallas_call x1, Pallas kernels, head(): pl.pallas_call(functools.partial(head_kernel, d_model, early), out_shape=...  30.6 us
    pallas_call x1, Pallas kernels, attend(): pl.pallas_call(functools.partial(attention_kernel, head_dim ** (-0.5)), o...  23.6 us
    ppermute x1, waiting for transfers between devices, local_step(): g_peer = lax.ppermute(g_send, 'x', [(0, 1), (1, 0)])  2.6 us
  transfers between devices with their start and end apart: 1, of which 1 were waited for; matrix products, arithmetic and copies ran while one was open for 3% of the time, Pallas kernels for 25%

profile of v5, /device:TPU:0, one launch (start us, length us, event | category | flops | bytes accessed | tf_op | source)
XLA Modules:
  0.0 93.7 jit_solution(16457463487786180852)
XLA Ops:
  0.6 30.6 %head.1 = (bf16[4,24,680]{2,1,0:T(8,128)(2,1)}, f32[2,96,512]{2,1,0:T(8,128)}, f32[80,4096]{1,0:T(8,128)}, f32[16,4096]{1,0:T(8,128)}, f32[96,5120]{1,0:T(8,128)}) custom-call(bf16[192,320]{1,0:T(8,128)(2,1)} %x_hbm.1, f32[320]{0:T(512)} %scale_hbm.1, bf16[1280,2,2560]{2,1,0:T(2,128)(2,1)} %wg_hbm.1, bf16[680,1280]{1,0:T(8,128)(2,1)} %bitcast.26), custom_call_target="tpu_custom_call" | custom-call | flops 5033164800 | bytes 13107200 | tf_op jit(solution)/shard_map/head/pallas_call | solution.py:301
  31.3 0.5 collective-permute-start
  31.8 0.7 convert_element_type.40
  32.5 1.0 %copy.22 = bf16[24,4,680]{2,1,0:T(4,128)(2,1)S(1)} copy(bf16[24,4,680]{2,0,1:T(8,128)(2,1)} %bitcast.23) | data formatting | bytes 261120 | tf_op jit(solution)/shard_map/transpose | solution.py:544
  33.4 0.1 reshape.134
  33.6 0.1 fusion.8
  33.7 0.1 fusion.5
  33.8 0.1 maximum_bitcast_fusion
  33.9 0.1 copy.23
  34.0 0.2 reshape.136
  34.3 0.1 multiply_cosine_fusion.1
  34.4 0.2 subtract_convert_fusion
  34.6 0.1 pad_maximum_fusion.q_ref
  34.7 0.0 copy-start.2
  34.7 0.6 copy-done.2
  35.4 0.0 copy-start
  35.4 0.0 copy-start.1
  35.4 23.6 %attend.1 = (bf16[24,32,80]{2,1,0:T(8,128)(2,1)S(1)}, bf16[24,80,4096]{2,1,0:T(8,128)(2,1)}, bf16[24,80,4096]{2,1,0:T(8,128)(2,1)}) custom-call(s32[24]{0:T(128)S(1)} %copy-done.2, bf16[24,32,80]{2,1,0:T(8,128)(2,1)S(1)} %pad_maximum_fusion.q_ref, f32[2,80,128]{2,1,0:T(8,128)S(1)} %pad_convert_fusion.cols_ref, bf16[24,80,4096]{2,1,0:T(8,128)(2,1)} %bitcast.20, ...), custom_call_target="tpu_custom_call" | custom-call | flops 1006632960 | bytes 62914560 | tf_op jit(solution)/shard_map/attend/pallas_call | solution.py:68
  59.0 0.0 copy-start.3
  59.0 0.2 reshape.135
  59.3 2.6 %collective-permute-done.g_peer = f32[80,4096]{1,0:T(8,128)S(1)} collective-permute-done((f32[80,4096]{1,0:T(8,128)}, f32[80,4096]{1,0:T(8,128)S(1)}, u32[]{:S(2)}, u32[]{:S(2)}) %collective-permute-start) | collective-permute-done | bytes 1310752 | tf_op jit(solution)/shard_map/ppermute | solution.py:543
  61.9 0.0 copy-done
  61.9 0.0 copy-done.1
  61.9 31.2 %tail.1 = f32[192,320]{1,0:T(8,128)S(1)} custom-call(f32[2,96,512]{2,1,0:T(8,128)S(1)} %copy-done, f32[80,4096]{1,0:T(8,128)S(1)} %collective-permute-done.g_peer, f32[16,4096]{1,0:T(8,128)S(1)} %copy-done.1, f32[96,5120]{1,0:T(8,128)} %get-tuple-element.14.own_hbm, bf16[4,24,640]{2,1,0:T(8,128)(2,1)S(1)} %bitcast.19, bf16[2560,1280]{1,0:T(8,128)(2,1)} %wd_hbm.1, ...), custom_call_target="tpu_custom_call" | custom-call | flops 1572864000 | bytes 8192000 | tf_op jit(solution)/shard_map/tail/pallas_call | solution.py:493
  93.0 0.0 copy-done.3
  93.0 0.7 add_convert_fusion.1
  (5 shorter events, 0.1 us)
Async XLA Ops:
  31.3 30.6 %collective-permute-start = (f32[80,4096]{1,0:T(8,128)}, f32[80,4096]{1,0:T(8,128)S(1)}, u32[]{:S(2)}, u32[]{:S(2)}) collective-permute-start(f32[80,4096]{1,0:T(8,128)} %get-tuple-element.12), channel_id=1, source_target_pairs={{0,4},{4,0},{1,5},{5,1},{2,6},{6,2},{3,7},{7,3}} | collective-permute-start | bytes 3932168 | tf_op jit(solution)/shard_map/ppermute | solution.py:543
  34.7 0.7 copy-start.2
  35.4 26.5 %copy-start = (f32[2,96,512]{2,1,0:T(8,128)S(1)}, f32[2,96,512]{2,1,0:T(8,128)}, u32[]{:S(2)}) copy-start(f32[2,96,512]{2,1,0:T(8,128)} %get-tuple-element.11.g_first) | copy-start | bytes 1179652
  35.4 26.5 %copy-start.1 = (f32[16,4096]{1,0:T(8,128)S(1)}, f32[16,4096]{1,0:T(8,128)}, u32[]{:S(2)}) copy-start(f32[16,4096]{1,0:T(8,128)} %get-tuple-element.13.g_late) | copy-start | bytes 786436
  59.0 34.0 %copy-start.3 = (bf16[192,320]{1,0:T(8,128)(2,1)S(1)}, bf16[192,320]{1,0:T(8,128)(2,1)}, u32[]{:S(2)}) copy-start(bf16[192,320]{1,0:T(8,128)(2,1)} %x_hbm.1) | copy-start | bytes 368644

commit v6 on v5

--- a/solution.py
+++ b/solution.py
@@ -135,7 +135,7 @@
     wg_in = [
         pltpu.make_async_copy(wg_hbm.at[pl.ds(depth * i, depth)], wg.at[pl.ds(depth * i, depth)], wg_sem.at[i]) for i in range(pieces)
     ]
-    for copy in (*x_in, scale_in, wa_in, *wg_in):
+    for copy in (*x_in, scale_in, wa_in):
         copy.start()
     others_ready = start_barrier(me_x, me_yz)
 
@@ -178,6 +178,8 @@
     for p in range(2):
         x_copy(1, p).start()
         x_copy(0, p).start()
+    for copy in wg_in:
+        copy.start()
     wide, thin = spread(128, 256, 0), spread(64, 128, 0)
     wide_u, thin_u = spread(128, 256, 1), spread(64, 128, 1)
     i = lax.broadcasted_iota(jnp.int32, (256, 128), 0)
@@ -338,8 +340,8 @@
 
 def tail_kernel(
     g_first, g_peer, g_late, own_hbm, ov, wd_hbm, wo_hbm, y_ref,
-    g_got, g_own, oa, of, hb, wd, wo, out_part, y_send, y_pair, y_over, y_recv, y_last,
-    in_sem, own_sem, b_send, b_recv, o_send, o_recv, h_send, h_recv, p_send, p_recv, y_ssem, y_rsem, l_send, l_recv,
+    g_got, g_own, oa, of, hb, wd, wo, out_part, y_send, y_pair, y_over, y_recv,
+    in_sem, own_sem, b_send, b_recv, o_send, o_recv, h_send, h_recv, p_send, p_recv, y_ssem, y_rsem,
 ):
     me_x = lax.axis_index('x')
     me_yz = lax.axis_index('yz')
@@ -425,7 +427,7 @@
         activate(i)
     wd_in.wait()
 
-    pair, over, last = [], [], []
+    pair, over = [], []
 
     def product(i):
         h_out[i].wait()
@@ -434,17 +436,11 @@
         for j in range(4):
             moved = part if j == 0 else pltpu.roll(part, (4 - j) * chunk, 1)
             y_send[i, j] = moved[:, :chunk]
-        if i < groups - 1:
-            pair.append([
-                remote(y_send.at[i, 2 * e + 1 - core], y_pair.at[i, e], p_send.at[i, e], p_recv.at[i, e], me_x, partner) for e in range(2)
-            ])
-            for copy in pair[i]:
-                copy.start()
-        else:
-            for k in (2, 3, 1):
-                there = lax.rem(me_yz + k, 4)
-                last.append(remote(y_send.at[i, there], y_last.at[me_yz], l_send.at[k], l_recv.at[k], me_x, there))
-                last[-1].start()
+        pair.append([
+            remote(y_send.at[i, 2 * e + 1 - core], y_pair.at[i, e], p_send.at[i, e], p_recv.at[i, e], me_x, partner) for e in range(2)
+        ])
+        for copy in pair[i]:
+            copy.start()
 
     def cross(i):
         for copy in pair[i]:
@@ -454,15 +450,8 @@
         over[i].start()
 
     def finish(i):
-        if i < groups - 1:
-            over[i].wait()
-            total = y_send[i, me_yz] + y_pair[i, col] + y_recv[i]
-        else:
-            for copy in last:
-                copy.wait()
-            total = y_send[i, me_yz]
-            for k in (1, 2, 3):
-                total = total + y_last[lax.rem(me_yz + k, 4)]
+        over[i].wait()
+        total = y_send[i, me_yz] + y_pair[i, col] + y_recv[i]
         for e in range(2):
             at = pl.ds(half * e + span * i, span)
             y_ref[at, :] = total[span * e:span * e + span]
@@ -471,10 +460,11 @@
         product(i)
         if i >= 1:
             cross(i - 1)
-        if i >= 2:
-            finish(i - 2)
-    finish(groups - 2)
-    finish(groups - 1)
+    for i in range(groups - 3):
+        finish(i)
+    cross(groups - 1)
+    for i in range(groups - 3, groups):
+        finish(i)
 
 
 def tail(g_first, g_peer, g_late, g_own, o_blocks, w_down, w_out):
@@ -508,9 +498,8 @@
             pltpu.VMEM((groups, 2, 2 * span, chunk), f32),
             pltpu.VMEM((groups, 2 * span, chunk), f32),
             pltpu.VMEM((groups, 2 * span, chunk), f32),
-            pltpu.VMEM((4, 2 * span, chunk), f32),
             dma((3,)), dma((groups,)), dma((late_groups,)), dma((late_groups,)), dma((8,)), dma((8,)), dma((groups,)), dma((groups,)),
-            dma((groups, 2)), dma((groups, 2)), dma((groups,)), dma((groups,)), dma((4,)), dma((4,)),
+            dma((groups, 2)), dma((groups, 2)), dma((groups,)), dma((groups,)),
         ],
         compiler_params=pltpu.CompilerParams(collective_id=1, has_side_effects=True, vmem_limit_bytes=51 * 1024 * 1024),
         cost_estimate=pl.CostEstimate(flops=2 * rows * (ff + o_width) * cols, bytes_accessed=2 * (ff + o_width) * cols, transcendentals=half * ff),

time: 93.9 us -> 89.1 us (0.949)
  Pallas kernels: 85.4 us -> 80.7 us
    pallas_call x1, Pallas kernels: 30.6 us -> 28.2 us  [head(): pl.pallas_call(functools.partial(head_kernel, d_model, early), out_shape=...]
    pallas_call x1, Pallas kernels: 31.2 us -> 28.8 us  [tail(): pl.pallas_call(tail_kernel, out_shape=jax.ShapeDtypeStruct((rows, chunk),...]
  transfers between devices with their start and end apart: 1 -> 1, of which waited for: 1 -> 1; matrix products, arithmetic and copies ran while one was open for 3% -> 3% of each run, Pallas kernels for 25% -> 27%
where the time goes in v6:
time: 89.1 us; the launch traced here: 88.9 us
  Pallas kernels  80.7 us (91%)
  local copies, waits for them, and re-layouts  2.3 us (3%)
  other arithmetic  2.14 us (2%)
  waiting for transfers between devices  2.01 us (2%)
  starting transfers between devices  1.08 us (1%)
    pallas_call x1, Pallas kernels, tail(): pl.pallas_call(tail_kernel, out_shape=jax.ShapeDtypeStruct((rows, chunk),...  28.8 us
    pallas_call x1, Pallas kernels, head(): pl.pallas_call(functools.partial(head_kernel, d_model, early), out_shape=...  28.2 us
    pallas_call x1, Pallas kernels, attend(): pl.pallas_call(functools.partial(attention_kernel, head_dim ** (-0.5)), o...  23.7 us
    ppermute x1, waiting for transfers between devices, local_step(): g_peer = lax.ppermute(g_send, 'x', [(0, 1), (1, 0)])  2.01 us
  transfers between devices with their start and end apart: 1, of which 1 were waited for; matrix products, arithmetic and copies ran while one was open for 3% of the time, Pallas kernels for 27%

profile of v6, /device:TPU:0, one launch (start us, length us, event | category | flops | bytes accessed | tf_op | source)
XLA Modules:
  0.0 88.9 jit_solution(15110892168993427828)
XLA Ops:
  0.6 28.2 %head.1 = (bf16[4,24,680]{2,1,0:T(8,128)(2,1)}, f32[2,96,512]{2,1,0:T(8,128)}, f32[80,4096]{1,0:T(8,128)}, f32[16,4096]{1,0:T(8,128)}, f32[96,5120]{1,0:T(8,128)}) custom-call(bf16[192,320]{1,0:T(8,128)(2,1)} %x_hbm.1, f32[320]{0:T(512)} %scale_hbm.1, bf16[1280,2,2560]{2,1,0:T(2,128)(2,1)} %wg_hbm.1, bf16[680,1280]{1,0:T(8,128)(2,1)} %bitcast.26), custom_call_target="tpu_custom_call" | custom-call | flops 5033164800 | bytes 13107200 | tf_op jit(solution)/shard_map/head/pallas_call | solution.py:303
  28.8 1.1 %collective-permute-start = (f32[80,4096]{1,0:T(8,128)}, f32[80,4096]{1,0:T(8,128)S(1)}, u32[]{:S(2)}, u32[]{:S(2)}) collective-permute-start(f32[80,4096]{1,0:T(8,128)} %get-tuple-element.12), channel_id=1, source_target_pairs={{0,4},{4,0},{1,5},{5,1},{2,6},{6,2},{3,7},{7,3}} | collective-permute-start | bytes 3932168 | tf_op jit(solution)/shard_map/ppermute | solution.py:532
  29.9 0.7 convert_element_type.40
  30.6 1.0 %copy.22 = bf16[24,4,680]{2,1,0:T(4,128)(2,1)S(1)} copy(bf16[24,4,680]{2,0,1:T(8,128)(2,1)} %bitcast.23) | data formatting | bytes 261120 | tf_op jit(solution)/shard_map/transpose | solution.py:533
  31.5 0.1 reshape.134
  31.7 0.1 fusion.8
  31.8 0.1 fusion.5
  31.9 0.1 maximum_bitcast_fusion
  32.0 0.1 copy.23
  32.1 0.2 reshape.136
  32.4 0.1 multiply_cosine_fusion.1
  32.5 0.2 subtract_convert_fusion
  32.7 0.1 pad_maximum_fusion.q_ref
  32.8 0.0 copy-start.2
  32.8 0.6 copy-done.2
  33.5 0.0 copy-start
  33.5 0.0 copy-start.1
  33.5 23.7 %attend.1 = (bf16[24,32,80]{2,1,0:T(8,128)(2,1)S(1)}, bf16[24,80,4096]{2,1,0:T(8,128)(2,1)}, bf16[24,80,4096]{2,1,0:T(8,128)(2,1)}) custom-call(s32[24]{0:T(128)S(1)} %copy-done.2, bf16[24,32,80]{2,1,0:T(8,128)(2,1)S(1)} %pad_maximum_fusion.q_ref, f32[2,80,128]{2,1,0:T(8,128)S(1)} %pad_convert_fusion.cols_ref, bf16[24,80,4096]{2,1,0:T(8,128)(2,1)} %bitcast.20, ...), custom_call_target="tpu_custom_call" | custom-call | flops 1006632960 | bytes 62914560 | tf_op jit(solution)/shard_map/attend/pallas_call | solution.py:68
  57.1 0.0 copy-start.3
  57.2 0.2 reshape.135
  57.4 2.0 %collective-permute-done.g_peer = f32[80,4096]{1,0:T(8,128)S(1)} collective-permute-done((f32[80,4096]{1,0:T(8,128)}, f32[80,4096]{1,0:T(8,128)S(1)}, u32[]{:S(2)}, u32[]{:S(2)}) %collective-permute-start) | collective-permute-done | bytes 1310752 | tf_op jit(solution)/shard_map/ppermute | solution.py:532
  59.4 0.0 copy-done
  59.4 0.0 copy-done.1
  59.4 28.8 %tail.1 = f32[192,320]{1,0:T(8,128)S(1)} custom-call(f32[2,96,512]{2,1,0:T(8,128)S(1)} %copy-done, f32[80,4096]{1,0:T(8,128)S(1)} %collective-permute-done.g_peer, f32[16,4096]{1,0:T(8,128)S(1)} %copy-done.1, f32[96,5120]{1,0:T(8,128)} %get-tuple-element.14.own_hbm, bf16[4,24,640]{2,1,0:T(8,128)(2,1)S(1)} %bitcast.19, bf16[2560,1280]{1,0:T(8,128)(2,1)} %wd_hbm.1, ...), custom_call_target="tpu_custom_call" | custom-call | flops 1572864000 | bytes 8192000 | tf_op jit(solution)/shard_map/tail/pallas_call | solution.py:483
  88.2 0.0 copy-done.3
  88.2 0.7 add_convert_fusion.1
  (5 shorter events, 0.1 us)
Async XLA Ops:
  28.8 30.6 %collective-permute-start = (f32[80,4096]{1,0:T(8,128)}, f32[80,4096]{1,0:T(8,128)S(1)}, u32[]{:S(2)}, u32[]{:S(2)}) collective-permute-start(f32[80,4096]{1,0:T(8,128)} %get-tuple-element.12), channel_id=1, source_target_pairs={{0,4},{4,0},{1,5},{5,1},{2,6},{6,2},{3,7},{7,3}} | collective-permute-start | bytes 3932168 | tf_op jit(solution)/shard_map/ppermute | solution.py:532
  32.8 0.7 copy-start.2
  33.5 25.9 %copy-start = (f32[2,96,512]{2,1,0:T(8,128)S(1)}, f32[2,96,512]{2,1,0:T(8,128)}, u32[]{:S(2)}) copy-start(f32[2,96,512]{2,1,0:T(8,128)} %get-tuple-element.11.g_first) | copy-start | bytes 1179652
  33.5 25.9 %copy-start.1 = (f32[16,4096]{1,0:T(8,128)S(1)}, f32[16,4096]{1,0:T(8,128)}, u32[]{:S(2)}) copy-start(f32[16,4096]{1,0:T(8,128)} %get-tuple-element.13.g_late) | copy-start | bytes 786436
  57.1 31.1 %copy-start.3 = (bf16[192,320]{1,0:T(8,128)(2,1)S(1)}, bf16[192,320]{1,0:T(8,128)(2,1)}, u32[]{:S(2)}) copy-start(bf16[192,320]{1,0:T(8,128)(2,1)} %x_hbm.1) | copy-start | bytes 368644

commit v7 on v6

--- a/solution.py
+++ b/solution.py
@@ -12,7 +12,6 @@
 MESH = pl.DeviceIdType.MESH
 VMEM_MOST = 64 * 1024 * 1024 - 64 * 1024
 EARLY = 2
-ROWS_A = 80
 
 
 def attention_kernel(scale, len_ref, q_ref, cols_ref, k_hbm, v_hbm, o_ref, ko_hbm, vo_hbm, k_buf, v_buf, in_sem, out_sem):
@@ -110,8 +109,8 @@
 
 
 def head_kernel(
-    d_model, early, x_hbm, scale_hbm, wg_hbm, wa_hbm, z_hbm, first_hbm, send_a_hbm, send_b_hbm, own_hbm,
-    xg, scale_row, sg, stats, h_buf, hx, hc, wg, wa, z_send, z_own, z_recv, zb, zg, g_first, g_rest, g_own,
+    d_model, early, x_hbm, scale_hbm, wg_hbm, wa_hbm, z_hbm, first_hbm, send_hbm, own_hbm,
+    xg, scale_row, sg, stats, h_buf, hx, hc, wg, wa, z_send, z_own, z_recv, r_send, r_own, r_recv, zb, zg, g_first, g_rest, g_own,
     in_sem, wg_sem, x_send, x_recv, s_send, s_recv, t_send, t_recv, z_sems, a_send, a_recv, f_send, f_recv, out_sem,
 ):
     me_x = lax.axis_index('x')
@@ -122,6 +121,9 @@
     depth = wg.shape[0] // pieces
     ff = wg.shape[2]
     wide_cols = 256
+    full = z_send.shape[2]
+    third = half // 3
+    tail_cols = wa.shape[0] - full
     other_x = lax.rem(me_x + 1, 2)
     across = lax.rem(me_yz + 2, 4)
     core = lax.rem(me_yz, 2)
@@ -224,15 +226,19 @@
         src = pl.ds(2 * part * half, half)
         for t in range(4 * chunk // 128):
             hc[:, 128 * t:128 * t + 128] = jnp.dot(hx[src, 256 * t:256 * t + 256], gather, preferred_element_type=jnp.float32).astype(jnp.bfloat16)
-        z = lax.dot_general(hc[...], wa[...], (((1,), (1,)), ((), ())), preferred_element_type=jnp.float32)
-        return z.reshape(z_send.shape)
+        contract = (((1,), (1,)), ((), ()))
+        z = lax.dot_general(hc[...], wa[:full, :], contract, preferred_element_type=jnp.float32)
+        r = lax.dot_general(hc[...], wa[full:, :], contract, preferred_element_type=jnp.float32)
+        r = jnp.concatenate([r[third * i:third * i + third] for i in range(3)], axis=1)
+        return z.reshape(z_send.shape), r
 
     normalize(0)
     spread_half(0, 0)
     wa_in.wait()
-    z_send[...] = project(0)
-    z_copy = remote(z_send, z_recv, z_sems.at[0], z_sems.at[1], other_x, me_yz)
-    z_copy.start()
+    z_send[...], r_send[...] = project(0)
+    z_out = [remote(z_send, z_recv, z_sems.at[0], z_sems.at[1], other_x, me_yz), remote(r_send, r_recv, z_sems.at[2], z_sems.at[3], other_x, me_yz)]
+    for copy in z_out:
+        copy.start()
     spread_half(0, 1)
     normalize(1)
     spread_half(1, 0)
@@ -265,24 +271,23 @@
         return carry
 
     lax.fori_loop(early, ff // wide_cols, rest, 0)
-    rows_a = send_a_hbm.shape[0]
-    save = [
-        pltpu.make_async_copy(g_rest.at[pl.ds(0, rows_a)], send_a_hbm, out_sem.at[0]),
-        pltpu.make_async_copy(g_rest.at[pl.ds(rows_a, half - rows_a)], send_b_hbm, out_sem.at[1]),
-        pltpu.make_async_copy(g_own, own_hbm, out_sem.at[2]),
-    ]
+    save = [pltpu.make_async_copy(g_rest, send_hbm, out_sem.at[0]), pltpu.make_async_copy(g_own, own_hbm, out_sem.at[1])]
     for copy in save:
         copy.start()
-    z_own[...] = project(1)
-    z_copy.wait()
-    zb[...] = (z_own[...] + z_recv[...]).astype(jnp.bfloat16)
+    z_own[...], r_own[...] = project(1)
+    for copy in z_out:
+        copy.wait()
+    zb[:, :, :full] = (z_own[...] + z_recv[...]).astype(jnp.bfloat16)
+    r = r_own[...] + r_recv[...]
+    r = jnp.concatenate([r[:, tail_cols * i:tail_cols * i + tail_cols] for i in range(3)], axis=0)
+    zb[:, :, full:] = r.reshape(zb.shape[0], zb.shape[1], tail_cols).astype(jnp.bfloat16)
     a_out = [remote(zb.at[lax.rem(me_yz + k, 4)], zg.at[me_yz], a_send.at[k], a_recv.at[k], me_x, lax.rem(me_yz + k, 4)) for k in (1, 2, 3)]
     for copy in a_out:
         copy.start()
     zg[me_yz] = zb[me_yz]
     for copy in a_out:
         copy.wait()
-    save.append(pltpu.make_async_copy(zg, z_hbm, out_sem.at[3]))
+    save.append(pltpu.make_async_copy(zg, z_hbm, out_sem.at[2]))
     save[-1].start()
     for copy in first:
         copy.wait()
@@ -290,10 +295,11 @@
         copy.wait()
 
 
-def head(x_in, ln_scale, w_gate_up, w_attn, d_model, early, rows_a):
+def head(x_in, ln_scale, w_gate_up, w_attn, d_model, early):
     rows, chunk = x_in.shape
     depth, _, ff = w_gate_up.shape
     z_cols = w_attn.shape[1]
+    full = z_cols // 128 * 128
     owned = rows // 8
     half = rows // 2
     width = 2 * (ff - 256 * early)
@@ -305,12 +311,11 @@
         out_shape=(
             jax.ShapeDtypeStruct((4, owned, z_cols), bf16),
             jax.ShapeDtypeStruct((early, half, 512), f32),
-            jax.ShapeDtypeStruct((rows_a, width), f32),
-            jax.ShapeDtypeStruct((half - rows_a, width), f32),
+            jax.ShapeDtypeStruct((half, width), f32),
             jax.ShapeDtypeStruct((half, 2 * ff), f32),
         ),
         in_specs=[any_spec] * 4,
-        out_specs=[any_spec] * 5,
+        out_specs=[any_spec] * 4,
         scratch_shapes=[
             pltpu.VMEM((4, 2, half, chunk), bf16),
             pltpu.VMEM((chunk,), f32),
@@ -321,16 +326,15 @@
             pltpu.VMEM((half, depth), bf16),
             pltpu.VMEM((depth, 2, ff), bf16),
             pltpu.VMEM((z_cols, depth), bf16),
-            pltpu.VMEM((4, owned, z_cols), f32),
-            pltpu.VMEM((4, owned, z_cols), f32),
-            pltpu.VMEM((4, owned, z_cols), f32),
+            *[pltpu.VMEM((4, owned, full), f32)] * 3,
+            *[pltpu.VMEM((half // 3, 3 * (z_cols - full)), f32)] * 3,
             pltpu.VMEM((4, owned, z_cols), bf16),
             pltpu.VMEM((4, owned, z_cols), bf16),
             pltpu.VMEM((early, half, 512), f32),
             pltpu.VMEM((half, width), f32),
             pltpu.VMEM((half, 2 * ff), f32),
-            dma((4,)), dma((8,)), dma((3, 2)), dma((3, 2)), dma((4,)), dma((4,)), dma((8,)), dma((8,)), dma((2,)), dma((4,)), dma((4,)),
-            dma((early,)), dma((early,)), dma((4,)),
+            dma((4,)), dma((8,)), dma((3, 2)), dma((3, 2)), dma((4,)), dma((4,)), dma((8,)), dma((8,)), dma((4,)), dma((4,)), dma((4,)),
+            dma((early,)), dma((early,)), dma((3,)),
         ],
         compiler_params=pltpu.CompilerParams(collective_id=0, has_side_effects=True, vmem_limit_bytes=VMEM_MOST),
         cost_estimate=pl.CostEstimate(flops=4 * rows * depth * 2 * ff, bytes_accessed=4 * depth * ff, transcendentals=0),
@@ -339,9 +343,9 @@
 
 
 def tail_kernel(
-    g_first, g_peer, g_late, own_hbm, ov, wd_hbm, wo_hbm, y_ref,
-    g_got, g_own, oa, of, hb, wd, wo, out_part, y_send, y_pair, y_over, y_recv,
-    in_sem, own_sem, b_send, b_recv, o_send, o_recv, h_send, h_recv, p_send, p_recv, y_ssem, y_rsem,
+    g_first, g_peer, own_hbm, ov, wd_hbm, wo_hbm, y_ref,
+    g_own, oa, of, hb, wd, wo, out_part, y_send, y_pair, y_over, y_recv,
+    in_sem, own_sem, o_send, o_recv, h_send, h_recv, p_send, p_recv, y_ssem, y_rsem,
 ):
     me_x = lax.axis_index('x')
     me_yz = lax.axis_index('yz')
@@ -351,7 +355,6 @@
     owned = ov.shape[1]
     early, _, wide = g_first.shape
     wide = wide // 2
-    groups_a = g_peer.shape[0] // span
     core = lax.rem(me_yz, 2)
     col = me_yz // 2
     partner = me_yz + 1 - 2 * core
@@ -374,11 +377,6 @@
             src_ref=src, dst_ref=dst, send_sem=send, recv_sem=recv, device_id=(to_x, to_yz), device_id_type=MESH,
         )
 
-    b_out = [
-        remote(g_late.at[rows_of(i)], g_got.at[rows_of(i)], b_send.at[i], b_recv.at[i], other_x, me_yz) for i in range(groups - groups_a)
-    ]
-    for copy in b_out:
-        copy.start()
     o_out = []
     for dx in range(2):
         for k in range(4):
@@ -394,12 +392,6 @@
     def activate(i):
         own_in[i].wait()
         at = rows_of(i)
-        if i < groups_a:
-            got, got_at = g_peer, at
-        else:
-            b_out[i - groups_a].wait()
-            got, got_at = g_got, rows_of(i - groups_a)
-
         def act(gate, up):
             gate = gate.astype(jnp.bfloat16).astype(jnp.float32)
             up = up.astype(jnp.bfloat16).astype(jnp.float32)
@@ -410,12 +402,12 @@
             up_cols = slice(ff + wide * c, ff + wide * c + wide)
             hb[i, me_x, :, cols] = act(g_own[at, cols] + g_first[c, at, :wide], g_own[at, up_cols] + g_first[c, at, wide:])
         done = early * wide
-        hb[i, me_x, :, done:] = act(g_own[at, done:ff] + got[got_at, :ff - done], g_own[at, ff + done:] + got[got_at, ff - done:])
+        hb[i, me_x, :, done:] = act(g_own[at, done:ff] + g_peer[at, :ff - done], g_own[at, ff + done:] + g_peer[at, ff - done:])
         copy = remote(hb.at[i, me_x], hb.at[i, me_x], h_send.at[i], h_recv.at[i], other_x, me_yz)
         copy.start()
         h_out.append(copy)
 
-    for i in range(groups_a):
+    for i in range(groups):
         activate(i)
     for copy in o_out:
         copy.wait()
@@ -423,8 +415,6 @@
         of[owned * e:owned * e + owned] = oa[e].astype(jnp.float32)
     wo_in.wait()
     out_part[...] = jnp.dot(of[...].astype(jnp.bfloat16), wo[...], preferred_element_type=jnp.float32)
-    for i in range(groups_a, groups):
-        activate(i)
     wd_in.wait()
 
     pair, over = [], []
@@ -467,7 +457,7 @@
         finish(i)
 
 
-def tail(g_first, g_peer, g_late, g_own, o_blocks, w_down, w_out):
+def tail(g_first, g_peer, g_own, o_blocks, w_down, w_out):
     half = g_own.shape[0]
     rows = 2 * half
     span = 16
@@ -479,14 +469,12 @@
     any_spec, vmem_spec = pl.BlockSpec(memory_space=pl.ANY), pl.BlockSpec(memory_space=pltpu.VMEM)
     dma = pltpu.SemaphoreType.DMA
     f32, bf16 = jnp.float32, jnp.bfloat16
-    late_groups = g_late.shape[0] // span
     return pl.pallas_call(
         tail_kernel,
         out_shape=jax.ShapeDtypeStruct((rows, chunk), f32),
-        in_specs=[vmem_spec, vmem_spec, vmem_spec, any_spec, vmem_spec, any_spec, any_spec],
+        in_specs=[vmem_spec, vmem_spec, any_spec, vmem_spec, any_spec, any_spec],
         out_specs=pl.BlockSpec(memory_space=pltpu.VMEM),
         scratch_shapes=[
-            pltpu.VMEM(g_late.shape, f32),
             pltpu.VMEM((half, 2 * ff), f32),
             pltpu.VMEM((8, owned, o_width), bf16),
             pltpu.VMEM((rows, o_width), f32),
@@ -498,13 +486,13 @@
             pltpu.VMEM((groups, 2, 2 * span, chunk), f32),
             pltpu.VMEM((groups, 2 * span, chunk), f32),
             pltpu.VMEM((groups, 2 * span, chunk), f32),
-            dma((3,)), dma((groups,)), dma((late_groups,)), dma((late_groups,)), dma((8,)), dma((8,)), dma((groups,)), dma((groups,)),
+            dma((3,)), dma((groups,)), dma((8,)), dma((8,)), dma((groups,)), dma((groups,)),
             dma((groups, 2)), dma((groups, 2)), dma((groups,)), dma((groups,)),
         ],
         compiler_params=pltpu.CompilerParams(collective_id=1, has_side_effects=True, vmem_limit_bytes=51 * 1024 * 1024),
         cost_estimate=pl.CostEstimate(flops=2 * rows * (ff + o_width) * cols, bytes_accessed=2 * (ff + o_width) * cols, transcendentals=half * ff),
         name='tail',
-    )(g_first, g_peer, g_late, g_own, o_blocks, w_down, w_out)
+    )(g_first, g_peer, g_own, o_blocks, w_down, w_out)
 
 
 def rotary(values, positions):
@@ -528,7 +516,7 @@
         q_width = w_out.shape[0] * yz_size
         num_heads = q_width // head_dim
         d_model = x_in.shape[1] * x_size * yz_size
-        z_blocks, g_first, g_send, g_late, g_own = head(x_in, ln_scale, w_gate_up, w_attn, d_model, EARLY, ROWS_A)
+        z_blocks, g_first, g_send, g_own = head(x_in, ln_scale, w_gate_up, w_attn, d_model, EARLY)
         g_peer = lax.ppermute(g_send, 'x', [(0, 1), (1, 0)])
         proj_local = z_blocks.transpose(1, 0, 2).reshape(local_rows, -1)
         q_raw = proj_local[:, :q_width].reshape(local_rows, num_heads, head_dim)
@@ -540,7 +528,7 @@
         cols = jnp.pad(cols, ((0, 0), (0, 0), (0, 128 - local_rows)))
         attn_out, k_new, v_new = attend(q_rot, cols, k_cache, v_cache, lengths)
         o_blocks = attn_out.reshape(local_rows, yz_size, q_width // yz_size).transpose(1, 0, 2)
-        mixed_sum = tail(g_first, g_peer, g_late, g_own, o_blocks, w_down, w_out)
+        mixed_sum = tail(g_first, g_peer, g_own, o_blocks, w_down, w_out)
         y_out = (x_in.astype(jnp.float32) + mixed_sum).astype(jnp.bfloat16)
         return y_out, k_new, v_new
 

time: 89.1 us -> 88.5 us (level)
  Pallas kernels: 80.7 us -> 74.3 us
  waiting for transfers between devices: 2.01 us -> 7.8 us
    ppermute x1, waiting for transfers between devices: 2.01 us -> 7.8 us  [local_step(): g_peer = lax.ppermute(g_send, 'x', [(0, 1), (1, 0)])]
    pallas_call x1, Pallas kernels: 28.8 us -> 23.2 us  [tail(): pl.pallas_call(tail_kernel, out_shape=jax.ShapeDtypeStruct((rows, chunk),...]
where the time goes in v7:
time: 88.5 us; the launch traced here: 88.3 us
  Pallas kernels  74.3 us (84%)
  waiting for transfers between devices  7.8 us (9%)
  local copies, waits for them, and re-layouts  2.3 us (3%)
  other arithmetic  2.14 us (2%)
  starting transfers between devices  1.08 us (1%)
    pallas_call x1, Pallas kernels, head(): pl.pallas_call(functools.partial(head_kernel, d_model, early), out_shape=...  27.4 us
    pallas_call x1, Pallas kernels, attend(): pl.pallas_call(functools.partial(attention_kernel, head_dim ** (-0.5)), o...  23.7 us
    pallas_call x1, Pallas kernels, tail(): pl.pallas_call(tail_kernel, out_shape=jax.ShapeDtypeStruct((rows, chunk),...  23.2 us
    ppermute x1, waiting for transfers between devices, local_step(): g_peer = lax.ppermute(g_send, 'x', [(0, 1), (1, 0)])  7.8 us
  transfers between devices with their start and end apart: 1, of which 1 were waited for; matrix products, arithmetic and copies ran while one was open for 3% of the time, Pallas kernels for 27%

profile of v7, /device:TPU:0, one launch (start us, length us, event | category | flops | bytes accessed | tf_op | source)
XLA Modules:
  0.0 88.3 jit_solution(11331612626135231367)
XLA Ops:
  0.6 27.4 %head.1 = (bf16[4,24,680]{2,1,0:T(8,128)(2,1)}, f32[2,96,512]{2,1,0:T(8,128)}, f32[96,4096]{1,0:T(8,128)}, f32[96,5120]{1,0:T(8,128)}) custom-call(bf16[192,320]{1,0:T(8,128)(2,1)} %x_hbm.1, f32[320]{0:T(512)} %scale_hbm.1, bf16[1280,2,2560]{2,1,0:T(2,128)(2,1)} %wg_hbm.1, bf16[680,1280]{1,0:T(8,128)(2,1)} %bitcast.26), custom_call_target="tpu_custom_call" | custom-call | flops 5033164800 | bytes 13107200 | tf_op jit(solution)/shard_map/head/pallas_call | solution.py:309
  28.1 1.1 %collective-permute-start = (f32[96,4096]{1,0:T(8,128)}, f32[96,4096]{1,0:T(8,128)S(1)}, u32[]{:S(2)}, u32[]{:S(2)}) collective-permute-start(f32[96,4096]{1,0:T(8,128)} %get-tuple-element.11), channel_id=1, source_target_pairs={{0,4},{4,0},{1,5},{5,1},{2,6},{6,2},{3,7},{7,3}} | collective-permute-start | bytes 4718600 | tf_op jit(solution)/shard_map/ppermute | solution.py:520
  29.2 0.7 convert_element_type.40
  29.8 1.0 %copy.22 = bf16[24,4,680]{2,1,0:T(4,128)(2,1)S(1)} copy(bf16[24,4,680]{2,0,1:T(8,128)(2,1)} %bitcast.23) | data formatting | bytes 261120 | tf_op jit(solution)/shard_map/transpose | solution.py:521
  30.8 0.1 reshape.134
  30.9 0.1 fusion.8
  31.0 0.1 fusion.5
  31.2 0.1 maximum_bitcast_fusion
  31.2 0.1 copy.23
  31.4 0.2 reshape.136
  31.6 0.1 multiply_cosine_fusion.1
  31.7 0.2 subtract_convert_fusion
  31.9 0.1 pad_maximum_fusion.q_ref
  32.1 0.0 copy-start.1
  32.1 0.6 copy-done.1
  32.7 0.0 copy-start
  32.7 23.7 %attend.1 = (bf16[24,32,80]{2,1,0:T(8,128)(2,1)S(1)}, bf16[24,80,4096]{2,1,0:T(8,128)(2,1)}, bf16[24,80,4096]{2,1,0:T(8,128)(2,1)}) custom-call(s32[24]{0:T(128)S(1)} %copy-done.1, bf16[24,32,80]{2,1,0:T(8,128)(2,1)S(1)} %pad_maximum_fusion.q_ref, f32[2,80,128]{2,1,0:T(8,128)S(1)} %pad_convert_fusion.cols_ref, bf16[24,80,4096]{2,1,0:T(8,128)(2,1)} %bitcast.20, ...), custom_call_target="tpu_custom_call" | custom-call | flops 1006632960 | bytes 62914560 | tf_op jit(solution)/shard_map/attend/pallas_call | solution.py:67
  56.4 0.0 copy-start.2
  56.4 0.2 reshape.135
  56.6 7.8 %collective-permute-done.g_peer = f32[96,4096]{1,0:T(8,128)S(1)} collective-permute-done((f32[96,4096]{1,0:T(8,128)}, f32[96,4096]{1,0:T(8,128)S(1)}, u32[]{:S(2)}, u32[]{:S(2)}) %collective-permute-start) | collective-permute-done | bytes 1572896 | tf_op jit(solution)/shard_map/ppermute | solution.py:520
  64.4 0.0 copy-done
  64.4 23.2 %tail.1 = f32[192,320]{1,0:T(8,128)S(1)} custom-call(f32[2,96,512]{2,1,0:T(8,128)S(1)} %copy-done, f32[96,4096]{1,0:T(8,128)S(1)} %collective-permute-done.g_peer, f32[96,5120]{1,0:T(8,128)} %get-tuple-element.12.own_hbm, bf16[4,24,640]{2,1,0:T(8,128)(2,1)S(1)} %bitcast.19, bf16[2560,1280]{1,0:T(8,128)(2,1)} %wd_hbm.1, bf16[640,1280]{1,0:T(8,128)(2,1)} %wo_hbm.1), custom_call_target="tpu_custom_call" | custom-call | flops 1572864000 | bytes 8192000 | tf_op jit(solution)/shard_map/tail/pallas_call | solution.py:472
  87.6 0.0 copy-done.2
  87.6 0.7 add_convert_fusion.1
  (5 shorter events, 0.1 us)
Async XLA Ops:
  28.1 36.4 %collective-permute-start = (f32[96,4096]{1,0:T(8,128)}, f32[96,4096]{1,0:T(8,128)S(1)}, u32[]{:S(2)}, u32[]{:S(2)}) collective-permute-start(f32[96,4096]{1,0:T(8,128)} %get-tuple-element.11), channel_id=1, source_target_pairs={{0,4},{4,0},{1,5},{5,1},{2,6},{6,2},{3,7},{7,3}} | collective-permute-start | bytes 4718600 | tf_op jit(solution)/shard_map/ppermute | solution.py:520
  32.1 0.7 copy-start.1
  32.7 31.7 %copy-start = (f32[2,96,512]{2,1,0:T(8,128)S(1)}, f32[2,96,512]{2,1,0:T(8,128)}, u32[]{:S(2)}) copy-start(f32[2,96,512]{2,1,0:T(8,128)} %get-tuple-element.10.g_first) | copy-start | bytes 1179652
  56.4 31.2 %copy-start.2 = (bf16[192,320]{1,0:T(8,128)(2,1)S(1)}, bf16[192,320]{1,0:T(8,128)(2,1)}, u32[]{:S(2)}) copy-start(bf16[192,320]{1,0:T(8,128)(2,1)} %x_hbm.1) | copy-start | bytes 368644

commit v8 on v7

--- a/solution.py
+++ b/solution.py
@@ -94,12 +94,10 @@
 
 def start_barrier(me_x, me_yz):
     barrier = pltpu.get_barrier_semaphore()
-    for dx in range(2):
-        for k in range(4):
-            if dx or k:
-                peer = (lax.rem(me_x + dx, 2), lax.rem(me_yz + k, 4))
-                pl.semaphore_signal(barrier, inc=1, device_id=peer, device_id_type=MESH)
-    return lambda: pl.semaphore_wait(barrier, 7)
+    peers = [(lax.rem(me_x + 1, 2), me_yz)] + [(me_x, lax.rem(me_yz + k, 4)) for k in (1, 2, 3)]
+    for peer in peers:
+        pl.semaphore_signal(barrier, inc=1, device_id=peer, device_id_type=MESH)
+    return lambda: pl.semaphore_wait(barrier, len(peers))
 
 
 def spread(rows, cols, first):
@@ -163,13 +161,9 @@
             col = e * (half // 8) + j
             tile = jnp.where(lane == col, sum_1[8 * j:8 * j + 8], tile)
             tile = jnp.where(lane == 32 + col, sum_2[8 * j:8 * j + 8], tile)
-    me = me_x * 4 + me_yz
-    stats[me] = tile
+    stats[me_yz] = tile
     others_ready()
-    t_out = [
-        remote(stats.at[me], stats.at[me], t_send.at[4 * dx + k], t_recv.at[4 * dx + k], lax.rem(me_x + dx, 2), lax.rem(me_yz + k, 4))
-        for dx in range(2) for k in range(4) if dx or k
-    ]
+    t_out = [remote(stats.at[me_yz], stats.at[me_yz], t_send.at[k], t_recv.at[k], me_x, lax.rem(me_yz + k, 4)) for k in (1, 2, 3)]
     for copy in t_out:
         copy.start()
     scale_in.wait()
@@ -189,9 +183,11 @@
     gather = jnp.where(i == 2 * c, 1.0, 0.0).astype(jnp.bfloat16)
     for copy in t_out:
         copy.wait()
-    total = stats[0]
-    for i in range(1, 8):
-        total = total + stats[i]
+    stats[4] = stats[0] + stats[1] + stats[2] + stats[3]
+    t_over = remote(stats.at[4], stats.at[5], t_send.at[0], t_recv.at[0], other_x, me_yz)
+    t_over.start()
+    t_over.wait()
+    total = stats[4] + stats[5]
     mean_t = total / d_model
     var_t = pltpu.roll(total, 96, 1) / d_model - mean_t * mean_t
     rstd_t = lax.rsqrt(var_t + LN_EPS)
@@ -320,7 +316,7 @@
             pltpu.VMEM((4, 2, half, chunk), bf16),
             pltpu.VMEM((chunk,), f32),
             pltpu.VMEM((4, 1, chunk), f32),
-            pltpu.VMEM((8, 8, 128), f32),
+            pltpu.VMEM((6, 8, 128), f32),
             pltpu.VMEM((4, half, chunk), bf16),
             pltpu.VMEM((2 * rows, 2 * depth), bf16),
             pltpu.VMEM((half, depth), bf16),
@@ -333,7 +329,7 @@
             pltpu.VMEM((early, half, 512), f32),
             pltpu.VMEM((half, width), f32),
             pltpu.VMEM((half, 2 * ff), f32),
-            dma((4,)), dma((8,)), dma((3, 2)), dma((3, 2)), dma((4,)), dma((4,)), dma((8,)), dma((8,)), dma((4,)), dma((4,)), dma((4,)),
+            dma((4,)), dma((8,)), dma((3, 2)), dma((3, 2)), dma((4,)), dma((4,)), dma((4,)), dma((4,)), dma((4,)), dma((4,)), dma((4,)),
             dma((early,)), dma((early,)), dma((3,)),
         ],
         compiler_params=pltpu.CompilerParams(collective_id=0, has_side_effects=True, vmem_limit_bytes=VMEM_MOST),
@@ -344,7 +340,7 @@
 
 def tail_kernel(
     g_first, g_peer, own_hbm, ov, wd_hbm, wo_hbm, y_ref,
-    g_own, oa, of, hb, wd, wo, out_part, y_send, y_pair, y_over, y_recv,
+    g_own, oy, oa, of, hb, wd, wo, out_part, y_send, y_pair, y_over, y_recv,
     in_sem, own_sem, o_send, o_recv, h_send, h_recv, p_send, p_recv, y_ssem, y_rsem,
 ):
     me_x = lax.axis_index('x')
@@ -361,10 +357,7 @@
     across = lax.rem(me_yz + 2, 4)
     other_x = lax.rem(me_x + 1, 2)
 
-    def rows_of(i):
-        return pl.ds(span * i, span)
-
-    own_in = [pltpu.make_async_copy(own_hbm.at[rows_of(i)], g_own.at[rows_of(i)], own_sem.at[i]) for i in range(groups)]
+    own_in = [pltpu.make_async_copy(own_hbm.at[pl.ds(span * i, span)], g_own.at[pl.ds(span * i, span)], own_sem.at[i]) for i in range(groups)]
     wo_in = pltpu.make_async_copy(wo_hbm, wo, in_sem.at[1])
     wd_in = pltpu.make_async_copy(wd_hbm, wd, in_sem.at[2])
     for copy in (*own_in, wo_in, wd_in):
@@ -377,21 +370,24 @@
             src_ref=src, dst_ref=dst, send_sem=send, recv_sem=recv, device_id=(to_x, to_yz), device_id_type=MESH,
         )
 
-    o_out = []
-    for dx in range(2):
-        for k in range(4):
-            if dx or k:
-                there = lax.rem(me_yz + k, 4)
-                o_out.append(remote(ov.at[there], oa.at[me], o_send.at[4 * dx + k], o_recv.at[4 * dx + k], lax.rem(me_x + dx, 2), there))
+    other = other_x * 4 + me_yz
+    o_over = remote(ov, oy, o_send.at[0], o_recv.at[0], other_x, me_yz)
+    o_over.start()
+    there = [lax.rem(me_yz + k, 4) for k in range(4)]
+    o_out = [remote(ov.at[there[k]], oa.at[me], o_send.at[k], o_recv.at[k], me_x, there[k]) for k in (1, 2, 3)]
     for copy in o_out:
         copy.start()
     oa[me] = ov[me_yz]
 
-    h_out = []
-
-    def activate(i):
-        own_in[i].wait()
-        at = rows_of(i)
+    def h_copy(i):
+        return remote(hb.at[i, me_x], hb.at[i, me_x], h_send.at[i], h_recv.at[i], other_x, me_yz)
+
+    for copy in own_in:
+        copy.wait()
+
+    def activate(i, carry):
+        at = pl.ds(pl.multiple_of(span * i, span), span)
+
         def act(gate, up):
             gate = gate.astype(jnp.bfloat16).astype(jnp.float32)
             up = up.astype(jnp.bfloat16).astype(jnp.float32)
@@ -403,13 +399,16 @@
             hb[i, me_x, :, cols] = act(g_own[at, cols] + g_first[c, at, :wide], g_own[at, up_cols] + g_first[c, at, wide:])
         done = early * wide
         hb[i, me_x, :, done:] = act(g_own[at, done:ff] + g_peer[at, :ff - done], g_own[at, ff + done:] + g_peer[at, ff - done:])
-        copy = remote(hb.at[i, me_x], hb.at[i, me_x], h_send.at[i], h_recv.at[i], other_x, me_yz)
-        copy.start()
-        h_out.append(copy)
-
-    for i in range(groups):
-        activate(i)
-    for copy in o_out:
+        h_copy(i).start()
+        return carry
+
+    lax.fori_loop(0, groups, activate, 0)
+    o_over.wait()
+    relay = [remote(oy.at[there[k]], oa.at[other], o_send.at[3 + k], o_recv.at[3 + k], me_x, there[k]) for k in (1, 2, 3)]
+    for copy in relay:
+        copy.start()
+    oa[other] = oy[me_yz]
+    for copy in (*o_out, *relay):
         copy.wait()
     for e in range(8):
         of[owned * e:owned * e + owned] = oa[e].astype(jnp.float32)
@@ -417,44 +416,46 @@
     out_part[...] = jnp.dot(of[...].astype(jnp.bfloat16), wo[...], preferred_element_type=jnp.float32)
     wd_in.wait()
 
-    pair, over = [], []
-
-    def product(i):
-        h_out[i].wait()
+    def pair_copies(i):
+        return [remote(y_send.at[i, 2 * e + 1 - core], y_pair.at[i, e], p_send.at[i, e], p_recv.at[i, e], me_x, partner) for e in range(2)]
+
+    def over_copy(i):
+        return remote(y_over.at[i], y_recv.at[i], y_ssem.at[i], y_rsem.at[i], me_x, across)
+
+    def cross(i):
+        for copy in pair_copies(i):
+            copy.wait()
+        y_over[i] = y_send[i, across] + y_pair[i, 1 - col]
+        over_copy(i).start()
+
+    def product(i, carry):
+        h_copy(i).wait()
         part = jnp.dot(hb[i].reshape(2 * span, ff), wd[...], preferred_element_type=jnp.float32)
-        part = part + jnp.concatenate([out_part[span * i:span * i + span], out_part[half + span * i:half + span * i + span]], axis=0)
+        first_at = pl.multiple_of(span * i, span)
+        part = part + jnp.concatenate([out_part[pl.ds(first_at, span)], out_part[pl.ds(half + first_at, span)]], axis=0)
         for j in range(4):
             moved = part if j == 0 else pltpu.roll(part, (4 - j) * chunk, 1)
             y_send[i, j] = moved[:, :chunk]
-        pair.append([
-            remote(y_send.at[i, 2 * e + 1 - core], y_pair.at[i, e], p_send.at[i, e], p_recv.at[i, e], me_x, partner) for e in range(2)
-        ])
-        for copy in pair[i]:
+        for copy in pair_copies(i):
             copy.start()
 
-    def cross(i):
-        for copy in pair[i]:
-            copy.wait()
-        y_over[i] = y_send[i, across] + y_pair[i, 1 - col]
-        over.append(remote(y_over.at[i], y_recv.at[i], y_ssem.at[i], y_rsem.at[i], me_x, across))
-        over[i].start()
-
-    def finish(i):
-        over[i].wait()
+        @pl.when(i > 0)
+        def _():
+            cross(i - 1)
+
+        return carry
+
+    def finish(i, carry):
+        over_copy(i).wait()
         total = y_send[i, me_yz] + y_pair[i, col] + y_recv[i]
         for e in range(2):
-            at = pl.ds(half * e + span * i, span)
-            y_ref[at, :] = total[span * e:span * e + span]
-
-    for i in range(groups):
-        product(i)
-        if i >= 1:
-            cross(i - 1)
-    for i in range(groups - 3):
-        finish(i)
+            y_ref[pl.ds(pl.multiple_of(half * e + span * i, span), span), :] = total[span * e:span * e + span]
+        return carry
+
+    lax.fori_loop(0, groups, product, 0)
+    lax.fori_loop(0, groups - 3, finish, 0)
     cross(groups - 1)
-    for i in range(groups - 3, groups):
-        finish(i)
+    lax.fori_loop(groups - 3, groups, finish, 0)
 
 
 def tail(g_first, g_peer, g_own, o_blocks, w_down, w_out):
@@ -476,6 +477,7 @@
         out_specs=pl.BlockSpec(memory_space=pltpu.VMEM),
         scratch_shapes=[
             pltpu.VMEM((half, 2 * ff), f32),
+            pltpu.VMEM((4, owned, o_width), bf16),
             pltpu.VMEM((8, owned, o_width), bf16),
             pltpu.VMEM((rows, o_width), f32),
             pltpu.VMEM((groups, 2, span, ff), bf16),

time: 88.5 us -> 88.7 us (level)
    pallas_call x1, Pallas kernels: 27.4 us -> 28.3 us  [head(): pl.pallas_call(functools.partial(head_kernel, d_model, early), out_shape=...]
where the time goes in v8:
time: 88.7 us; the launch traced here: 88.5 us
  Pallas kernels  74.6 us (84%)
  waiting for transfers between devices  7.67 us (9%)
  local copies, waits for them, and re-layouts  2.3 us (3%)
  other arithmetic  2.14 us (2%)
  starting transfers between devices  1.06 us (1%)
    pallas_call x1, Pallas kernels, head(): pl.pallas_call(functools.partial(head_kernel, d_model, early), out_shape=...  28.3 us
    pallas_call x1, Pallas kernels, attend(): pl.pallas_call(functools.partial(attention_kernel, head_dim ** (-0.5)), o...  23.7 us
    pallas_call x1, Pallas kernels, tail(): pl.pallas_call(tail_kernel, out_shape=jax.ShapeDtypeStruct((rows, chunk),...  22.6 us
    ppermute x1, waiting for transfers between devices, local_step(): g_peer = lax.ppermute(g_send, 'x', [(0, 1), (1, 0)])  7.67 us
  transfers between devices with their start and end apart: 1, of which 1 were waited for; matrix products, arithmetic and copies ran while one was open for 3% of the time, Pallas kernels for 27%

profile of v8, /device:TPU:0, one launch (start us, length us, event | category | flops | bytes accessed | tf_op | source)
XLA Modules:
  0.0 88.5 jit_solution(14851186054546815381)
XLA Ops:
  0.6 28.3 %head.1 = (bf16[4,24,680]{2,1,0:T(8,128)(2,1)}, f32[2,96,512]{2,1,0:T(8,128)}, f32[96,4096]{1,0:T(8,128)}, f32[96,5120]{1,0:T(8,128)}) custom-call(bf16[192,320]{1,0:T(8,128)(2,1)} %x_hbm.1, f32[320]{0:T(512)} %scale_hbm.1, bf16[1280,2,2560]{2,1,0:T(2,128)(2,1)} %wg_hbm.1, bf16[680,1280]{1,0:T(8,128)(2,1)} %bitcast.26), custom_call_target="tpu_custom_call" | custom-call | flops 5033164800 | bytes 13107200 | tf_op jit(solution)/shard_map/head/pallas_call | solution.py:305
  29.0 1.1 %collective-permute-start = (f32[96,4096]{1,0:T(8,128)}, f32[96,4096]{1,0:T(8,128)S(1)}, u32[]{:S(2)}, u32[]{:S(2)}) collective-permute-start(f32[96,4096]{1,0:T(8,128)} %get-tuple-element.11), channel_id=1, source_target_pairs={{0,4},{4,0},{1,5},{5,1},{2,6},{6,2},{3,7},{7,3}} | collective-permute-start | bytes 4718600 | tf_op jit(solution)/shard_map/ppermute | solution.py:522
  30.0 0.7 convert_element_type.40
  30.7 1.0 %copy.22 = bf16[24,4,680]{2,1,0:T(4,128)(2,1)S(1)} copy(bf16[24,4,680]{2,0,1:T(8,128)(2,1)} %bitcast.23) | data formatting | bytes 261120 | tf_op jit(solution)/shard_map/transpose | solution.py:523
  31.7 0.1 reshape.134
  31.8 0.1 fusion.8
  31.9 0.1 fusion.5
  32.0 0.1 maximum_bitcast_fusion
  32.1 0.1 copy.23
  32.3 0.2 reshape.136
  32.5 0.1 multiply_cosine_fusion.1
  32.6 0.2 subtract_convert_fusion
  32.8 0.1 pad_maximum_fusion.q_ref
  32.9 0.0 copy-start.1
  33.0 0.6 copy-done.1
  33.6 0.0 copy-start
  33.6 23.7 %attend.1 = (bf16[24,32,80]{2,1,0:T(8,128)(2,1)S(1)}, bf16[24,80,4096]{2,1,0:T(8,128)(2,1)}, bf16[24,80,4096]{2,1,0:T(8,128)(2,1)}) custom-call(s32[24]{0:T(128)S(1)} %copy-done.1, bf16[24,32,80]{2,1,0:T(8,128)(2,1)S(1)} %pad_maximum_fusion.q_ref, f32[2,80,128]{2,1,0:T(8,128)S(1)} %pad_convert_fusion.cols_ref, bf16[24,80,4096]{2,1,0:T(8,128)(2,1)} %bitcast.20, ...), custom_call_target="tpu_custom_call" | custom-call | flops 1006632960 | bytes 62914560 | tf_op jit(solution)/shard_map/attend/pallas_call | solution.py:67
  57.3 0.0 copy-start.2
  57.3 0.2 reshape.135
  57.5 7.7 %collective-permute-done.g_peer = f32[96,4096]{1,0:T(8,128)S(1)} collective-permute-done((f32[96,4096]{1,0:T(8,128)}, f32[96,4096]{1,0:T(8,128)S(1)}, u32[]{:S(2)}, u32[]{:S(2)}) %collective-permute-start) | collective-permute-done | bytes 1572896 | tf_op jit(solution)/shard_map/ppermute | solution.py:522
  65.2 0.0 copy-done
  65.2 22.6 %tail.1 = f32[192,320]{1,0:T(8,128)S(1)} custom-call(f32[2,96,512]{2,1,0:T(8,128)S(1)} %copy-done, f32[96,4096]{1,0:T(8,128)S(1)} %collective-permute-done.g_peer, f32[96,5120]{1,0:T(8,128)} %get-tuple-element.12.own_hbm, bf16[4,24,640]{2,1,0:T(8,128)(2,1)S(1)} %bitcast.19, bf16[2560,1280]{1,0:T(8,128)(2,1)} %wd_hbm.1, bf16[640,1280]{1,0:T(8,128)(2,1)} %wo_hbm.1), custom_call_target="tpu_custom_call" | custom-call | flops 1572864000 | bytes 8192000 | tf_op jit(solution)/shard_map/tail/pallas_call | solution.py:473
  87.8 0.0 copy-done.2
  87.8 0.7 add_convert_fusion.1
  (5 shorter events, 0.1 us)
Async XLA Ops:
  29.0 36.2 %collective-permute-start = (f32[96,4096]{1,0:T(8,128)}, f32[96,4096]{1,0:T(8,128)S(1)}, u32[]{:S(2)}, u32[]{:S(2)}) collective-permute-start(f32[96,4096]{1,0:T(8,128)} %get-tuple-element.11), channel_id=1, source_target_pairs={{0,4},{4,0},{1,5},{5,1},{2,6},{6,2},{3,7},{7,3}} | collective-permute-start | bytes 4718600 | tf_op jit(solution)/shard_map/ppermute | solution.py:522
  32.9 0.7 copy-start.1
  33.6 31.6 %copy-start = (f32[2,96,512]{2,1,0:T(8,128)S(1)}, f32[2,96,512]{2,1,0:T(8,128)}, u32[]{:S(2)}) copy-start(f32[2,96,512]{2,1,0:T(8,128)} %get-tuple-element.10.g_first) | copy-start | bytes 1179652
  57.3 30.6 %copy-start.2 = (bf16[192,320]{1,0:T(8,128)(2,1)S(1)}, bf16[192,320]{1,0:T(8,128)(2,1)}, u32[]{:S(2)}) copy-start(bf16[192,320]{1,0:T(8,128)(2,1)} %x_hbm.1) | copy-start | bytes 368644

commit v9 on v8

--- a/solution.py
+++ b/solution.py
@@ -92,11 +92,11 @@
     return o, jnp.swapaxes(k_new, 1, 2), jnp.swapaxes(v_new, 1, 2)
 
 
-def start_barrier(me_x, me_yz):
+def start_barrier(me_x, me_yz, everyone):
     barrier = pltpu.get_barrier_semaphore()
-    peers = [(lax.rem(me_x + 1, 2), me_yz)] + [(me_x, lax.rem(me_yz + k, 4)) for k in (1, 2, 3)]
-    for peer in peers:
-        pl.semaphore_signal(barrier, inc=1, device_id=peer, device_id_type=MESH)
+    peers = [(dx, k) for dx in range(2) for k in range(4) if (dx or k) and (everyone or not (dx and k))]
+    for dx, k in peers:
+        pl.semaphore_signal(barrier, inc=1, device_id=(lax.rem(me_x + dx, 2), lax.rem(me_yz + k, 4)), device_id_type=MESH)
     return lambda: pl.semaphore_wait(barrier, len(peers))
 
 
@@ -108,7 +108,7 @@
 
 def head_kernel(
     d_model, early, x_hbm, scale_hbm, wg_hbm, wa_hbm, z_hbm, first_hbm, send_hbm, own_hbm,
-    xg, scale_row, sg, stats, h_buf, hx, hc, wg, wa, z_send, z_own, z_recv, r_send, r_own, r_recv, zb, zg, g_first, g_rest, g_own,
+    xg, scale_row, sg, stats, h_buf, hx, wg, wa, z_send, z_own, z_recv, r_send, r_own, r_recv, zb, zg, g_first, g_rest, g_own,
     in_sem, wg_sem, x_send, x_recv, s_send, s_recv, t_send, t_recv, z_sems, a_send, a_recv, f_send, f_recv, out_sem,
 ):
     me_x = lax.axis_index('x')
@@ -137,7 +137,7 @@
     ]
     for copy in (*x_in, scale_in, wa_in):
         copy.start()
-    others_ready = start_barrier(me_x, me_yz)
+    others_ready = start_barrier(me_x, me_yz, True)
 
     def remote(src, dst, send, recv, to_x, to_yz):
         return pltpu.make_async_remote_copy(
@@ -161,9 +161,13 @@
             col = e * (half // 8) + j
             tile = jnp.where(lane == col, sum_1[8 * j:8 * j + 8], tile)
             tile = jnp.where(lane == 32 + col, sum_2[8 * j:8 * j + 8], tile)
-    stats[me_yz] = tile
+    me = me_x * 4 + me_yz
+    stats[me] = tile
     others_ready()
-    t_out = [remote(stats.at[me_yz], stats.at[me_yz], t_send.at[k], t_recv.at[k], me_x, lax.rem(me_yz + k, 4)) for k in (1, 2, 3)]
+    t_out = [
+        remote(stats.at[me], stats.at[me], t_send.at[4 * dx + k], t_recv.at[4 * dx + k], lax.rem(me_x + dx, 2), lax.rem(me_yz + k, 4))
+        for dx in range(2) for k in range(4) if dx or k
+    ]
     for copy in t_out:
         copy.start()
     scale_in.wait()
@@ -178,34 +182,52 @@
         copy.start()
     wide, thin = spread(128, 256, 0), spread(64, 128, 0)
     wide_u, thin_u = spread(128, 256, 1), spread(64, 128, 1)
-    i = lax.broadcasted_iota(jnp.int32, (256, 128), 0)
-    c = lax.broadcasted_iota(jnp.int32, (256, 128), 1)
-    gather = jnp.where(i == 2 * c, 1.0, 0.0).astype(jnp.bfloat16)
     for copy in t_out:
         copy.wait()
-    stats[4] = stats[0] + stats[1] + stats[2] + stats[3]
-    t_over = remote(stats.at[4], stats.at[5], t_send.at[0], t_recv.at[0], other_x, me_yz)
-    t_over.start()
-    t_over.wait()
-    total = stats[4] + stats[5]
+    total = stats[0]
+    for i in range(1, 8):
+        total = total + stats[i]
     mean_t = total / d_model
     var_t = pltpu.roll(total, 96, 1) / d_model - mean_t * mean_t
     rstd_t = lax.rsqrt(var_t + LN_EPS)
     for copy in s_out:
         copy.wait()
 
-    def normalize(p):
+    def rows_scale(p):
         shift = lax.rem(128 - order[p] * (half // 8), 128)
         mean_p = pltpu.roll(mean_t, shift, 1)
         rstd_p = pltpu.roll(rstd_t, shift, 1)
         mean = jnp.concatenate([mean_p[:, j:j + 1] for j in range(half // 8)], axis=0)
         rstd = jnp.concatenate([rstd_p[:, j:j + 1] for j in range(half // 8)], axis=0)
+        return mean, rstd
+
+    chip = me_yz // 2
+    contract = (((1,), (1,)), ((), ()))
+
+    def project_chip(p, which, mean, rstd):
+        both = []
+        for e in range(2):
+            s = 2 * which + e
+            h = (xg[s, order[p]].astype(jnp.float32) - mean) * rstd * sg[s]
+            h_buf[s] = h.astype(jnp.bfloat16)
+            both.append(h)
+        h = jnp.concatenate(both, axis=1).astype(jnp.bfloat16)
+        at = pl.ds(pl.multiple_of(2 * chunk * which, 128), 2 * chunk)
+        z = lax.dot_general(h, wa[:full, at], contract, preferred_element_type=jnp.float32)
+        r = lax.dot_general(h, wa[full:, at], contract, preferred_element_type=jnp.float32)
+        return z, r
+
+    def project(p):
+        mean, rstd = rows_scale(p)
         x_copy(1, p).wait()
         x_copy(2, p).start()
         x_copy(0, p).wait()
+        z_near, r_near = project_chip(p, chip, mean, rstd)
         x_copy(2, p).wait()
-        for s in range(4):
-            h_buf[s] = ((xg[s, order[p]].astype(jnp.float32) - mean) * rstd * sg[s]).astype(jnp.bfloat16)
+        z_far, r_far = project_chip(p, 1 - chip, mean, rstd)
+        r = r_near + r_far
+        r = jnp.concatenate([r[third * i:third * i + third] for i in range(3)], axis=1)
+        return (z_near + z_far).reshape(z_send.shape), r
 
     def spread_half(part, g):
         out = pl.ds((2 * part + g) * half, half)
@@ -218,25 +240,14 @@
             piece = h_buf[s, :, 256:320]
             hx[out, base + 512:base + 640] = jnp.dot(piece, b, preferred_element_type=jnp.float32).astype(jnp.bfloat16)
 
-    def project(part):
-        src = pl.ds(2 * part * half, half)
-        for t in range(4 * chunk // 128):
-            hc[:, 128 * t:128 * t + 128] = jnp.dot(hx[src, 256 * t:256 * t + 256], gather, preferred_element_type=jnp.float32).astype(jnp.bfloat16)
-        contract = (((1,), (1,)), ((), ()))
-        z = lax.dot_general(hc[...], wa[:full, :], contract, preferred_element_type=jnp.float32)
-        r = lax.dot_general(hc[...], wa[full:, :], contract, preferred_element_type=jnp.float32)
-        r = jnp.concatenate([r[third * i:third * i + third] for i in range(3)], axis=1)
-        return z.reshape(z_send.shape), r
-
-    normalize(0)
-    spread_half(0, 0)
     wa_in.wait()
     z_send[...], r_send[...] = project(0)
     z_out = [remote(z_send, z_recv, z_sems.at[0], z_sems.at[1], other_x, me_yz), remote(r_send, r_recv, z_sems.at[2], z_sems.at[3], other_x, me_yz)]
     for copy in z_out:
         copy.start()
+    spread_half(0, 0)
     spread_half(0, 1)
-    normalize(1)
+    z_own[...], r_own[...] = project(1)
     spread_half(1, 0)
     spread_half(1, 1)
     for copy in wg_in:
@@ -270,7 +281,6 @@
     save = [pltpu.make_async_copy(g_rest, send_hbm, out_sem.at[0]), pltpu.make_async_copy(g_own, own_hbm, out_sem.at[1])]
     for copy in save:
         copy.start()
-    z_own[...], r_own[...] = project(1)
     for copy in z_out:
         copy.wait()
     zb[:, :, :full] = (z_own[...] + z_recv[...]).astype(jnp.bfloat16)
@@ -316,10 +326,9 @@
             pltpu.VMEM((4, 2, half, chunk), bf16),
             pltpu.VMEM((chunk,), f32),
             pltpu.VMEM((4, 1, chunk), f32),
-            pltpu.VMEM((6, 8, 128), f32),
+            pltpu.VMEM((8, 8, 128), f32),
             pltpu.VMEM((4, half, chunk), bf16),
             pltpu.VMEM((2 * rows, 2 * depth), bf16),
-            pltpu.VMEM((half, depth), bf16),
             pltpu.VMEM((depth, 2, ff), bf16),
             pltpu.VMEM((z_cols, depth), bf16),
             *[pltpu.VMEM((4, owned, full), f32)] * 3,
@@ -329,7 +338,7 @@
             pltpu.VMEM((early, half, 512), f32),
             pltpu.VMEM((half, width), f32),
             pltpu.VMEM((half, 2 * ff), f32),
-            dma((4,)), dma((8,)), dma((3, 2)), dma((3, 2)), dma((4,)), dma((4,)), dma((4,)), dma((4,)), dma((4,)), dma((4,)), dma((4,)),
+            dma((4,)), dma((8,)), dma((3, 2)), dma((3, 2)), dma((4,)), dma((4,)), dma((8,)), dma((8,)), dma((4,)), dma((4,)), dma((4,)),
             dma((early,)), dma((early,)), dma((3,)),
         ],
         compiler_params=pltpu.CompilerParams(collective_id=0, has_side_effects=True, vmem_limit_bytes=VMEM_MOST),
@@ -362,7 +371,7 @@
     wd_in = pltpu.make_async_copy(wd_hbm, wd, in_sem.at[2])
     for copy in (*own_in, wo_in, wd_in):
         copy.start()
-    start_barrier(me_x, me_yz)()
+    start_barrier(me_x, me_yz, False)()
     me = me_x * 4 + me_yz
 
     def remote(src, dst, send, recv, to_x, to_yz):
@@ -416,28 +425,27 @@
     out_part[...] = jnp.dot(of[...].astype(jnp.bfloat16), wo[...], preferred_element_type=jnp.float32)
     wd_in.wait()
 
-    def pair_copies(i):
-        return [remote(y_send.at[i, 2 * e + 1 - core], y_pair.at[i, e], p_send.at[i, e], p_recv.at[i, e], me_x, partner) for e in range(2)]
+    def pair_copy(i, which):
+        return remote(y_send.at[i, 2 * which + 1 - core], y_pair.at[i, which], p_send.at[i, which], p_recv.at[i, which], me_x, partner)
 
     def over_copy(i):
         return remote(y_over.at[i], y_recv.at[i], y_ssem.at[i], y_rsem.at[i], me_x, across)
 
     def cross(i):
-        for copy in pair_copies(i):
-            copy.wait()
+        pair_copy(i, 1 - col).wait()
         y_over[i] = y_send[i, across] + y_pair[i, 1 - col]
         over_copy(i).start()
 
     def product(i, carry):
         h_copy(i).wait()
-        part = jnp.dot(hb[i].reshape(2 * span, ff), wd[...], preferred_element_type=jnp.float32)
         first_at = pl.multiple_of(span * i, span)
-        part = part + jnp.concatenate([out_part[pl.ds(first_at, span)], out_part[pl.ds(half + first_at, span)]], axis=0)
-        for j in range(4):
-            moved = part if j == 0 else pltpu.roll(part, (4 - j) * chunk, 1)
-            y_send[i, j] = moved[:, :chunk]
-        for copy in pair_copies(i):
-            copy.start()
+        for which in (1 - col, col):
+            at = pl.ds(pl.multiple_of(2 * chunk * which, 128), 2 * chunk)
+            part = jnp.dot(hb[i].reshape(2 * span, ff), wd[:, at], preferred_element_type=jnp.float32)
+            part = part + jnp.concatenate([out_part[pl.ds(first_at, span), at], out_part[pl.ds(half + first_at, span), at]], axis=0)
+            y_send[i, 2 * which] = part[:, :chunk]
+            y_send[i, 2 * which + 1] = pltpu.roll(part, chunk, 1)[:, :chunk]
+            pair_copy(i, which).start()
 
         @pl.when(i > 0)
         def _():
@@ -446,6 +454,7 @@
         return carry
 
     def finish(i, carry):
+        pair_copy(i, col).wait()
         over_copy(i).wait()
         total = y_send[i, me_yz] + y_pair[i, col] + y_recv[i]
         for e in range(2):

time: 88.7 us -> 88.7 us (level)
    pallas_call x1, Pallas kernels: 22.6 us -> 24.1 us  [tail(): pl.pallas_call(tail_kernel, out_shape=jax.ShapeDtypeStruct((rows, chunk),...]
    pallas_call x1, Pallas kernels: 28.3 us -> 26.9 us  [head(): pl.pallas_call(functools.partial(head_kernel, d_model, early), out_shape=...]
where the time goes in v9:
time: 88.7 us; the launch traced here: 88.5 us
  Pallas kernels  74.6 us (84%)
  waiting for transfers between devices  7.64 us (9%)
  local copies, waits for them, and re-layouts  2.3 us (3%)
  other arithmetic  2.14 us (2%)
  starting transfers between devices  1.09 us (1%)
    pallas_call x1, Pallas kernels, head(): pl.pallas_call(functools.partial(head_kernel, d_model, early), out_shape=...  26.9 us
    pallas_call x1, Pallas kernels, tail(): pl.pallas_call(tail_kernel, out_shape=jax.ShapeDtypeStruct((rows, chunk),...  24.1 us
    pallas_call x1, Pallas kernels, attend(): pl.pallas_call(functools.partial(attention_kernel, head_dim ** (-0.5)), o...  23.7 us
    ppermute x1, waiting for transfers between devices, local_step(): g_peer = lax.ppermute(g_send, 'x', [(0, 1), (1, 0)])  7.64 us
  transfers between devices with their start and end apart: 1, of which 1 were waited for; matrix products, arithmetic and copies ran while one was open for 3% of the time, Pallas kernels for 27%

profile of v9, /device:TPU:0, one launch (start us, length us, event | category | flops | bytes accessed | tf_op | source)
XLA Modules:
  0.0 88.5 jit_solution(15273310261150713808)
XLA Ops:
  0.6 26.9 %head.1 = (bf16[4,24,680]{2,1,0:T(8,128)(2,1)}, f32[2,96,512]{2,1,0:T(8,128)}, f32[96,4096]{1,0:T(8,128)}, f32[96,5120]{1,0:T(8,128)}) custom-call(bf16[192,320]{1,0:T(8,128)(2,1)} %x_hbm.1, f32[320]{0:T(512)} %scale_hbm.1, bf16[1280,2,2560]{2,1,0:T(2,128)(2,1)} %wg_hbm.1, bf16[680,1280]{1,0:T(8,128)(2,1)} %bitcast.26), custom_call_target="tpu_custom_call" | custom-call | flops 5033164800 | bytes 13107200 | tf_op jit(solution)/shard_map/head/pallas_call | solution.py:315
  27.5 1.1 %collective-permute-start = (f32[96,4096]{1,0:T(8,128)}, f32[96,4096]{1,0:T(8,128)S(1)}, u32[]{:S(2)}, u32[]{:S(2)}) collective-permute-start(f32[96,4096]{1,0:T(8,128)} %get-tuple-element.11), channel_id=1, source_target_pairs={{0,4},{4,0},{1,5},{5,1},{2,6},{6,2},{3,7},{7,3}} | collective-permute-start | bytes 4718600 | tf_op jit(solution)/shard_map/ppermute | solution.py:531
  28.6 0.7 convert_element_type.40
  29.3 1.0 %copy.22 = bf16[24,4,680]{2,1,0:T(4,128)(2,1)S(1)} copy(bf16[24,4,680]{2,0,1:T(8,128)(2,1)} %bitcast.23) | data formatting | bytes 261120 | tf_op jit(solution)/shard_map/transpose | solution.py:532
  30.2 0.1 reshape.134
  30.4 0.1 fusion.8
  30.5 0.1 fusion.5
  30.6 0.1 maximum_bitcast_fusion
  30.7 0.1 copy.23
  30.8 0.2 reshape.136
  31.1 0.1 multiply_cosine_fusion.1
  31.2 0.2 subtract_convert_fusion
  31.4 0.1 pad_maximum_fusion.q_ref
  31.5 0.0 copy-start.1
  31.5 0.6 copy-done.1
  32.2 0.0 copy-start
  32.2 23.7 %attend.1 = (bf16[24,32,80]{2,1,0:T(8,128)(2,1)S(1)}, bf16[24,80,4096]{2,1,0:T(8,128)(2,1)}, bf16[24,80,4096]{2,1,0:T(8,128)(2,1)}) custom-call(s32[24]{0:T(128)S(1)} %copy-done.1, bf16[24,32,80]{2,1,0:T(8,128)(2,1)S(1)} %pad_maximum_fusion.q_ref, f32[2,80,128]{2,1,0:T(8,128)S(1)} %pad_convert_fusion.cols_ref, bf16[24,80,4096]{2,1,0:T(8,128)(2,1)} %bitcast.20, ...), custom_call_target="tpu_custom_call" | custom-call | flops 1006632960 | bytes 62914560 | tf_op jit(solution)/shard_map/attend/pallas_call | solution.py:67
  55.8 0.0 copy-start.2
  55.8 0.2 reshape.135
  56.1 7.6 %collective-permute-done.g_peer = f32[96,4096]{1,0:T(8,128)S(1)} collective-permute-done((f32[96,4096]{1,0:T(8,128)}, f32[96,4096]{1,0:T(8,128)S(1)}, u32[]{:S(2)}, u32[]{:S(2)}) %collective-permute-start) | collective-permute-done | bytes 1572896 | tf_op jit(solution)/shard_map/ppermute | solution.py:531
  63.7 0.0 copy-done
  63.7 24.1 %tail.1 = f32[192,320]{1,0:T(8,128)S(1)} custom-call(f32[2,96,512]{2,1,0:T(8,128)S(1)} %copy-done, f32[96,4096]{1,0:T(8,128)S(1)} %collective-permute-done.g_peer, f32[96,5120]{1,0:T(8,128)} %get-tuple-element.12.own_hbm, bf16[4,24,640]{2,1,0:T(8,128)(2,1)S(1)} %bitcast.19, bf16[2560,1280]{1,0:T(8,128)(2,1)} %wd_hbm.1, bf16[640,1280]{1,0:T(8,128)(2,1)} %wo_hbm.1), custom_call_target="tpu_custom_call" | custom-call | flops 1572864000 | bytes 8192000 | tf_op jit(solution)/shard_map/tail/pallas_call | solution.py:482
  87.8 0.0 copy-done.2
  87.8 0.7 add_convert_fusion.1
  (5 shorter events, 0.1 us)
Async XLA Ops:
  27.5 36.2 %collective-permute-start = (f32[96,4096]{1,0:T(8,128)}, f32[96,4096]{1,0:T(8,128)S(1)}, u32[]{:S(2)}, u32[]{:S(2)}) collective-permute-start(f32[96,4096]{1,0:T(8,128)} %get-tuple-element.11), channel_id=1, source_target_pairs={{0,4},{4,0},{1,5},{5,1},{2,6},{6,2},{3,7},{7,3}} | collective-permute-start | bytes 4718600 | tf_op jit(solution)/shard_map/ppermute | solution.py:531
  31.5 0.7 copy-start.1
  32.2 31.5 %copy-start = (f32[2,96,512]{2,1,0:T(8,128)S(1)}, f32[2,96,512]{2,1,0:T(8,128)}, u32[]{:S(2)}) copy-start(f32[2,96,512]{2,1,0:T(8,128)} %get-tuple-element.10.g_first) | copy-start | bytes 1179652
  55.8 32.0 %copy-start.2 = (bf16[192,320]{1,0:T(8,128)(2,1)S(1)}, bf16[192,320]{1,0:T(8,128)(2,1)}, u32[]{:S(2)}) copy-start(bf16[192,320]{1,0:T(8,128)(2,1)} %x_hbm.1) | copy-start | bytes 368644

commit v10 on v9

--- a/solution.py
+++ b/solution.py
@@ -120,7 +120,8 @@
     ff = wg.shape[2]
     wide_cols = 256
     full = z_send.shape[2]
-    third = half // 3
+    quarter = half // 2
+    third = quarter // 3
     tail_cols = wa.shape[0] - full
     other_x = lax.rem(me_x + 1, 2)
     across = lax.rem(me_yz + 2, 4)
@@ -144,10 +145,10 @@
             src_ref=src, dst_ref=dst, send_sem=send, recv_sem=recv, device_id=(to_x, to_yz), device_id_type=MESH,
         )
 
-    def x_copy(kind, p):
+    def x_copy(kind, piece):
         owner = across if kind == 2 else me_yz
-        at = xg.at[owner, order[p]]
-        return remote(at, at, x_send.at[kind, p], x_recv.at[kind, p], me_x, across if kind == 1 else partner)
+        at = xg.at[owner, order[piece // 2], pl.ds(quarter * (piece % 2), quarter)]
+        return remote(at, at, x_send.at[kind, piece], x_recv.at[kind, piece], me_x, across if kind == 1 else partner)
 
     for p in range(2):
         x_in[p].wait()
@@ -175,9 +176,9 @@
     s_out = [remote(sg.at[me_yz], sg.at[me_yz], s_send.at[k], s_recv.at[k], me_x, lax.rem(me_yz + k, 4)) for k in (1, 2, 3)]
     for copy in s_out:
         copy.start()
-    for p in range(2):
-        x_copy(1, p).start()
-        x_copy(0, p).start()
+    for piece in range(4):
+        x_copy(1, piece).start()
+        x_copy(0, piece).start()
     for copy in wg_in:
         copy.start()
     wide, thin = spread(128, 256, 0), spread(64, 128, 0)
@@ -193,23 +194,27 @@
     for copy in s_out:
         copy.wait()
 
-    def rows_scale(p):
-        shift = lax.rem(128 - order[p] * (half // 8), 128)
+    chip = me_yz // 2
+    contract = (((1,), (1,)), ((), ()))
+
+    def pass_on(piece):
+        x_copy(1, piece).wait()
+        x_copy(2, piece).start()
+
+    def project_chip(piece, which):
+        p, q = piece // 2, piece % 2
+        blocks = quarter // 8
+        shift = lax.rem(256 - order[p] * (half // 8) - q * blocks, 128)
         mean_p = pltpu.roll(mean_t, shift, 1)
         rstd_p = pltpu.roll(rstd_t, shift, 1)
-        mean = jnp.concatenate([mean_p[:, j:j + 1] for j in range(half // 8)], axis=0)
-        rstd = jnp.concatenate([rstd_p[:, j:j + 1] for j in range(half // 8)], axis=0)
-        return mean, rstd
-
-    chip = me_yz // 2
-    contract = (((1,), (1,)), ((), ()))
-
-    def project_chip(p, which, mean, rstd):
+        mean = jnp.concatenate([mean_p[:, j:j + 1] for j in range(blocks)], axis=0)
+        rstd = jnp.concatenate([rstd_p[:, j:j + 1] for j in range(blocks)], axis=0)
+        here = pl.ds(quarter * q, quarter)
         both = []
         for e in range(2):
             s = 2 * which + e
-            h = (xg[s, order[p]].astype(jnp.float32) - mean) * rstd * sg[s]
-            h_buf[s] = h.astype(jnp.bfloat16)
+            h = (xg[s, order[p], here].astype(jnp.float32) - mean) * rstd * sg[s]
+            h_buf[s, here] = h.astype(jnp.bfloat16)
             both.append(h)
         h = jnp.concatenate(both, axis=1).astype(jnp.bfloat16)
         at = pl.ds(pl.multiple_of(2 * chunk * which, 128), 2 * chunk)
@@ -217,17 +222,24 @@
         r = lax.dot_general(h, wa[full:, at], contract, preferred_element_type=jnp.float32)
         return z, r
 
-    def project(p):
-        mean, rstd = rows_scale(p)
-        x_copy(1, p).wait()
-        x_copy(2, p).start()
-        x_copy(0, p).wait()
-        z_near, r_near = project_chip(p, chip, mean, rstd)
-        x_copy(2, p).wait()
-        z_far, r_far = project_chip(p, 1 - chip, mean, rstd)
-        r = r_near + r_far
-        r = jnp.concatenate([r[third * i:third * i + third] for i in range(3)], axis=1)
-        return (z_near + z_far).reshape(z_send.shape), r
+    def near(piece):
+        x_copy(0, piece).wait()
+        return project_chip(piece, chip)
+
+    def far(piece, z, r, z_ref, r_ref):
+        x_copy(2, piece).wait()
+        z_far, r_far = project_chip(piece, 1 - chip)
+        q = piece % 2
+        z_ref[2 * q:2 * q + 2] = (z + z_far).reshape(2, quarter // 2, full)
+        r = r + r_far
+        r_ref[q] = jnp.concatenate([r[third * i:third * i + third] for i in range(3)], axis=1)
+
+    def z_copies(q):
+        at = pl.ds(2 * q, 2)
+        return (
+            remote(z_send.at[at], z_recv.at[at], z_sems.at[0, q], z_sems.at[1, q], other_x, me_yz),
+            remote(r_send.at[q], r_recv.at[q], z_sems.at[2, q], z_sems.at[3, q], other_x, me_yz),
+        )
 
     def spread_half(part, g):
         out = pl.ds((2 * part + g) * half, half)
@@ -241,13 +253,22 @@
             hx[out, base + 512:base + 640] = jnp.dot(piece, b, preferred_element_type=jnp.float32).astype(jnp.bfloat16)
 
     wa_in.wait()
-    z_send[...], r_send[...] = project(0)
-    z_out = [remote(z_send, z_recv, z_sems.at[0], z_sems.at[1], other_x, me_yz), remote(r_send, r_recv, z_sems.at[2], z_sems.at[3], other_x, me_yz)]
-    for copy in z_out:
-        copy.start()
+    z_out = [*z_copies(0), *z_copies(1)]
+    pass_on(0)
+    far(0, *near(0), z_send, r_send)
+    z_out[0].start()
+    z_out[1].start()
+    pass_on(1)
+    part_1 = near(1)
+    pass_on(2)
+    far(1, *part_1, z_send, r_send)
+    z_out[2].start()
+    z_out[3].start()
+    pass_on(3)
     spread_half(0, 0)
     spread_half(0, 1)
-    z_own[...], r_own[...] = project(1)
+    for piece in (2, 3):
+        far(piece, *near(piece), z_own, r_own)
     spread_half(1, 0)
     spread_half(1, 1)
     for copy in wg_in:
@@ -284,9 +305,10 @@
     for copy in z_out:
         copy.wait()
     zb[:, :, :full] = (z_own[...] + z_recv[...]).astype(jnp.bfloat16)
-    r = r_own[...] + r_recv[...]
-    r = jnp.concatenate([r[:, tail_cols * i:tail_cols * i + tail_cols] for i in range(3)], axis=0)
-    zb[:, :, full:] = r.reshape(zb.shape[0], zb.shape[1], tail_cols).astype(jnp.bfloat16)
+    for q in range(2):
+        r = r_own[q] + r_recv[q]
+        r = jnp.concatenate([r[:, tail_cols * i:tail_cols * i + tail_cols] for i in range(3)], axis=0)
+        zb[2 * q:2 * q + 2, :, full:] = r.reshape(2, quarter // 2, tail_cols).astype(jnp.bfloat16)
     a_out = [remote(zb.at[lax.rem(me_yz + k, 4)], zg.at[me_yz], a_send.at[k], a_recv.at[k], me_x, lax.rem(me_yz + k, 4)) for k in (1, 2, 3)]
     for copy in a_out:
         copy.start()
@@ -332,13 +354,13 @@
             pltpu.VMEM((depth, 2, ff), bf16),
             pltpu.VMEM((z_cols, depth), bf16),
             *[pltpu.VMEM((4, owned, full), f32)] * 3,
-            *[pltpu.VMEM((half // 3, 3 * (z_cols - full)), f32)] * 3,
+            *[pltpu.VMEM((2, half // 6, 3 * (z_cols - full)), f32)] * 3,
             pltpu.VMEM((4, owned, z_cols), bf16),
             pltpu.VMEM((4, owned, z_cols), bf16),
             pltpu.VMEM((early, half, 512), f32),
             pltpu.VMEM((half, width), f32),
             pltpu.VMEM((half, 2 * ff), f32),
-            dma((4,)), dma((8,)), dma((3, 2)), dma((3, 2)), dma((4,)), dma((4,)), dma((8,)), dma((8,)), dma((4,)), dma((4,)), dma((4,)),
+            dma((4,)), dma((8,)), dma((3, 4)), dma((3, 4)), dma((4,)), dma((4,)), dma((8,)), dma((8,)), dma((4, 2)), dma((4,)), dma((4,)),
             dma((early,)), dma((early,)), dma((3,)),
         ],
         compiler_params=pltpu.CompilerParams(collective_id=0, has_side_effects=True, vmem_limit_bytes=VMEM_MOST),
@@ -439,12 +461,12 @@
     def product(i, carry):
         h_copy(i).wait()
         first_at = pl.multiple_of(span * i, span)
+        part = jnp.dot(hb[i].reshape(2 * span, ff), wd[...], preferred_element_type=jnp.float32)
+        part = part + jnp.concatenate([out_part[pl.ds(first_at, span)], out_part[pl.ds(half + first_at, span)]], axis=0)
+        for j in range(4):
+            moved = part if j == 0 else pltpu.roll(part, (4 - j) * chunk, 1)
+            y_send[i, j] = moved[:, :chunk]
         for which in (1 - col, col):
-            at = pl.ds(pl.multiple_of(2 * chunk * which, 128), 2 * chunk)
-            part = jnp.dot(hb[i].reshape(2 * span, ff), wd[:, at], preferred_element_type=jnp.float32)
-            part = part + jnp.concatenate([out_part[pl.ds(first_at, span), at], out_part[pl.ds(half + first_at, span), at]], axis=0)
-            y_send[i, 2 * which] = part[:, :chunk]
-            y_send[i, 2 * which + 1] = pltpu.roll(part, chunk, 1)[:, :chunk]
             pair_copy(i, which).start()
 
         @pl.when(i > 0)

time: 88.7 us -> 88.1 us (level)
  Pallas kernels: 74.6 us -> 73.7 us
    pallas_call x1, Pallas kernels: 24.1 us -> 22.6 us  [tail(): pl.pallas_call(tail_kernel, out_shape=jax.ShapeDtypeStruct((rows, chunk),...]
where the time goes in v10:
time: 88.1 us; the launch traced here: 87.9 us
  Pallas kernels  73.7 us (84%)
  waiting for transfers between devices  8.4 us (10%)
  local copies, waits for them, and re-layouts  2.3 us (3%)
  other arithmetic  2.14 us (2%)
    pallas_call x1, Pallas kernels, head(): pl.pallas_call(functools.partial(head_kernel, d_model, early), out_shape=...  27.4 us
    pallas_call x1, Pallas kernels, attend(): pl.pallas_call(functools.partial(attention_kernel, head_dim ** (-0.5)), o...  23.7 us
    pallas_call x1, Pallas kernels, tail(): pl.pallas_call(tail_kernel, out_shape=jax.ShapeDtypeStruct((rows, chunk),...  22.6 us
    ppermute x1, waiting for transfers between devices, local_step(): g_peer = lax.ppermute(g_send, 'x', [(0, 1), (1, 0)])  8.4 us
  transfers between devices with their start and end apart: 1, of which 1 were waited for; matrix products, arithmetic and copies ran while one was open for 3% of the time, Pallas kernels for 27%

profile of v10, /device:TPU:0, one launch (start us, length us, event | category | flops | bytes accessed | tf_op | source)
XLA Modules:
  0.0 87.9 jit_solution(12752514068989010643)
XLA Ops:
  0.6 27.4 %head.1 = (bf16[4,24,680]{2,1,0:T(8,128)(2,1)}, f32[2,96,512]{2,1,0:T(8,128)}, f32[96,4096]{1,0:T(8,128)}, f32[96,5120]{1,0:T(8,128)}) custom-call(bf16[192,320]{1,0:T(8,128)(2,1)} %x_hbm.1, f32[320]{0:T(512)} %scale_hbm.1, bf16[1280,2,2560]{2,1,0:T(2,128)(2,1)} %wg_hbm.1, bf16[680,1280]{1,0:T(8,128)(2,1)} %bitcast.26), custom_call_target="tpu_custom_call" | custom-call | flops 5033164800 | bytes 13107200 | tf_op jit(solution)/shard_map/head/pallas_call | solution.py:337
  28.0 0.6 collective-permute-start
  28.7 0.7 convert_element_type.40
  29.3 1.0 %copy.22 = bf16[24,4,680]{2,1,0:T(4,128)(2,1)S(1)} copy(bf16[24,4,680]{2,0,1:T(8,128)(2,1)} %bitcast.23) | data formatting | bytes 261120 | tf_op jit(solution)/shard_map/transpose | solution.py:554
  30.3 0.1 reshape.134
  30.5 0.1 fusion.8
  30.5 0.1 fusion.5
  30.7 0.1 maximum_bitcast_fusion
  30.8 0.1 copy.23
  30.9 0.2 reshape.136
  31.1 0.1 multiply_cosine_fusion.1
  31.3 0.2 subtract_convert_fusion
  31.4 0.1 pad_maximum_fusion.q_ref
  31.6 0.0 copy-start.1
  31.6 0.6 copy-done.1
  32.2 0.0 copy-start
  32.2 23.7 %attend.1 = (bf16[24,32,80]{2,1,0:T(8,128)(2,1)S(1)}, bf16[24,80,4096]{2,1,0:T(8,128)(2,1)}, bf16[24,80,4096]{2,1,0:T(8,128)(2,1)}) custom-call(s32[24]{0:T(128)S(1)} %copy-done.1, bf16[24,32,80]{2,1,0:T(8,128)(2,1)S(1)} %pad_maximum_fusion.q_ref, f32[2,80,128]{2,1,0:T(8,128)S(1)} %pad_convert_fusion.cols_ref, bf16[24,80,4096]{2,1,0:T(8,128)(2,1)} %bitcast.20, ...), custom_call_target="tpu_custom_call" | custom-call | flops 1006632960 | bytes 62914560 | tf_op jit(solution)/shard_map/attend/pallas_call | solution.py:67
  55.9 0.0 copy-start.2
  55.9 0.2 reshape.135
  56.2 8.4 %collective-permute-done.g_peer = f32[96,4096]{1,0:T(8,128)S(1)} collective-permute-done((f32[96,4096]{1,0:T(8,128)}, f32[96,4096]{1,0:T(8,128)S(1)}, u32[]{:S(2)}, u32[]{:S(2)}) %collective-permute-start) | collective-permute-done | bytes 1572896 | tf_op jit(solution)/shard_map/ppermute | solution.py:553
  64.6 0.0 copy-done
  64.6 22.6 %tail.1 = f32[192,320]{1,0:T(8,128)S(1)} custom-call(f32[2,96,512]{2,1,0:T(8,128)S(1)} %copy-done, f32[96,4096]{1,0:T(8,128)S(1)} %collective-permute-done.g_peer, f32[96,5120]{1,0:T(8,128)} %get-tuple-element.12.own_hbm, bf16[4,24,640]{2,1,0:T(8,128)(2,1)S(1)} %bitcast.19, bf16[2560,1280]{1,0:T(8,128)(2,1)} %wd_hbm.1, bf16[640,1280]{1,0:T(8,128)(2,1)} %wo_hbm.1), custom_call_target="tpu_custom_call" | custom-call | flops 1572864000 | bytes 8192000 | tf_op jit(solution)/shard_map/tail/pallas_call | solution.py:504
  87.2 0.0 copy-done.2
  87.2 0.7 add_convert_fusion.1
  (5 shorter events, 0.1 us)
Async XLA Ops:
  28.0 36.5 %collective-permute-start = (f32[96,4096]{1,0:T(8,128)}, f32[96,4096]{1,0:T(8,128)S(1)}, u32[]{:S(2)}, u32[]{:S(2)}) collective-permute-start(f32[96,4096]{1,0:T(8,128)} %get-tuple-element.11), channel_id=1, source_target_pairs={{0,4},{4,0},{1,5},{5,1},{2,6},{6,2},{3,7},{7,3}} | collective-permute-start | bytes 4718600 | tf_op jit(solution)/shard_map/ppermute | solution.py:553
  31.6 0.7 copy-start.1
  32.2 32.3 %copy-start = (f32[2,96,512]{2,1,0:T(8,128)S(1)}, f32[2,96,512]{2,1,0:T(8,128)}, u32[]{:S(2)}) copy-start(f32[2,96,512]{2,1,0:T(8,128)} %get-tuple-element.10.g_first) | copy-start | bytes 1179652
  55.9 31.3 %copy-start.2 = (bf16[192,320]{1,0:T(8,128)(2,1)S(1)}, bf16[192,320]{1,0:T(8,128)(2,1)}, u32[]{:S(2)}) copy-start(bf16[192,320]{1,0:T(8,128)(2,1)} %x_hbm.1) | copy-start | bytes 368644

commit v11 on v10

--- a/solution.py
+++ b/solution.py
@@ -267,32 +267,34 @@
     pass_on(3)
     spread_half(0, 0)
     spread_half(0, 1)
+    for copy in wg_in:
+        copy.wait()
+
+    def block(c):
+        at = pl.ds(pl.multiple_of(c * wide_cols, wide_cols), wide_cols)
+        return wg[:, :, at].reshape(2 * wg.shape[0], wide_cols)
+
+    def keep_own(c, out):
+        g_own[:, pl.ds(pl.multiple_of(c * wide_cols, wide_cols), wide_cols)] = out[:half]
+        g_own[:, pl.ds(pl.multiple_of(ff + c * wide_cols, wide_cols), wide_cols)] = out[half:]
+
+    first = []
+    for c in range(early):
+        out = jnp.dot(hx[:rows], block(c), preferred_element_type=jnp.float32)
+        g_first[c, :, :wide_cols] = out[:half]
+        g_first[c, :, wide_cols:] = out[half:]
+        first.append(remote(g_first.at[c], first_hbm.at[c], f_send.at[c], f_recv.at[c], other_x, me_yz))
+        first[-1].start()
     for piece in (2, 3):
         far(piece, *near(piece), z_own, r_own)
     spread_half(1, 0)
     spread_half(1, 1)
-    for copy in wg_in:
-        copy.wait()
-
-    def columns(c):
-        at = pl.ds(pl.multiple_of(c * wide_cols, wide_cols), wide_cols)
-        block = wg[:, :, at].reshape(2 * wg.shape[0], wide_cols)
-        out = jnp.dot(hx[...], block, preferred_element_type=jnp.float32)
-        up = pl.ds(pl.multiple_of(ff + c * wide_cols, wide_cols), wide_cols)
-        g_own[:, at] = out[2 * half:3 * half]
-        g_own[:, up] = out[3 * half:]
-        return out
-
-    first = []
     for c in range(early):
-        out = columns(c)
-        g_first[c, :, :wide_cols] = out[:half]
-        g_first[c, :, wide_cols:] = out[half:2 * half]
-        first.append(remote(g_first.at[c], first_hbm.at[c], f_send.at[c], f_recv.at[c], other_x, me_yz))
-        first[-1].start()
+        keep_own(c, jnp.dot(hx[rows:], block(c), preferred_element_type=jnp.float32))
 
     def rest(c, carry):
-        out = columns(c)
+        out = jnp.dot(hx[...], block(c), preferred_element_type=jnp.float32)
+        keep_own(c, out[rows:])
         at = (c - early) * wide_cols
         g_rest[:, pl.ds(pl.multiple_of(at, wide_cols), wide_cols)] = out[:half]
         g_rest[:, pl.ds(pl.multiple_of(ff - early * wide_cols + at, wide_cols), wide_cols)] = out[half:2 * half]

time: 88.1 us -> 87.7 us (level)
  transfers between devices with their start and end apart: 1 -> 1, of which waited for: 1 -> 1; matrix products, arithmetic and copies ran while one was open for 3% -> 4% of each run, Pallas kernels for 27% -> 27%
where the time goes in v11:
time: 87.7 us; the launch traced here: 87.6 us
  Pallas kernels  73.3 us (84%)
  waiting for transfers between devices  8.4 us (10%)
  local copies, waits for them, and re-layouts  2.3 us (3%)
  other arithmetic  2.14 us (2%)
    pallas_call x1, Pallas kernels, head(): pl.pallas_call(functools.partial(head_kernel, d_model, early), out_shape=...  27 us
    pallas_call x1, Pallas kernels, attend(): pl.pallas_call(functools.partial(attention_kernel, head_dim ** (-0.5)), o...  23.7 us
    pallas_call x1, Pallas kernels, tail(): pl.pallas_call(tail_kernel, out_shape=jax.ShapeDtypeStruct((rows, chunk),...  22.6 us
    ppermute x1, waiting for transfers between devices, local_step(): g_peer = lax.ppermute(g_send, 'x', [(0, 1), (1, 0)])  8.4 us
  transfers between devices with their start and end apart: 1, of which 1 were waited for; matrix products, arithmetic and copies ran while one was open for 4% of the time, Pallas kernels for 27%

profile of v11, /device:TPU:0, one launch (start us, length us, event | category | flops | bytes accessed | tf_op | source)
XLA Modules:
  0.0 87.6 jit_solution(6143567552896057858)
XLA Ops:
  0.6 27.0 %head.1 = (bf16[4,24,680]{2,1,0:T(8,128)(2,1)}, f32[2,96,512]{2,1,0:T(8,128)}, f32[96,4096]{1,0:T(8,128)}, f32[96,5120]{1,0:T(8,128)}) custom-call(bf16[192,320]{1,0:T(8,128)(2,1)} %x_hbm.1, f32[320]{0:T(512)} %scale_hbm.1, bf16[1280,2,2560]{2,1,0:T(2,128)(2,1)} %wg_hbm.1, bf16[680,1280]{1,0:T(8,128)(2,1)} %bitcast.26), custom_call_target="tpu_custom_call" | custom-call | flops 5033164800 | bytes 13107200 | tf_op jit(solution)/shard_map/head/pallas_call | solution.py:339
  27.7 0.6 collective-permute-start
  28.3 0.7 convert_element_type.40
  29.0 1.0 %copy.22 = bf16[24,4,680]{2,1,0:T(4,128)(2,1)S(1)} copy(bf16[24,4,680]{2,0,1:T(8,128)(2,1)} %bitcast.23) | data formatting | bytes 261120 | tf_op jit(solution)/shard_map/transpose | solution.py:556
  30.0 0.1 reshape.134
  30.1 0.1 fusion.8
  30.2 0.1 fusion.5
  30.3 0.1 maximum_bitcast_fusion
  30.4 0.1 copy.23
  30.5 0.2 reshape.136
  30.8 0.1 multiply_cosine_fusion.1
  30.9 0.2 subtract_convert_fusion
  31.1 0.1 pad_maximum_fusion.q_ref
  31.2 0.0 copy-start.1
  31.2 0.6 copy-done.1
  31.9 0.0 copy-start
  31.9 23.7 %attend.1 = (bf16[24,32,80]{2,1,0:T(8,128)(2,1)S(1)}, bf16[24,80,4096]{2,1,0:T(8,128)(2,1)}, bf16[24,80,4096]{2,1,0:T(8,128)(2,1)}) custom-call(s32[24]{0:T(128)S(1)} %copy-done.1, bf16[24,32,80]{2,1,0:T(8,128)(2,1)S(1)} %pad_maximum_fusion.q_ref, f32[2,80,128]{2,1,0:T(8,128)S(1)} %pad_convert_fusion.cols_ref, bf16[24,80,4096]{2,1,0:T(8,128)(2,1)} %bitcast.20, ...), custom_call_target="tpu_custom_call" | custom-call | flops 1006632960 | bytes 62914560 | tf_op jit(solution)/shard_map/attend/pallas_call | solution.py:67
  55.6 0.0 copy-start.2
  55.6 0.2 reshape.135
  55.8 8.4 %collective-permute-done.g_peer = f32[96,4096]{1,0:T(8,128)S(1)} collective-permute-done((f32[96,4096]{1,0:T(8,128)}, f32[96,4096]{1,0:T(8,128)S(1)}, u32[]{:S(2)}, u32[]{:S(2)}) %collective-permute-start) | collective-permute-done | bytes 1572896 | tf_op jit(solution)/shard_map/ppermute | solution.py:555
  64.2 0.0 copy-done
  64.2 22.6 %tail.1 = f32[192,320]{1,0:T(8,128)S(1)} custom-call(f32[2,96,512]{2,1,0:T(8,128)S(1)} %copy-done, f32[96,4096]{1,0:T(8,128)S(1)} %collective-permute-done.g_peer, f32[96,5120]{1,0:T(8,128)} %get-tuple-element.12.own_hbm, bf16[4,24,640]{2,1,0:T(8,128)(2,1)S(1)} %bitcast.19, bf16[2560,1280]{1,0:T(8,128)(2,1)} %wd_hbm.1, bf16[640,1280]{1,0:T(8,128)(2,1)} %wo_hbm.1), custom_call_target="tpu_custom_call" | custom-call | flops 1572864000 | bytes 8192000 | tf_op jit(solution)/shard_map/tail/pallas_call | solution.py:506
  86.8 0.0 copy-done.2
  86.9 0.7 add_convert_fusion.1
  (5 shorter events, 0.1 us)
Async XLA Ops:
  27.7 36.5 %collective-permute-start = (f32[96,4096]{1,0:T(8,128)}, f32[96,4096]{1,0:T(8,128)S(1)}, u32[]{:S(2)}, u32[]{:S(2)}) collective-permute-start(f32[96,4096]{1,0:T(8,128)} %get-tuple-element.11), channel_id=1, source_target_pairs={{0,4},{4,0},{1,5},{5,1},{2,6},{6,2},{3,7},{7,3}} | collective-permute-start | bytes 4718600 | tf_op jit(solution)/shard_map/ppermute | solution.py:555
  31.2 0.7 copy-start.1
  31.9 32.3 %copy-start = (f32[2,96,512]{2,1,0:T(8,128)S(1)}, f32[2,96,512]{2,1,0:T(8,128)}, u32[]{:S(2)}) copy-start(f32[2,96,512]{2,1,0:T(8,128)} %get-tuple-element.10.g_first) | copy-start | bytes 1179652
  55.6 31.3 %copy-start.2 = (bf16[192,320]{1,0:T(8,128)(2,1)S(1)}, bf16[192,320]{1,0:T(8,128)(2,1)}, u32[]{:S(2)}) copy-start(bf16[192,320]{1,0:T(8,128)(2,1)} %x_hbm.1) | copy-start | bytes 368644

commit v12 on v11

--- a/solution.py
+++ b/solution.py
@@ -300,10 +300,8 @@
         g_rest[:, pl.ds(pl.multiple_of(ff - early * wide_cols + at, wide_cols), wide_cols)] = out[half:2 * half]
         return carry
 
-    lax.fori_loop(early, ff // wide_cols, rest, 0)
-    save = [pltpu.make_async_copy(g_rest, send_hbm, out_sem.at[0]), pltpu.make_async_copy(g_own, own_hbm, out_sem.at[1])]
-    for copy in save:
-        copy.start()
+    middle = early + 4
+    lax.fori_loop(early, middle, rest, 0)
     for copy in z_out:
         copy.wait()
     zb[:, :, :full] = (z_own[...] + z_recv[...]).astype(jnp.bfloat16)
@@ -315,6 +313,10 @@
     for copy in a_out:
         copy.start()
     zg[me_yz] = zb[me_yz]
+    lax.fori_loop(middle, ff // wide_cols, rest, 0)
+    save = [pltpu.make_async_copy(g_rest, send_hbm, out_sem.at[0]), pltpu.make_async_copy(g_own, own_hbm, out_sem.at[1])]
+    for copy in save:
+        copy.start()
     for copy in a_out:
         copy.wait()
     save.append(pltpu.make_async_copy(zg, z_hbm, out_sem.at[2]))

time: 87.7 us -> 87 us (level)
  no operation moved by 1% of the time
where the time goes in v12:
time: 87 us; the launch traced here: 86.9 us
  Pallas kernels  73 us (84%)
  waiting for transfers between devices  7.69 us (9%)
  local copies, waits for them, and re-layouts  2.3 us (3%)
  other arithmetic  2.14 us (2%)
  starting transfers between devices  1.02 us (1%)
    pallas_call x1, Pallas kernels, head(): pl.pallas_call(functools.partial(head_kernel, d_model, early), out_shape=...  26.2 us
    pallas_call x1, Pallas kernels, attend(): pl.pallas_call(functools.partial(attention_kernel, head_dim ** (-0.5)), o...  23.7 us
    pallas_call x1, Pallas kernels, tail(): pl.pallas_call(tail_kernel, out_shape=jax.ShapeDtypeStruct((rows, chunk),...  23.1 us
    ppermute x1, waiting for transfers between devices, local_step(): g_peer = lax.ppermute(g_send, 'x', [(0, 1), (1, 0)])  7.69 us
  transfers between devices with their start and end apart: 1, of which 1 were waited for; matrix products, arithmetic and copies ran while one was open for 4% of the time, Pallas kernels for 27%

profile of v12, /device:TPU:0, one launch (start us, length us, event | category | flops | bytes accessed | tf_op | source)
XLA Modules:
  0.0 86.9 jit_solution(15741850475962911456)
XLA Ops:
  0.6 26.2 %head.1 = (bf16[4,24,680]{2,1,0:T(8,128)(2,1)}, f32[2,96,512]{2,1,0:T(8,128)}, f32[96,4096]{1,0:T(8,128)}, f32[96,5120]{1,0:T(8,128)}) custom-call(bf16[192,320]{1,0:T(8,128)(2,1)} %x_hbm.1, f32[320]{0:T(512)} %scale_hbm.1, bf16[1280,2,2560]{2,1,0:T(2,128)(2,1)} %wg_hbm.1, bf16[680,1280]{1,0:T(8,128)(2,1)} %bitcast.26), custom_call_target="tpu_custom_call" | custom-call | flops 5033164800 | bytes 13107200 | tf_op jit(solution)/shard_map/head/pallas_call | solution.py:341
  26.9 1.0 %collective-permute-start = (f32[96,4096]{1,0:T(8,128)}, f32[96,4096]{1,0:T(8,128)S(1)}, u32[]{:S(2)}, u32[]{:S(2)}) collective-permute-start(f32[96,4096]{1,0:T(8,128)} %get-tuple-element.11), channel_id=1, source_target_pairs={{0,4},{4,0},{1,5},{5,1},{2,6},{6,2},{3,7},{7,3}} | collective-permute-start | bytes 4718600 | tf_op jit(solution)/shard_map/ppermute | solution.py:557
  27.9 0.7 convert_element_type.40
  28.6 1.0 %copy.22 = bf16[24,4,680]{2,1,0:T(4,128)(2,1)S(1)} copy(bf16[24,4,680]{2,0,1:T(8,128)(2,1)} %bitcast.23) | data formatting | bytes 261120 | tf_op jit(solution)/shard_map/transpose | solution.py:558
  29.5 0.1 reshape.134
  29.7 0.1 fusion.8
  29.8 0.1 fusion.5
  29.9 0.1 maximum_bitcast_fusion
  30.0 0.1 copy.23
  30.1 0.2 reshape.136
  30.4 0.1 multiply_cosine_fusion.1
  30.5 0.2 subtract_convert_fusion
  30.7 0.1 pad_maximum_fusion.q_ref
  30.8 0.0 copy-start.1
  30.8 0.6 copy-done.1
  31.5 0.0 copy-start
  31.5 23.7 %attend.1 = (bf16[24,32,80]{2,1,0:T(8,128)(2,1)S(1)}, bf16[24,80,4096]{2,1,0:T(8,128)(2,1)}, bf16[24,80,4096]{2,1,0:T(8,128)(2,1)}) custom-call(s32[24]{0:T(128)S(1)} %copy-done.1, bf16[24,32,80]{2,1,0:T(8,128)(2,1)S(1)} %pad_maximum_fusion.q_ref, f32[2,80,128]{2,1,0:T(8,128)S(1)} %pad_convert_fusion.cols_ref, bf16[24,80,4096]{2,1,0:T(8,128)(2,1)} %bitcast.20, ...), custom_call_target="tpu_custom_call" | custom-call | flops 1006632960 | bytes 62914560 | tf_op jit(solution)/shard_map/attend/pallas_call | solution.py:67
  55.2 0.0 copy-start.2
  55.2 0.2 reshape.135
  55.4 7.7 %collective-permute-done.g_peer = f32[96,4096]{1,0:T(8,128)S(1)} collective-permute-done((f32[96,4096]{1,0:T(8,128)}, f32[96,4096]{1,0:T(8,128)S(1)}, u32[]{:S(2)}, u32[]{:S(2)}) %collective-permute-start) | collective-permute-done | bytes 1572896 | tf_op jit(solution)/shard_map/ppermute | solution.py:557
  63.1 0.0 copy-done
  63.1 23.1 %tail.1 = f32[192,320]{1,0:T(8,128)S(1)} custom-call(f32[2,96,512]{2,1,0:T(8,128)S(1)} %copy-done, f32[96,4096]{1,0:T(8,128)S(1)} %collective-permute-done.g_peer, f32[96,5120]{1,0:T(8,128)} %get-tuple-element.12.own_hbm, bf16[4,24,640]{2,1,0:T(8,128)(2,1)S(1)} %bitcast.19, bf16[2560,1280]{1,0:T(8,128)(2,1)} %wd_hbm.1, bf16[640,1280]{1,0:T(8,128)(2,1)} %wo_hbm.1), custom_call_target="tpu_custom_call" | custom-call | flops 1572864000 | bytes 8192000 | tf_op jit(solution)/shard_map/tail/pallas_call | solution.py:508
  86.1 0.0 copy-done.2
  86.2 0.7 add_convert_fusion.1
  (5 shorter events, 0.1 us)
Async XLA Ops:
  26.9 36.2 %collective-permute-start = (f32[96,4096]{1,0:T(8,128)}, f32[96,4096]{1,0:T(8,128)S(1)}, u32[]{:S(2)}, u32[]{:S(2)}) collective-permute-start(f32[96,4096]{1,0:T(8,128)} %get-tuple-element.11), channel_id=1, source_target_pairs={{0,4},{4,0},{1,5},{5,1},{2,6},{6,2},{3,7},{7,3}} | collective-permute-start | bytes 4718600 | tf_op jit(solution)/shard_map/ppermute | solution.py:557
  30.8 0.7 copy-start.1
  31.5 31.6 %copy-start = (f32[2,96,512]{2,1,0:T(8,128)S(1)}, f32[2,96,512]{2,1,0:T(8,128)}, u32[]{:S(2)}) copy-start(f32[2,96,512]{2,1,0:T(8,128)} %get-tuple-element.10.g_first) | copy-start | bytes 1179652
  55.2 31.0 %copy-start.2 = (bf16[192,320]{1,0:T(8,128)(2,1)S(1)}, bf16[192,320]{1,0:T(8,128)(2,1)}, u32[]{:S(2)}) copy-start(bf16[192,320]{1,0:T(8,128)(2,1)} %x_hbm.1) | copy-start | bytes 368644

commit v13 on v12

--- a/solution.py
+++ b/solution.py
@@ -11,7 +11,7 @@
 ROPE_BASE = 10000.0
 MESH = pl.DeviceIdType.MESH
 VMEM_MOST = 64 * 1024 * 1024 - 64 * 1024
-EARLY = 2
+EARLY = 3
 
 
 def attention_kernel(scale, len_ref, q_ref, cols_ref, k_hbm, v_hbm, o_ref, ko_hbm, vo_hbm, k_buf, v_buf, in_sem, out_sem):
@@ -300,7 +300,7 @@
         g_rest[:, pl.ds(pl.multiple_of(ff - early * wide_cols + at, wide_cols), wide_cols)] = out[half:2 * half]
         return carry
 
-    middle = early + 4
+    middle = early + 3
     lax.fori_loop(early, middle, rest, 0)
     for copy in z_out:
         copy.wait()

time: 87 us -> 87.2 us (level)
  Pallas kernels: 73 us -> 77.4 us
  waiting for transfers between devices: 7.69 us -> 3.48 us
    pallas_call x1, Pallas kernels: 26.2 us -> 30.6 us  [head(): pl.pallas_call(functools.partial(head_kernel, d_model, early), out_shape=...]
    ppermute x1, waiting for transfers between devices: 7.69 us -> 3.48 us  [local_step(): g_peer = lax.ppermute(g_send, 'x', [(0, 1), (1, 0)])]
where the time goes in v13:
time: 87.2 us; the launch traced here: 87.1 us
  Pallas kernels  77.4 us (89%)
  waiting for transfers between devices  3.48 us (4%)
  local copies, waits for them, and re-layouts  2.3 us (3%)
  other arithmetic  2.14 us (2%)
  starting transfers between devices  1.02 us (1%)
    pallas_call x1, Pallas kernels, head(): pl.pallas_call(functools.partial(head_kernel, d_model, early), out_shape=...  30.6 us
    pallas_call x1, Pallas kernels, attend(): pl.pallas_call(functools.partial(attention_kernel, head_dim ** (-0.5)), o...  23.7 us
    pallas_call x1, Pallas kernels, tail(): pl.pallas_call(tail_kernel, out_shape=jax.ShapeDtypeStruct((rows, chunk),...  23.1 us
    ppermute x1, waiting for transfers between devices, local_step(): g_peer = lax.ppermute(g_send, 'x', [(0, 1), (1, 0)])  3.48 us
  transfers between devices with their start and end apart: 1, of which 1 were waited for; matrix products, arithmetic and copies ran while one was open for 4% of the time, Pallas kernels for 27%

profile of v13, /device:TPU:0, one launch (start us, length us, event | category | flops | bytes accessed | tf_op | source)
XLA Modules:
  0.0 87.1 jit_solution(12166019758940709814)
XLA Ops:
  0.6 30.6 %head.1 = (bf16[4,24,680]{2,1,0:T(8,128)(2,1)}, f32[3,96,512]{2,1,0:T(8,128)}, f32[96,3584]{1,0:T(8,128)}, f32[96,5120]{1,0:T(8,128)}) custom-call(bf16[192,320]{1,0:T(8,128)(2,1)} %x_hbm.1, f32[320]{0:T(512)} %scale_hbm.1, bf16[1280,2,2560]{2,1,0:T(2,128)(2,1)} %wg_hbm.1, bf16[680,1280]{1,0:T(8,128)(2,1)} %bitcast.26), custom_call_target="tpu_custom_call" | custom-call | flops 5033164800 | bytes 13107200 | tf_op jit(solution)/shard_map/head/pallas_call | solution.py:341
  31.3 1.0 %collective-permute-start = (f32[96,3584]{1,0:T(8,128)}, f32[96,3584]{1,0:T(8,128)S(1)}, u32[]{:S(2)}, u32[]{:S(2)}) collective-permute-start(f32[96,3584]{1,0:T(8,128)} %get-tuple-element.11), channel_id=1, source_target_pairs={{0,4},{4,0},{1,5},{5,1},{2,6},{6,2},{3,7},{7,3}} | collective-permute-start | bytes 4128776 | tf_op jit(solution)/shard_map/ppermute | solution.py:557
  32.3 0.7 convert_element_type.40
  33.0 1.0 %copy.22 = bf16[24,4,680]{2,1,0:T(4,128)(2,1)S(1)} copy(bf16[24,4,680]{2,0,1:T(8,128)(2,1)} %bitcast.23) | data formatting | bytes 261120 | tf_op jit(solution)/shard_map/transpose | solution.py:558
  33.9 0.1 reshape.134
  34.1 0.1 fusion.8
  34.2 0.1 fusion.5
  34.3 0.1 maximum_bitcast_fusion
  34.4 0.1 copy.23
  34.5 0.2 reshape.136
  34.8 0.1 multiply_cosine_fusion.1
  34.9 0.2 subtract_convert_fusion
  35.1 0.1 pad_maximum_fusion.q_ref
  35.2 0.0 copy-start.1
  35.2 0.6 copy-done.1
  35.9 0.0 copy-start
  35.9 23.7 %attend.1 = (bf16[24,32,80]{2,1,0:T(8,128)(2,1)S(1)}, bf16[24,80,4096]{2,1,0:T(8,128)(2,1)}, bf16[24,80,4096]{2,1,0:T(8,128)(2,1)}) custom-call(s32[24]{0:T(128)S(1)} %copy-done.1, bf16[24,32,80]{2,1,0:T(8,128)(2,1)S(1)} %pad_maximum_fusion.q_ref, f32[2,80,128]{2,1,0:T(8,128)S(1)} %pad_convert_fusion.cols_ref, bf16[24,80,4096]{2,1,0:T(8,128)(2,1)} %bitcast.20, ...), custom_call_target="tpu_custom_call" | custom-call | flops 1006632960 | bytes 62914560 | tf_op jit(solution)/shard_map/attend/pallas_call | solution.py:67
  59.5 0.0 copy-start.2
  59.6 0.2 reshape.135
  59.8 3.5 %collective-permute-done.g_peer = f32[96,3584]{1,0:T(8,128)S(1)} collective-permute-done((f32[96,3584]{1,0:T(8,128)}, f32[96,3584]{1,0:T(8,128)S(1)}, u32[]{:S(2)}, u32[]{:S(2)}) %collective-permute-start) | collective-permute-done | bytes 1376288 | tf_op jit(solution)/shard_map/ppermute | solution.py:557
  63.3 0.0 copy-done
  63.3 23.1 %tail.1 = f32[192,320]{1,0:T(8,128)S(1)} custom-call(f32[3,96,512]{2,1,0:T(8,128)S(1)} %copy-done, f32[96,3584]{1,0:T(8,128)S(1)} %collective-permute-done.g_peer, f32[96,5120]{1,0:T(8,128)} %get-tuple-element.12.own_hbm, bf16[4,24,640]{2,1,0:T(8,128)(2,1)S(1)} %bitcast.19, bf16[2560,1280]{1,0:T(8,128)(2,1)} %wd_hbm.1, bf16[640,1280]{1,0:T(8,128)(2,1)} %wo_hbm.1), custom_call_target="tpu_custom_call" | custom-call | flops 1572864000 | bytes 8192000 | tf_op jit(solution)/shard_map/tail/pallas_call | solution.py:508
  86.3 0.0 copy-done.2
  86.3 0.7 add_convert_fusion.1
  (5 shorter events, 0.1 us)
Async XLA Ops:
  31.3 32.0 %collective-permute-start = (f32[96,3584]{1,0:T(8,128)}, f32[96,3584]{1,0:T(8,128)S(1)}, u32[]{:S(2)}, u32[]{:S(2)}) collective-permute-start(f32[96,3584]{1,0:T(8,128)} %get-tuple-element.11), channel_id=1, source_target_pairs={{0,4},{4,0},{1,5},{5,1},{2,6},{6,2},{3,7},{7,3}} | collective-permute-start | bytes 4128776 | tf_op jit(solution)/shard_map/ppermute | solution.py:557
  35.2 0.7 copy-start.1
  35.9 27.4 %copy-start = (f32[3,96,512]{2,1,0:T(8,128)S(1)}, f32[3,96,512]{2,1,0:T(8,128)}, u32[]{:S(2)}) copy-start(f32[3,96,512]{2,1,0:T(8,128)} %get-tuple-element.10.g_first) | copy-start | bytes 1769476
  59.5 26.8 %copy-start.2 = (bf16[192,320]{1,0:T(8,128)(2,1)S(1)}, bf16[192,320]{1,0:T(8,128)(2,1)}, u32[]{:S(2)}) copy-start(bf16[192,320]{1,0:T(8,128)(2,1)} %x_hbm.1) | copy-start | bytes 368644

commit v14 on v12

--- a/solution.py
+++ b/solution.py
@@ -165,6 +165,8 @@
     me = me_x * 4 + me_yz
     stats[me] = tile
     others_ready()
+    x_copy(1, 0).start()
+    x_copy(0, 0).start()
     t_out = [
         remote(stats.at[me], stats.at[me], t_send.at[4 * dx + k], t_recv.at[4 * dx + k], lax.rem(me_x + dx, 2), lax.rem(me_yz + k, 4))
         for dx in range(2) for k in range(4) if dx or k
@@ -176,13 +178,15 @@
     s_out = [remote(sg.at[me_yz], sg.at[me_yz], s_send.at[k], s_recv.at[k], me_x, lax.rem(me_yz + k, 4)) for k in (1, 2, 3)]
     for copy in s_out:
         copy.start()
-    for piece in range(4):
+    for piece in range(1, 4):
         x_copy(1, piece).start()
         x_copy(0, piece).start()
     for copy in wg_in:
         copy.start()
     wide, thin = spread(128, 256, 0), spread(64, 128, 0)
     wide_u, thin_u = spread(128, 256, 1), spread(64, 128, 1)
+    x_copy(1, 0).wait()
+    x_copy(2, 0).start()
     for copy in t_out:
         copy.wait()
     total = stats[0]
@@ -254,7 +258,6 @@
 
     wa_in.wait()
     z_out = [*z_copies(0), *z_copies(1)]
-    pass_on(0)
     far(0, *near(0), z_send, r_send)
     z_out[0].start()
     z_out[1].start()

time: 87 us -> 86.6 us (level)
  no operation moved by 1% of the time
where the time goes in v14:
time: 86.6 us; the launch traced here: 86.5 us
  Pallas kernels  72.8 us (84%)
  waiting for transfers between devices  7.44 us (9%)
  local copies, waits for them, and re-layouts  2.3 us (3%)
  other arithmetic  2.14 us (2%)
  starting transfers between devices  1.04 us (1%)
    pallas_call x1, Pallas kernels, head(): pl.pallas_call(functools.partial(head_kernel, d_model, early), out_shape=...  25.8 us
    pallas_call x1, Pallas kernels, attend(): pl.pallas_call(functools.partial(attention_kernel, head_dim ** (-0.5)), o...  23.7 us
    pallas_call x1, Pallas kernels, tail(): pl.pallas_call(tail_kernel, out_shape=jax.ShapeDtypeStruct((rows, chunk),...  23.3 us
    ppermute x1, waiting for transfers between devices, local_step(): g_peer = lax.ppermute(g_send, 'x', [(0, 1), (1, 0)])  7.44 us
  transfers between devices with their start and end apart: 1, of which 1 were waited for; matrix products, arithmetic and copies ran while one was open for 4% of the time, Pallas kernels for 27%

profile of v14, /device:TPU:0, one launch (start us, length us, event | category | flops | bytes accessed | tf_op | source)
XLA Modules:
  0.0 86.5 jit_solution(11514143278079278295)
XLA Ops:
  0.6 25.8 %head.1 = (bf16[4,24,680]{2,1,0:T(8,128)(2,1)}, f32[2,96,512]{2,1,0:T(8,128)}, f32[96,4096]{1,0:T(8,128)}, f32[96,5120]{1,0:T(8,128)}) custom-call(bf16[192,320]{1,0:T(8,128)(2,1)} %x_hbm.1, f32[320]{0:T(512)} %scale_hbm.1, bf16[1280,2,2560]{2,1,0:T(2,128)(2,1)} %wg_hbm.1, bf16[680,1280]{1,0:T(8,128)(2,1)} %bitcast.26), custom_call_target="tpu_custom_call" | custom-call | flops 5033164800 | bytes 13107200 | tf_op jit(solution)/shard_map/head/pallas_call | solution.py:344
  26.5 1.0 %collective-permute-start = (f32[96,4096]{1,0:T(8,128)}, f32[96,4096]{1,0:T(8,128)S(1)}, u32[]{:S(2)}, u32[]{:S(2)}) collective-permute-start(f32[96,4096]{1,0:T(8,128)} %get-tuple-element.11), channel_id=1, source_target_pairs={{0,4},{4,0},{1,5},{5,1},{2,6},{6,2},{3,7},{7,3}} | collective-permute-start | bytes 4718600 | tf_op jit(solution)/shard_map/ppermute | solution.py:560
  27.5 0.7 convert_element_type.40
  28.2 1.0 %copy.22 = bf16[24,4,680]{2,1,0:T(4,128)(2,1)S(1)} copy(bf16[24,4,680]{2,0,1:T(8,128)(2,1)} %bitcast.23) | data formatting | bytes 261120 | tf_op jit(solution)/shard_map/transpose | solution.py:561
  29.2 0.1 reshape.134
  29.3 0.1 fusion.8
  29.4 0.1 fusion.5
  29.5 0.1 maximum_bitcast_fusion
  29.6 0.1 copy.23
  29.7 0.2 reshape.136
  30.0 0.1 multiply_cosine_fusion.1
  30.1 0.2 subtract_convert_fusion
  30.3 0.1 pad_maximum_fusion.q_ref
  30.4 0.0 copy-start.1
  30.4 0.6 copy-done.1
  31.1 0.0 copy-start
  31.1 23.7 %attend.1 = (bf16[24,32,80]{2,1,0:T(8,128)(2,1)S(1)}, bf16[24,80,4096]{2,1,0:T(8,128)(2,1)}, bf16[24,80,4096]{2,1,0:T(8,128)(2,1)}) custom-call(s32[24]{0:T(128)S(1)} %copy-done.1, bf16[24,32,80]{2,1,0:T(8,128)(2,1)S(1)} %pad_maximum_fusion.q_ref, f32[2,80,128]{2,1,0:T(8,128)S(1)} %pad_convert_fusion.cols_ref, bf16[24,80,4096]{2,1,0:T(8,128)(2,1)} %bitcast.20, ...), custom_call_target="tpu_custom_call" | custom-call | flops 1006632960 | bytes 62914560 | tf_op jit(solution)/shard_map/attend/pallas_call | solution.py:67
  54.8 0.0 copy-start.2
  54.8 0.2 reshape.135
  55.0 7.4 %collective-permute-done.g_peer = f32[96,4096]{1,0:T(8,128)S(1)} collective-permute-done((f32[96,4096]{1,0:T(8,128)}, f32[96,4096]{1,0:T(8,128)S(1)}, u32[]{:S(2)}, u32[]{:S(2)}) %collective-permute-start) | collective-permute-done | bytes 1572896 | tf_op jit(solution)/shard_map/ppermute | solution.py:560
  62.4 0.0 copy-done
  62.4 23.3 %tail.1 = f32[192,320]{1,0:T(8,128)S(1)} custom-call(f32[2,96,512]{2,1,0:T(8,128)S(1)} %copy-done, f32[96,4096]{1,0:T(8,128)S(1)} %collective-permute-done.g_peer, f32[96,5120]{1,0:T(8,128)} %get-tuple-element.12.own_hbm, bf16[4,24,640]{2,1,0:T(8,128)(2,1)S(1)} %bitcast.19, bf16[2560,1280]{1,0:T(8,128)(2,1)} %wd_hbm.1, bf16[640,1280]{1,0:T(8,128)(2,1)} %wo_hbm.1), custom_call_target="tpu_custom_call" | custom-call | flops 1572864000 | bytes 8192000 | tf_op jit(solution)/shard_map/tail/pallas_call | solution.py:511
  85.7 0.0 copy-done.2
  85.8 0.7 add_convert_fusion.1
  (5 shorter events, 0.1 us)
Async XLA Ops:
  26.5 36.0 %collective-permute-start = (f32[96,4096]{1,0:T(8,128)}, f32[96,4096]{1,0:T(8,128)S(1)}, u32[]{:S(2)}, u32[]{:S(2)}) collective-permute-start(f32[96,4096]{1,0:T(8,128)} %get-tuple-element.11), channel_id=1, source_target_pairs={{0,4},{4,0},{1,5},{5,1},{2,6},{6,2},{3,7},{7,3}} | collective-permute-start | bytes 4718600 | tf_op jit(solution)/shard_map/ppermute | solution.py:560
  30.4 0.7 copy-start.1
  31.1 31.4 %copy-start = (f32[2,96,512]{2,1,0:T(8,128)S(1)}, f32[2,96,512]{2,1,0:T(8,128)}, u32[]{:S(2)}) copy-start(f32[2,96,512]{2,1,0:T(8,128)} %get-tuple-element.10.g_first) | copy-start | bytes 1179652
  54.8 31.0 %copy-start.2 = (bf16[192,320]{1,0:T(8,128)(2,1)S(1)}, bf16[192,320]{1,0:T(8,128)(2,1)}, u32[]{:S(2)}) copy-start(bf16[192,320]{1,0:T(8,128)(2,1)} %x_hbm.1) | copy-start | bytes 368644

commit v15 on v14

--- a/solution.py
+++ b/solution.py
@@ -417,8 +417,9 @@
         copy.start()
     oa[me] = ov[me_yz]
 
-    def h_copy(i):
-        return remote(hb.at[i, me_x], hb.at[i, me_x], h_send.at[i], h_recv.at[i], other_x, me_yz)
+    def h_copy(i, part):
+        at = hb.at[i, me_x, :, pl.ds(part * (ff // 2), ff // 2)]
+        return remote(at, at, h_send.at[i, part], h_recv.at[i, part], other_x, me_yz)
 
     for copy in own_in:
         copy.wait()
@@ -437,7 +438,8 @@
             hb[i, me_x, :, cols] = act(g_own[at, cols] + g_first[c, at, :wide], g_own[at, up_cols] + g_first[c, at, wide:])
         done = early * wide
         hb[i, me_x, :, done:] = act(g_own[at, done:ff] + g_peer[at, :ff - done], g_own[at, ff + done:] + g_peer[at, ff - done:])
-        h_copy(i).start()
+        h_copy(i, 0).start()
+        h_copy(i, 1).start()
         return carry
 
     lax.fori_loop(0, groups, activate, 0)
@@ -466,9 +468,12 @@
         over_copy(i).start()
 
     def product(i, carry):
-        h_copy(i).wait()
         first_at = pl.multiple_of(span * i, span)
-        part = jnp.dot(hb[i].reshape(2 * span, ff), wd[...], preferred_element_type=jnp.float32)
+        part = 0.0
+        for k in range(2):
+            h_copy(i, k).wait()
+            cols = slice(k * (ff // 2), (k + 1) * (ff // 2))
+            part = part + jnp.dot(hb[i, :, :, cols].reshape(2 * span, ff // 2), wd[cols, :], preferred_element_type=jnp.float32)
         part = part + jnp.concatenate([out_part[pl.ds(first_at, span)], out_part[pl.ds(half + first_at, span)]], axis=0)
         for j in range(4):
             moved = part if j == 0 else pltpu.roll(part, (4 - j) * chunk, 1)
@@ -526,7 +531,7 @@
             pltpu.VMEM((groups, 2, 2 * span, chunk), f32),
             pltpu.VMEM((groups, 2 * span, chunk), f32),
             pltpu.VMEM((groups, 2 * span, chunk), f32),
-            dma((3,)), dma((groups,)), dma((8,)), dma((8,)), dma((groups,)), dma((groups,)),
+            dma((3,)), dma((groups,)), dma((8,)), dma((8,)), dma((groups, 2)), dma((groups, 2)),
             dma((groups, 2)), dma((groups, 2)), dma((groups,)), dma((groups,)),
         ],
         compiler_params=pltpu.CompilerParams(collective_id=1, has_side_effects=True, vmem_limit_bytes=51 * 1024 * 1024),

time: 86.6 us -> 88 us (1.016)
  Pallas kernels: 72.8 us -> 74.2 us
    pallas_call x1, Pallas kernels: 23.3 us -> 24.7 us  [tail(): pl.pallas_call(tail_kernel, out_shape=jax.ShapeDtypeStruct((rows, chunk),...]
  transfers between devices with their start and end apart: 1 -> 1, of which waited for: 1 -> 1; matrix products, arithmetic and copies ran while one was open for 4% -> 3% of each run, Pallas kernels for 27% -> 27%
where the time goes in v15:
time: 88 us; the launch traced here: 87.9 us
  Pallas kernels  74.2 us (84%)
  waiting for transfers between devices  7.44 us (8%)
  local copies, waits for them, and re-layouts  2.3 us (3%)
  other arithmetic  2.14 us (2%)
  starting transfers between devices  1.04 us (1%)
    pallas_call x1, Pallas kernels, head(): pl.pallas_call(functools.partial(head_kernel, d_model, early), out_shape=...  25.8 us
    pallas_call x1, Pallas kernels, tail(): pl.pallas_call(tail_kernel, out_shape=jax.ShapeDtypeStruct((rows, chunk),...  24.7 us
    pallas_call x1, Pallas kernels, attend(): pl.pallas_call(functools.partial(attention_kernel, head_dim ** (-0.5)), o...  23.7 us
    ppermute x1, waiting for transfers between devices, local_step(): g_peer = lax.ppermute(g_send, 'x', [(0, 1), (1, 0)])  7.44 us
  transfers between devices with their start and end apart: 1, of which 1 were waited for; matrix products, arithmetic and copies ran while one was open for 3% of the time, Pallas kernels for 27%

profile of v15, /device:TPU:0, one launch (start us, length us, event | category | flops | bytes accessed | tf_op | source)
XLA Modules:
  0.0 87.9 jit_solution(17052211647928912828)
XLA Ops:
  0.6 25.8 %head.1 = (bf16[4,24,680]{2,1,0:T(8,128)(2,1)}, f32[2,96,512]{2,1,0:T(8,128)}, f32[96,4096]{1,0:T(8,128)}, f32[96,5120]{1,0:T(8,128)}) custom-call(bf16[192,320]{1,0:T(8,128)(2,1)} %x_hbm.1, f32[320]{0:T(512)} %scale_hbm.1, bf16[1280,2,2560]{2,1,0:T(2,128)(2,1)} %wg_hbm.1, bf16[680,1280]{1,0:T(8,128)(2,1)} %bitcast.26), custom_call_target="tpu_custom_call" | custom-call | flops 5033164800 | bytes 13107200 | tf_op jit(solution)/shard_map/head/pallas_call | solution.py:344
  26.5 1.0 %collective-permute-start = (f32[96,4096]{1,0:T(8,128)}, f32[96,4096]{1,0:T(8,128)S(1)}, u32[]{:S(2)}, u32[]{:S(2)}) collective-permute-start(f32[96,4096]{1,0:T(8,128)} %get-tuple-element.11), channel_id=1, source_target_pairs={{0,4},{4,0},{1,5},{5,1},{2,6},{6,2},{3,7},{7,3}} | collective-permute-start | bytes 4718600 | tf_op jit(solution)/shard_map/ppermute | solution.py:565
  27.5 0.7 convert_element_type.40
  28.2 1.0 %copy.22 = bf16[24,4,680]{2,1,0:T(4,128)(2,1)S(1)} copy(bf16[24,4,680]{2,0,1:T(8,128)(2,1)} %bitcast.23) | data formatting | bytes 261120 | tf_op jit(solution)/shard_map/transpose | solution.py:566
  29.2 0.1 reshape.134
  29.3 0.1 fusion.8
  29.4 0.1 fusion.5
  29.5 0.1 maximum_bitcast_fusion
  29.6 0.1 copy.23
  29.7 0.2 reshape.136
  30.0 0.1 multiply_cosine_fusion.1
  30.1 0.2 subtract_convert_fusion
  30.3 0.1 pad_maximum_fusion.q_ref
  30.4 0.0 copy-start.1
  30.4 0.6 copy-done.1
  31.1 0.0 copy-start
  31.1 23.7 %attend.1 = (bf16[24,32,80]{2,1,0:T(8,128)(2,1)S(1)}, bf16[24,80,4096]{2,1,0:T(8,128)(2,1)}, bf16[24,80,4096]{2,1,0:T(8,128)(2,1)}) custom-call(s32[24]{0:T(128)S(1)} %copy-done.1, bf16[24,32,80]{2,1,0:T(8,128)(2,1)S(1)} %pad_maximum_fusion.q_ref, f32[2,80,128]{2,1,0:T(8,128)S(1)} %pad_convert_fusion.cols_ref, bf16[24,80,4096]{2,1,0:T(8,128)(2,1)} %bitcast.20, ...), custom_call_target="tpu_custom_call" | custom-call | flops 1006632960 | bytes 62914560 | tf_op jit(solution)/shard_map/attend/pallas_call | solution.py:67
  54.8 0.0 copy-start.2
  54.8 0.2 reshape.135
  55.0 7.4 %collective-permute-done.g_peer = f32[96,4096]{1,0:T(8,128)S(1)} collective-permute-done((f32[96,4096]{1,0:T(8,128)}, f32[96,4096]{1,0:T(8,128)S(1)}, u32[]{:S(2)}, u32[]{:S(2)}) %collective-permute-start) | collective-permute-done | bytes 1572896 | tf_op jit(solution)/shard_map/ppermute | solution.py:565
  62.4 0.0 copy-done
  62.4 24.7 %tail.1 = f32[192,320]{1,0:T(8,128)S(1)} custom-call(f32[2,96,512]{2,1,0:T(8,128)S(1)} %copy-done, f32[96,4096]{1,0:T(8,128)S(1)} %collective-permute-done.g_peer, f32[96,5120]{1,0:T(8,128)} %get-tuple-element.12.own_hbm, bf16[4,24,640]{2,1,0:T(8,128)(2,1)S(1)} %bitcast.19, bf16[2560,1280]{1,0:T(8,128)(2,1)} %wd_hbm.1, bf16[640,1280]{1,0:T(8,128)(2,1)} %wo_hbm.1), custom_call_target="tpu_custom_call" | custom-call | flops 1572864000 | bytes 8192000 | tf_op jit(solution)/shard_map/tail/pallas_call | solution.py:516
  87.2 0.0 copy-done.2
  87.2 0.7 add_convert_fusion.1
  (5 shorter events, 0.1 us)
Async XLA Ops:
  26.5 36.0 %collective-permute-start = (f32[96,4096]{1,0:T(8,128)}, f32[96,4096]{1,0:T(8,128)S(1)}, u32[]{:S(2)}, u32[]{:S(2)}) collective-permute-start(f32[96,4096]{1,0:T(8,128)} %get-tuple-element.11), channel_id=1, source_target_pairs={{0,4},{4,0},{1,5},{5,1},{2,6},{6,2},{3,7},{7,3}} | collective-permute-start | bytes 4718600 | tf_op jit(solution)/shard_map/ppermute | solution.py:565
  30.4 0.7 copy-start.1
  31.1 31.4 %copy-start = (f32[2,96,512]{2,1,0:T(8,128)S(1)}, f32[2,96,512]{2,1,0:T(8,128)}, u32[]{:S(2)}) copy-start(f32[2,96,512]{2,1,0:T(8,128)} %get-tuple-element.10.g_first) | copy-start | bytes 1179652
  54.8 32.4 %copy-start.2 = (bf16[192,320]{1,0:T(8,128)(2,1)S(1)}, bf16[192,320]{1,0:T(8,128)(2,1)}, u32[]{:S(2)}) copy-start(bf16[192,320]{1,0:T(8,128)(2,1)} %x_hbm.1) | copy-start | bytes 368644

commit v16 on v14

--- a/solution.py
+++ b/solution.py
@@ -476,9 +476,9 @@
         for which in (1 - col, col):
             pair_copy(i, which).start()
 
-        @pl.when(i > 0)
+        @pl.when(i > 1)
         def _():
-            cross(i - 1)
+            cross(i - 2)
 
         return carry
 
@@ -491,6 +491,7 @@
         return carry
 
     lax.fori_loop(0, groups, product, 0)
+    cross(groups - 2)
     lax.fori_loop(0, groups - 3, finish, 0)
     cross(groups - 1)
     lax.fori_loop(groups - 3, groups, finish, 0)

time: 86.6 us -> 87.6 us (1.012)
  Pallas kernels: 72.8 us -> 73.8 us
    pallas_call x1, Pallas kernels: 23.3 us -> 24.3 us  [tail(): pl.pallas_call(tail_kernel, out_shape=jax.ShapeDtypeStruct((rows, chunk),...]
where the time goes in v16:
time: 87.6 us; the launch traced here: 87.5 us
  Pallas kernels  73.8 us (84%)
  waiting for transfers between devices  7.45 us (9%)
  local copies, waits for them, and re-layouts  2.3 us (3%)
  other arithmetic  2.14 us (2%)
  starting transfers between devices  1.04 us (1%)
    pallas_call x1, Pallas kernels, head(): pl.pallas_call(functools.partial(head_kernel, d_model, early), out_shape=...  25.8 us
    pallas_call x1, Pallas kernels, tail(): pl.pallas_call(tail_kernel, out_shape=jax.ShapeDtypeStruct((rows, chunk),...  24.3 us
    pallas_call x1, Pallas kernels, attend(): pl.pallas_call(functools.partial(attention_kernel, head_dim ** (-0.5)), o...  23.6 us
    ppermute x1, waiting for transfers between devices, local_step(): g_peer = lax.ppermute(g_send, 'x', [(0, 1), (1, 0)])  7.45 us
  transfers between devices with their start and end apart: 1, of which 1 were waited for; matrix products, arithmetic and copies ran while one was open for 4% of the time, Pallas kernels for 27%

profile of v16, /device:TPU:0, one launch (start us, length us, event | category | flops | bytes accessed | tf_op | source)
XLA Modules:
  0.0 87.5 jit_solution(6553120149318957246)
XLA Ops:
  0.6 25.8 %head.1 = (bf16[4,24,680]{2,1,0:T(8,128)(2,1)}, f32[2,96,512]{2,1,0:T(8,128)}, f32[96,4096]{1,0:T(8,128)}, f32[96,5120]{1,0:T(8,128)}) custom-call(bf16[192,320]{1,0:T(8,128)(2,1)} %x_hbm.1, f32[320]{0:T(512)} %scale_hbm.1, bf16[1280,2,2560]{2,1,0:T(2,128)(2,1)} %wg_hbm.1, bf16[680,1280]{1,0:T(8,128)(2,1)} %bitcast.26), custom_call_target="tpu_custom_call" | custom-call | flops 5033164800 | bytes 13107200 | tf_op jit(solution)/shard_map/head/pallas_call | solution.py:344
  26.5 1.0 %collective-permute-start = (f32[96,4096]{1,0:T(8,128)}, f32[96,4096]{1,0:T(8,128)S(1)}, u32[]{:S(2)}, u32[]{:S(2)}) collective-permute-start(f32[96,4096]{1,0:T(8,128)} %get-tuple-element.11), channel_id=1, source_target_pairs={{0,4},{4,0},{1,5},{5,1},{2,6},{6,2},{3,7},{7,3}} | collective-permute-start | bytes 4718600 | tf_op jit(solution)/shard_map/ppermute | solution.py:561
  27.5 0.7 convert_element_type.40
  28.2 1.0 %copy.22 = bf16[24,4,680]{2,1,0:T(4,128)(2,1)S(1)} copy(bf16[24,4,680]{2,0,1:T(8,128)(2,1)} %bitcast.23) | data formatting | bytes 261120 | tf_op jit(solution)/shard_map/transpose | solution.py:562
  29.2 0.1 reshape.134
  29.3 0.1 fusion.8
  29.4 0.1 fusion.5
  29.5 0.1 maximum_bitcast_fusion
  29.6 0.1 copy.23
  29.7 0.2 reshape.136
  30.0 0.1 multiply_cosine_fusion.1
  30.1 0.2 subtract_convert_fusion
  30.3 0.1 pad_maximum_fusion.q_ref
  30.4 0.0 copy-start.1
  30.4 0.6 copy-done.1
  31.1 0.0 copy-start
  31.1 23.6 %attend.1 = (bf16[24,32,80]{2,1,0:T(8,128)(2,1)S(1)}, bf16[24,80,4096]{2,1,0:T(8,128)(2,1)}, bf16[24,80,4096]{2,1,0:T(8,128)(2,1)}) custom-call(s32[24]{0:T(128)S(1)} %copy-done.1, bf16[24,32,80]{2,1,0:T(8,128)(2,1)S(1)} %pad_maximum_fusion.q_ref, f32[2,80,128]{2,1,0:T(8,128)S(1)} %pad_convert_fusion.cols_ref, bf16[24,80,4096]{2,1,0:T(8,128)(2,1)} %bitcast.20, ...), custom_call_target="tpu_custom_call" | custom-call | flops 1006632960 | bytes 62914560 | tf_op jit(solution)/shard_map/attend/pallas_call | solution.py:67
  54.7 0.0 copy-start.2
  54.8 0.2 reshape.135
  55.0 7.5 %collective-permute-done.g_peer = f32[96,4096]{1,0:T(8,128)S(1)} collective-permute-done((f32[96,4096]{1,0:T(8,128)}, f32[96,4096]{1,0:T(8,128)S(1)}, u32[]{:S(2)}, u32[]{:S(2)}) %collective-permute-start) | collective-permute-done | bytes 1572896 | tf_op jit(solution)/shard_map/ppermute | solution.py:561
  62.4 0.0 copy-done
  62.4 24.3 %tail.1 = f32[192,320]{1,0:T(8,128)S(1)} custom-call(f32[2,96,512]{2,1,0:T(8,128)S(1)} %copy-done, f32[96,4096]{1,0:T(8,128)S(1)} %collective-permute-done.g_peer, f32[96,5120]{1,0:T(8,128)} %get-tuple-element.12.own_hbm, bf16[4,24,640]{2,1,0:T(8,128)(2,1)S(1)} %bitcast.19, bf16[2560,1280]{1,0:T(8,128)(2,1)} %wd_hbm.1, bf16[640,1280]{1,0:T(8,128)(2,1)} %wo_hbm.1), custom_call_target="tpu_custom_call" | custom-call | flops 1572864000 | bytes 8192000 | tf_op jit(solution)/shard_map/tail/pallas_call | solution.py:512
  86.8 0.0 copy-done.2
  86.8 0.7 add_convert_fusion.1
  (5 shorter events, 0.1 us)
Async XLA Ops:
  26.5 36.0 %collective-permute-start = (f32[96,4096]{1,0:T(8,128)}, f32[96,4096]{1,0:T(8,128)S(1)}, u32[]{:S(2)}, u32[]{:S(2)}) collective-permute-start(f32[96,4096]{1,0:T(8,128)} %get-tuple-element.11), channel_id=1, source_target_pairs={{0,4},{4,0},{1,5},{5,1},{2,6},{6,2},{3,7},{7,3}} | collective-permute-start | bytes 4718600 | tf_op jit(solution)/shard_map/ppermute | solution.py:561
  30.4 0.7 copy-start.1
  31.1 31.4 %copy-start = (f32[2,96,512]{2,1,0:T(8,128)S(1)}, f32[2,96,512]{2,1,0:T(8,128)}, u32[]{:S(2)}) copy-start(f32[2,96,512]{2,1,0:T(8,128)} %get-tuple-element.10.g_first) | copy-start | bytes 1179652
  54.7 32.0 %copy-start.2 = (bf16[192,320]{1,0:T(8,128)(2,1)S(1)}, bf16[192,320]{1,0:T(8,128)(2,1)}, u32[]{:S(2)}) copy-start(bf16[192,320]{1,0:T(8,128)(2,1)} %x_hbm.1) | copy-start | bytes 368644
